TPU v7x, 16 devices: a whole 2x2x2 slice. The times are simulated.
16 devices in a mesh: data: 4 (over z, y), dap: 4 (over x, core).
Axes of the slice: x: 2, y: 2, z: 2, core: 2. Of those that a mesh axis runs over, the one named last changes fastest.
Arguments:
- msa_act: bfloat16 [512, 64, 384], P(('data', 'dap')), parts along dimension 0
- pair_act: bfloat16 [256, 64, 128], P(('data', 'dap')), parts along dimension 0
- msa_mask: int32 [512, 64], P('data'), parts along dimension 0
- res_mask: int32 [256], P('data'), parts along dimension 0
- w_row_bias: bfloat16 [2, 128, 16], replicated
- w_row_in: bfloat16 [2, 384, 4, 16, 24], replicated
- w_row_out: bfloat16 [2, 16, 24, 384], replicated
- w_col_in: bfloat16 [2, 384, 4, 16, 24], replicated
- w_col_out: bfloat16 [2, 16, 24, 384], replicated
- w_opm_in: bfloat16 [2, 384, 2, 32], replicated
- w_opm_out: bfloat16 [2, 32, 32, 128], replicated
- w_ts_bias: bfloat16 [2, 128, 4], replicated
- w_ts_in: bfloat16 [2, 128, 4, 4, 32], replicated
- w_ts_out: bfloat16 [2, 4, 32, 128], replicated
- w_te_bias: bfloat16 [2, 128, 4], replicated
- w_te_in: bfloat16 [2, 128, 4, 4, 32], replicated
- w_te_out: bfloat16 [2, 4, 32, 128], replicated
Outputs:
- output 1: bfloat16 [512, 64, 384], P(('data', 'dap')), parts along dimension 0
- output 2: bfloat16 [256, 64, 128], P(('data', 'dap')), parts along dimension 0
There are 4 independent parts. A program takes and returns all parts, laid end to end along the dimension named above; an argument that names none is the same for every part.
All inputs are finite; a program needn't handle non-finite values.
Results may differ from a plain program's by a relative error of at most 0.0182426.
Values are sent between devices in bfloat16 or wider.
A program may use at most 1 GiB of HBM per device.

v0:
```python
import jax
import jax.numpy as jnp
from jax import lax
from jax.sharding import PartitionSpec as P


def layer_norm(values):
    flat = values.astype(jnp.float32)
    row_mean = jnp.mean(flat, axis=-1, keepdims=True)
    centered = flat - row_mean
    row_var = jnp.mean(centered * centered, axis=-1, keepdims=True)
    return (centered * lax.rsqrt(row_var + 1e-5)).astype(jnp.bfloat16)


def add_residual(current, update):
    return (current.astype(jnp.float32) + update).astype(jnp.bfloat16)


def pair_bias(pair_ln, w_bias, form):
    return jnp.einsum(form, pair_ln, w_bias, preferred_element_type=jnp.float32).astype(jnp.bfloat16)


def gated_attention(x_ln, w_in, w_out, bias_hqk, key_mask, batch_first):
    head_dim = w_in.shape[3]
    projected = jnp.einsum('abc,cfhd->abfhd', x_ln, w_in, preferred_element_type=jnp.float32).astype(jnp.bfloat16)
    query = projected[:, :, 0]
    keys = projected[:, :, 1]
    values = projected[:, :, 2]
    gate_raw = projected[:, :, 3]
    if batch_first:
        logits = jnp.einsum('bqhd,bkhd->bhqk', query, keys, preferred_element_type=jnp.float32)
    else:
        logits = jnp.einsum('qbhd,kbhd->bhqk', query, keys, preferred_element_type=jnp.float32)
    logits = logits * head_dim ** -0.5
    if bias_hqk is not None:
        logits = logits + bias_hqk.astype(jnp.float32)
    logits = jnp.where(key_mask > 0, logits, -1e9)
    attn_probs = jax.nn.softmax(logits, axis=-1).astype(jnp.bfloat16)
    if batch_first:
        attended = jnp.einsum('bhqk,bkhd->bqhd', attn_probs, values, preferred_element_type=jnp.float32)
    else:
        attended = jnp.einsum('bhqk,kbhd->qbhd', attn_probs, values, preferred_element_type=jnp.float32)
    gated = (attended * jax.nn.sigmoid(gate_raw.astype(jnp.float32))).astype(jnp.bfloat16)
    return jnp.einsum('abhd,hdc->abc', gated, w_out, preferred_element_type=jnp.float32)


def opm_halves(value_a8, mask_cols, w_in):
    projected = jnp.einsum('sic,cfp->sifp', layer_norm(value_a8), w_in, preferred_element_type=jnp.float32)
    projected = (projected * mask_cols.astype(jnp.float32)[:, :, None, None]).astype(jnp.bfloat16)
    return projected[:, :, 0], projected[:, :, 1]


def opm_update(pair_act, left, right, left_mask, right_mask, w_out):
    outer = jnp.einsum('sip,sjq->ijpq', left, right, preferred_element_type=jnp.float32).astype(jnp.bfloat16)
    update = jnp.einsum('ijpq,pqc->ijc', outer, w_out, preferred_element_type=jnp.float32)
    pair_norm = jnp.einsum('si,sj->ij', left_mask.astype(jnp.bfloat16), right_mask.astype(jnp.bfloat16), preferred_element_type=jnp.float32)
    return add_residual(pair_act, update / (1e-3 + pair_norm)[:, :, None])


def solution(mesh):
    def local_step(value_a7, pair_blk, array_b8, res_mask, w_row_bias, w_row_in, w_row_out, w_col_in, w_col_out, w_opm_in, w_opm_out, w_ts_bias, w_ts_in, w_ts_out, w_te_bias, w_te_in, w_te_out):
        dev_index = lax.axis_index('dap')
        seq_loc = value_a7.shape[0]
        res_loc = pair_blk.shape[0]
        mask_seq = lax.dynamic_slice_in_dim(array_b8, dev_index * seq_loc, seq_loc, 0)
        mask_cols = lax.dynamic_slice_in_dim(array_b8, dev_index * res_loc, res_loc, 1)
        row_keys = mask_seq[:, None, None, :]
        col_keys = mask_cols.T[:, None, None, :]
        tri_keys = res_mask[None, None, None, :]

        row_bias = lax.all_gather(pair_bias(layer_norm(pair_blk), w_row_bias[0], 'ijc,ch->hij'), 'dap', axis=1, tiled=True)
        value_a7 = add_residual(value_a7, gated_attention(layer_norm(value_a7), w_row_in[0], w_row_out[0], row_bias, row_keys, True))
        value_a7 = lax.all_to_all(value_a7, 'dap', 1, 0, tiled=True)
        value_a7 = add_residual(value_a7, gated_attention(layer_norm(value_a7), w_col_in[0], w_col_out[0], None, col_keys, False))
        left, right = opm_halves(value_a7, mask_cols, w_opm_in[0])
        right_full = lax.all_gather(right, 'dap', axis=1, tiled=True)
        pair_blk = opm_update(pair_blk, left, right_full, mask_cols, array_b8, w_opm_out[0])
        pair_ln = layer_norm(pair_blk)
        tri_bias = lax.all_gather(pair_bias(pair_ln, w_ts_bias[0], 'ijc,ch->hij'), 'dap', axis=1, tiled=True)
        pair_blk = add_residual(pair_blk, gated_attention(pair_ln, w_ts_in[0], w_ts_out[0], tri_bias, tri_keys, True))
        pair_blk = lax.all_to_all(pair_blk, 'dap', 1, 0, tiled=True)
        pair_ln = layer_norm(pair_blk)
        tri_bias = lax.all_gather(pair_bias(pair_ln, w_te_bias[0], 'kic,ch->hik'), 'dap', axis=1, tiled=True)
        pair_blk = add_residual(pair_blk, gated_attention(pair_ln, w_te_in[0], w_te_out[0], tri_bias, tri_keys, False))

        row_bias = lax.all_gather(pair_bias(layer_norm(pair_blk), w_row_bias[1], 'ijc,ch->hij'), 'dap', axis=2, tiled=True)
        value_a7 = add_residual(value_a7, gated_attention(layer_norm(value_a7), w_col_in[1], w_col_out[1], None, col_keys, False))
        left, right = opm_halves(value_a7, mask_cols, w_opm_in[1])
        left_full = lax.all_gather(left, 'dap', axis=1, tiled=True)
        pair_blk = opm_update(pair_blk, left_full, right, array_b8, mask_cols, w_opm_out[1])
        value_a7 = lax.all_to_all(value_a7, 'dap', 0, 1, tiled=True)
        value_a7 = add_residual(value_a7, gated_attention(layer_norm(value_a7), w_row_in[1], w_row_out[1], row_bias, row_keys, True))
        pair_ln = layer_norm(pair_blk)
        tri_bias = lax.all_gather(pair_bias(pair_ln, w_te_bias[1], 'kic,ch->hik'), 'dap', axis=1, tiled=True)
        pair_blk = add_residual(pair_blk, gated_attention(pair_ln, w_te_in[1], w_te_out[1], tri_bias, tri_keys, False))
        pair_blk = lax.all_to_all(pair_blk, 'dap', 0, 1, tiled=True)
        pair_ln = layer_norm(pair_blk)
        tri_bias = lax.all_gather(pair_bias(pair_ln, w_ts_bias[1], 'ijc,ch->hij'), 'dap', axis=1, tiled=True)
        pair_blk = add_residual(pair_blk, gated_attention(pair_ln, w_ts_in[1], w_ts_out[1], tri_bias, tri_keys, True))
        return value_a7, pair_blk

    in_specs = (P(('data', 'dap')), P(('data', 'dap')), P('data'), P('data')) + (P(),) * 13
    out_specs = (P(('data', 'dap')), P(('data', 'dap')))
    return jax.shard_map(local_step, mesh=mesh, in_specs=in_specs, out_specs=out_specs, check_vma=False)
```

profile of v0, /device:TPU:0, one launch (start us, length us, event | category | flops | bytes accessed | tf_op | source)
XLA Modules:
  0.0 337.8 jit_solution(12062597505230803113)
XLA Ops:
  6.9 7.9 %all_gather.24 = bf16[16,64,64]{2,0,1:T(8,128)(2,1)S(1)} all-gather(bf16[16,16,64]{2,0,1:T(8,128)(2,1)S(1)} %fusion.134), channel_id=1, replica_groups=mesh['data'=4,'dap'=4] {'dap'}, dimensions={1}, use_global_device_ids=true | all-gather | bytes 163840 | tf_op jit(solution)/shard_map/all_gather | solution.py:71
  15.1 10.6 %convolution_convert_fusion.1 = bf16[32,64,4,16,24]{1,4,3,2,0:T(8,128)(2,1)} fusion(bf16[32,64,384]{2,1,0:T(8,128)(2,1)S(1)} %copy-done.1, f32[32,64]{1,0:T(8,128)S(1)} %add_rsqrt_fusion.6, f32[32,64]{1,0:T(8,128)S(1)} %broadcast_multiply_fusion.6, bf16[2,384,4,16,24]{1,4,3,2,0:T(8,128)(2,1)} %param.22), kind=kOutput, calls=%fused_computation.46 | convolution fusion | flops 2422210560 | bytes 9060352 | tf_op jit(solution)/shard_map/abc,cfhd->abfhd/dot_general | solution.py:25
  25.7 14.3 %fusion.305 = (f32[32,16,64]{2,1,0:T(8,128)}, f32[32,16,64,64]{2,3,1,0:T(8,128)}) fusion(f32[16,64,64]{1,2,0:T(8,128)S(1)} %copy.104, pred[32,64]{1,0:T(8,128)(4,1)S(1)} %broadcast_compare_fusion, bf16[32,64,4,16,24]{1,4,3,2,0:T(8,128)(2,1)} %convolution_convert_fusion.1), kind=kOutput, calls=%fused_computation.393 | convolution fusion | flops 111149120 | bytes 15075328 | tf_op jit(solution)/shard_map/sub | solution.py:38
  40.0 10.0 %fusion.53 = bf16[32,64,384]{2,1,0:T(8,128)(2,1)S(1)} fusion(bf16[32,64,384]{2,1,0:T(8,128)(2,1)S(1)} %copy-done.1, bf16[32,64,4,16,24]{1,4,3,2,0:T(8,128)(2,1)} %convolution_convert_fusion.1, f32[32,16,64,64]{2,3,1,0:T(8,128)} %get-tuple-element.12, f32[32,16,64]{2,1,0:T(8,128)} %get-tuple-element.11, bf16[2,16,24,384]{3,2,1,0:T(8,128)(2,1)} %param.23), kind=kOutput, calls=%fused_computation.77 | convolution fusion | flops 715915264 | bytes 26771456 | tf_op jit(solution)/shard_map/abhd,hdc->abc/dot_general | solution.py:44
  50.0 2.1 copy.106
  52.0 3.7 %all-to-all-start = ((bf16[32,64,384]{2,0,1:T(8,128)(2,1)}), bf16[32,64,384]{2,0,1:T(8,128)(2,1)S(1)}, u32[]{:S(2)}, u32[]{:S(2)}) async-start(bf16[32,64,384]{2,0,1:T(8,128)(2,1)} %copy.106), calls=%async_computation | async-start | bytes 3145728 | tf_op jit(solution)/shard_map/all_to_all | solution.py:73
  56.1 19.5 %all-to-all-done = bf16[32,64,384]{2,0,1:T(8,128)(2,1)S(1)} async-done(((bf16[32,64,384]{2,0,1:T(8,128)(2,1)}), bf16[32,64,384]{2,0,1:T(8,128)(2,1)S(1)}, u32[]{:S(2)}, u32[]{:S(2)}) %all-to-all-start) | async-done | bytes 1572896 | tf_op jit(solution)/shard_map/all_to_all | solution.py:73
  77.2 2.1 copy.107
  80.0 5.4 %convolution_convert_fusion.3 = bf16[128,16,4,16,24]{0,4,3,2,1:T(8,128)(2,1)} fusion(bf16[128,16,384,1,1]{2,0,4,3,1:T(8,128)(2,1)S(1)} %bitcast.637, bf16[2,384,4,16,24]{1,4,3,2,0:T(8,128)(2,1)S(1)} %copy-done.18), kind=kOutput, calls=%fused_computation.69 | convolution fusion | flops 2419064832 | bytes 9043968 | tf_op jit(solution)/shard_map/abc,cfhd->abfhd/dot_general | solution.py:25
  85.4 12.9 %fusion.306 = (f32[16,16,128]{2,1,0:T(8,128)}, f32[16,16,128,128]{2,3,1,0:T(8,128)}) fusion(pred[16,128]{1,0:T(8,128)(4,1)S(1)} %compare_bitcast_fusion, bf16[128,16,4,16,24]{0,4,3,2,1:T(8,128)(2,1)} %convolution_convert_fusion.3), kind=kOutput, calls=%fused_computation.394 | convolution fusion | flops 218103936 | bytes 20056064 | tf_op jit(solution)/shard_map/sub | solution.py:38
  98.3 9.7 %convert_reduce_fusion = (f32[128,16]{0,1:T(8,128)S(1)}, bf16[128,16,384]{2,0,1:T(8,128)(2,1)}) fusion(bf16[2,16,24,384]{3,2,1,0:T(8,128)(2,1)} %param.25, f32[16,16,128,128]{2,3,1,0:T(8,128)} %get-tuple-element.14, f32[16,16,128]{2,1,0:T(8,128)} %get-tuple-element.13, bf16[128,16,4,16,24]{0,4,3,2,1:T(8,128)(2,1)} %convolution_convert_fusion.3, ...), kind=kOutput, calls=%fused_computation.53 | convolution fusion | flops 821557248 | bytes 25075712 | tf_op jit(solution)/shard_map/abhd,hdc->abc/dot_general | solution.py:44
  108.0 2.2 fusion.47
  110.2 7.3 %convolution_convert_fusion.2 = bf16[128,16,4,16,24]{0,4,3,2,1:T(8,128)(2,1)} fusion(bf16[128,16,384]{2,0,1:T(8,128)(2,1)} %get-tuple-element.16, f32[128,16]{0,1:T(8,128)S(1)} %add_rsqrt_fusion.9, f32[128,16]{0,1:T(8,128)S(1)} %broadcast_multiply_fusion.8, bf16[2,384,4,16,24]{1,4,3,2,0:T(8,128)(2,1)} %param.24), kind=kOutput, calls=%fused_computation.68 | convolution fusion | flops 2422210560 | bytes 9060352 | tf_op jit(solution)/shard_map/abc,cfhd->abfhd/dot_general | solution.py:25
  118.9 6.5 %all-gather = bf16[128,64,1,32]{0,3,2,1:T(8,128)(2,1)S(1)} all-gather(bf16[128,16,1,32]{0,3,2,1:T(8,128)(2,1)S(1)} %slice.263), channel_id=2, replica_groups=mesh['data'=4,'dap'=4] {'dap'}, dimensions={1}, use_global_device_ids=true | all-gather | bytes 655360 | tf_op jit(solution)/shard_map/all_gather | solution.py:76
  125.4 5.6 %convert_bitcast_fusion = bf16[16,64,32,32]{2,3,0,1:T(8,128)(2,1)} fusion(bf16[128,64,1,32]{0,3,2,1:T(8,128)(2,1)S(1)} %all-gather, bf16[128,16,2,32]{0,3,2,1:T(8,128)(2,1)S(1)} %fusion.108), kind=kOutput, calls=%fused_computation.27 | convolution fusion | flops 269484032 | bytes 2752512 | tf_op jit(solution)/shard_map/sip,sjq->ijpq/dot_general | solution.py:54
  131.0 14.7 %copy.112 = bf16[16,64,32,32]{1,3,2,0:T(8,128)(2,1)} copy(bf16[16,64,32,32]{2,3,0,1:T(8,128)(2,1)} %convert_bitcast_fusion) | data formatting | bytes 4194304 | tf_op jit(solution)/shard_map/convert_element_type | solution.py:54
  145.7 3.7 %fusion.308 = (f32[16,64]{1,0:T(8,128)S(1)}, f32[16,64,128]{2,1,0:T(8,128)S(1)}) fusion(f32[16,64]{1,0:T(8,128)S(1)} %convolution_add_fusion, bf16[16,64,32,32]{1,3,2,0:T(8,128)(2,1)} %copy.112, bf16[2,32,32,128]{3,2,1,0:T(8,128)(2,1)S(1)} %copy-done.20, bf16[16,64,128]{2,1,0:T(8,128)(2,1)S(1)} %copy-done.6), kind=kOutput, calls=%fused_computation.396 | convolution fusion | flops 269220864 | bytes 3158016 | tf_op jit(solution)/shard_map/ijpq,pqc->ijc/dot_general | solution.py:55
  150.3 5.2 %all_gather.26 = bf16[4,64,64]{2,0,1:T(4,128)(2,1)S(1)} all-gather(bf16[4,16,64]{2,0,1:T(4,128)(2,1)S(1)} %fusion.137), channel_id=1, replica_groups=mesh['data'=4,'dap'=4] {'dap'}, dimensions={1}, use_global_device_ids=true | all-gather | bytes 40960 | tf_op jit(solution)/shard_map/all_gather | solution.py:79
  156.5 2.4 fusion.309
  158.9 2.2 fusion.118
  162.0 3.8 %all-to-all-start.2 = ((bf16[16,64,128]{2,0,1:T(8,128)(2,1)}), bf16[16,64,128]{2,0,1:T(8,128)(2,1)S(1)}, u32[]{:S(2)}, u32[]{:S(2)}) async-start(bf16[16,64,128]{2,0,1:T(8,128)(2,1)} %copy.116), calls=%async_computation.2 | async-start | bytes 524288 | tf_op jit(solution)/shard_map/all_to_all | solution.py:81
  165.8 12.9 %fusion.307 = (f32[16,16,128]{2,1,0:T(8,128)}, f32[16,16,128,128]{2,3,1,0:T(8,128)}) fusion(pred[16,128]{1,0:T(8,128)(4,1)S(1)} %compare_bitcast_fusion, bf16[128,16,4,16,24]{0,4,3,2,1:T(8,128)(2,1)} %convolution_convert_fusion.2), kind=kOutput, calls=%fused_computation.395 | convolution fusion | flops 218103936 | bytes 20056064 | tf_op jit(solution)/shard_map/sub | solution.py:38
  178.6 8.7 %convert_reduce_fusion.2 = (f32[128,16]{0,1:T(8,128)S(1)}, bf16[128,16,384]{2,0,1:T(8,128)(2,1)S(1)}) fusion(bf16[2,16,24,384]{3,2,1,0:T(8,128)(2,1)} %param.25, f32[16,16,128,128]{2,3,1,0:T(8,128)} %get-tuple-element.18, f32[16,16,128]{2,1,0:T(8,128)} %get-tuple-element.17, bf16[128,16,4,16,24]{0,4,3,2,1:T(8,128)(2,1)} %convolution_convert_fusion.2, ...), kind=kOutput, calls=%fused_computation.61 | convolution fusion | flops 822343680 | bytes 23502848 | tf_op jit(solution)/shard_map/abhd,hdc->abc/dot_general | solution.py:44
  187.4 2.1 copy.110
  191.6 7.7 %all-gather.1 = bf16[128,64,1,32]{0,3,2,1:T(8,128)(2,1)S(1)} all-gather(bf16[128,16,1,32]{0,3,2,1:T(8,128)(2,1)S(1)} %slice.275), channel_id=3, replica_groups=mesh['data'=4,'dap'=4] {'dap'}, dimensions={1}, use_global_device_ids=true | all-gather | bytes 655360 | tf_op jit(solution)/shard_map/all_gather | solution.py:89
  199.3 2.6 fusion.101
  203.8 5.4 %all_gather.27 = bf16[4,64,64]{2,0,1:T(4,128)(2,1)S(1)} all-gather(bf16[4,16,64]{2,0,1:T(4,128)(2,1)S(1)} %copy.120), channel_id=1, replica_groups=mesh['data'=4,'dap'=4] {'dap'}, dimensions={1}, use_global_device_ids=true | all-gather | bytes 40960 | tf_op jit(solution)/shard_map/all_gather | solution.py:83
  214.0 5.0 %fusion.310 = (f32[16,4,64]{2,1,0:T(4,128)S(1)}, f32[16,4,64,64]{2,3,1,0:T(8,128)}) fusion(f32[4,64,64]{1,2,0:T(8,128)} %copy.122, pred[64]{0:T(512)(128)(4,1)S(1)} %broadcast_compare_fusion.1, bf16[64,16,4,32]{3,1,2,0:T(8,128)(2,1)S(1)} %get-tuple-element.8, bf16[64,16,4,32]{3,1,2,0:T(8,128)(2,1)S(1)} %get-tuple-element.7), kind=kOutput, calls=%fused_computation.398 | convolution fusion | flops 18088000 | bytes 1654848 | tf_op jit(solution)/shard_map/sub | solution.py:38
  219.1 2.9 fusion.146
  222.0 1.8 copy.125
  223.9 2.2 fusion.315
  228.1 3.2 convolution_convert_fusion.4
  231.4 5.4 %all_gather.30 = bf16[4,64,64]{2,0,1:T(4,128)(2,1)S(1)} all-gather(bf16[4,16,64]{2,0,1:T(4,128)(2,1)S(1)} %copy.135), channel_id=1, replica_groups=mesh['data'=4,'dap'=4] {'dap'}, dimensions={1}, use_global_device_ids=true | all-gather | bytes 40960 | tf_op jit(solution)/shard_map/all_gather | solution.py:94
  237.6 2.6 slice_bitcast_fusion.57
  240.2 5.0 %fusion.317 = (f32[16,4,64]{2,1,0:T(4,128)S(1)}, f32[16,4,64,64]{2,3,1,0:T(8,128)}) fusion(f32[4,64,64]{1,2,0:T(8,128)} %copy.137, pred[64]{0:T(512)(128)(4,1)S(1)} %broadcast_compare_fusion.1, bf16[64,16,4,32]{3,1,2,0:T(8,128)(2,1)S(1)} %get-tuple-element.5, bf16[64,16,4,32]{3,1,2,0:T(8,128)(2,1)S(1)} %get-tuple-element.4), kind=kOutput, calls=%fused_computation.401 | convolution fusion | flops 18088000 | bytes 1654848 | tf_op jit(solution)/shard_map/sub | solution.py:38
  245.3 2.9 fusion.141
  250.0 2.7 fusion.114
  252.7 3.4 %all-to-all-start.3 = ((bf16[64,16,128]{2,1,0:T(8,128)(2,1)}), bf16[64,16,128]{2,1,0:T(8,128)(2,1)S(1)}, u32[]{:S(2)}, u32[]{:S(2)}) async-start(bf16[64,16,128]{2,1,0:T(8,128)(2,1)} %fusion.114), calls=%async_computation.3 | async-start | bytes 524288 | tf_op jit(solution)/shard_map/all_to_all | solution.py:96
  256.9 7.3 %all_gather.28 = bf16[16,64,64]{1,0,2:T(8,128)(2,1)S(1)} all-gather(bf16[16,64,16]{1,0,2:T(8,128)(2,1)S(1)} %copy.126), channel_id=1, replica_groups=mesh['data'=4,'dap'=4] {'dap'}, dimensions={2}, use_global_device_ids=true | all-gather | bytes 163840 | tf_op jit(solution)/shard_map/all_gather | solution.py:86
  265.4 3.7 %all-to-all-start.1 = ((bf16[128,16,384]{2,1,0:T(8,128)(2,1)}), bf16[128,16,384]{2,1,0:T(8,128)(2,1)S(1)}, u32[]{:S(2)}, u32[]{:S(2)}) async-start(bf16[128,16,384]{2,1,0:T(8,128)(2,1)} %copy.110), calls=%async_computation.1 | async-start | bytes 3145728 | tf_op jit(solution)/shard_map/all_to_all | solution.py:91
  270.4 19.7 %all_gather.31 = bf16[4,64,64]{2,0,1:T(4,128)(2,1)S(1)} all-gather(bf16[4,16,64]{2,0,1:T(4,128)(2,1)S(1)} %fusion.138), channel_id=1, replica_groups=mesh['data'=4,'dap'=4] {'dap'}, dimensions={1}, use_global_device_ids=true | all-gather | bytes 40960 | tf_op jit(solution)/shard_map/all_gather | solution.py:98
  290.3 2.1 convolution_convert_fusion.6
  292.4 3.6 %fusion.322 = (f32[16,4,64]{2,1,0:T(4,128)S(1)}, f32[16,4,64,64]{2,3,1,0:T(8,128)}) fusion(f32[4,64,64]{1,2,0:T(8,128)S(1)} %copy.144, pred[64]{0:T(512)(128)(4,1)S(1)} %broadcast_compare_fusion.1, bf16[16,64,4,4,32]{1,4,3,2,0:T(8,128)(2,1)} %convolution_convert_fusion.6), kind=kOutput, calls=%fused_computation.402 | convolution fusion | flops 18088000 | bytes 2179136 | tf_op jit(solution)/shard_map/sub | solution.py:38
  296.0 3.1 fusion.117
  300.6 2.1 copy.111
  303.4 9.2 %convolution_convert_fusion = bf16[32,64,4,16,24]{1,4,3,2,0:T(8,128)(2,1)} fusion(bf16[32,64,384,1,1]{2,1,4,3,0:T(8,128)(2,1)S(1)} %bitcast.638, bf16[2,384,4,16,24]{1,4,3,2,0:T(8,128)(2,1)S(1)} %copy-done.19), kind=kOutput, calls=%fused_computation.45 | convolution fusion | flops 2419064832 | bytes 9043968 | tf_op jit(solution)/shard_map/abc,cfhd->abfhd/dot_general | solution.py:25
  312.6 13.7 %fusion.316 = (f32[32,16,64]{2,1,0:T(8,128)S(1)}, f32[32,16,64,64]{2,3,1,0:T(8,128)}) fusion(f32[16,64,64]{1,2,0:T(8,128)} %copy.128, pred[32,64]{1,0:T(8,128)(4,1)S(1)} %copy-done.15, bf16[32,64,4,16,24]{1,4,3,2,0:T(8,128)(2,1)} %convolution_convert_fusion), kind=kOutput, calls=%fused_computation.400 | convolution fusion | flops 111149120 | bytes 15337472 | tf_op jit(solution)/shard_map/sub | solution.py:38
  326.3 11.1 %fusion.57 = bf16[32,64,384]{2,1,0:T(8,128)(2,1)} fusion(f32[4,32,16,384]{3,2,0,1:T(8,128)S(1)} %copy-done.3, bf16[32,64,4,16,24]{1,4,3,2,0:T(8,128)(2,1)} %convolution_convert_fusion, f32[32,16,64,64]{2,3,1,0:T(8,128)} %get-tuple-element.30, f32[32,16,64]{2,1,0:T(8,128)S(1)} %get-tuple-element.29, bf16[2,16,24,384]{3,2,1,0:T(8,128)(2,1)} %param.23), kind=kOutput, calls=%fused_computation.88 | convolution fusion | flops 715128832 | bytes 28213248 | tf_op jit(solution)/shard_map/abhd,hdc->abc/dot_general | solution.py:44
  (147 shorter events, 31.9 us)
Async XLA Ops:
  0.6 5.8 %copy-start.6 = (bf16[16,64,128]{2,1,0:T(8,128)(2,1)S(1)}, bf16[16,64,128]{2,1,0:T(8,128)(2,1)}, u32[]{:S(2)}) copy-start(bf16[16,64,128]{2,1,0:T(8,128)(2,1)} %param.18) | copy-start | bytes 786436
  0.6 4.5 %copy-start.1 = (bf16[32,64,384]{2,1,0:T(8,128)(2,1)S(1)}, bf16[32,64,384]{2,1,0:T(8,128)(2,1)}, u32[]{:S(2)}) copy-start(bf16[32,64,384]{2,1,0:T(8,128)(2,1)} %param.17) | copy-start | bytes 4718596
  0.7 5.6 %copy-start.13 = (s32[128,64]{0,1:T(8,128)S(1)}, s32[128,64]{0,1:T(8,128)}, u32[]{:S(2)}) copy-start(s32[128,64]{0,1:T(8,128)} %param.19) | copy-start | bytes 98308
  0.7 5.7 %copy-start.26 = (bf16[2,128,16]{1,2,0:T(8,128)(2,1)S(1)}, bf16[2,128,16]{1,2,0:T(8,128)(2,1)}, u32[]{:S(2)}) copy-start(bf16[2,128,16]{1,2,0:T(8,128)(2,1)} %param.21) | copy-start | bytes 24580
  6.4 19.3 %copy-start.14 = (pred[32,64]{1,0:T(8,128)(4,1)}, pred[32,64]{1,0:T(8,128)(4,1)S(1)}, u32[]{:S(2)}) copy-start(pred[32,64]{1,0:T(8,128)(4,1)S(1)} %broadcast_compare_fusion) | copy-start | bytes 6148
  50.0 6.1 %copy-start.28 = (s32[64]{0:T(128)S(1)}, s32[64]{0:T(128)}, u32[]{:S(2)}) copy-start(s32[64]{0:T(128)} %param.20) | copy-start | bytes 772
  52.0 23.5 %all-to-all-start = ((bf16[32,64,384]{2,0,1:T(8,128)(2,1)}), bf16[32,64,384]{2,0,1:T(8,128)(2,1)S(1)}, u32[]{:S(2)}, u32[]{:S(2)}) async-start(bf16[32,64,384]{2,0,1:T(8,128)(2,1)} %copy.106), calls=%async_computation | async-start | bytes 3145728 | tf_op jit(solution)/shard_map/all_to_all | solution.py:73
  77.1 2.8 copy-start.18
  85.4 12.9 %copy-start.2 = (f32[32,4,16,384]{3,0,1,2:T(8,128)S(1)}, f32[32,4,16,384]{3,0,1,2:T(8,128)}, u32[]{:S(2)}) copy-start(f32[32,4,16,384]{3,0,1,2:T(8,128)} %copy.107) | copy-start | bytes 9437188
  110.2 7.4 %copy-start.4 = (bf16[128,16,384]{2,0,1:T(8,128)(2,1)S(1)}, bf16[128,16,384]{2,0,1:T(8,128)(2,1)}, u32[]{:S(2)}) copy-start(bf16[128,16,384]{2,0,1:T(8,128)(2,1)} %get-tuple-element.16) | copy-start | bytes 4718596
  110.2 7.3 %copy-start.22 = (bf16[2,384,2,32]{1,3,2,0:T(8,128)(2,1)S(1)}, bf16[2,384,2,32]{1,3,2,0:T(8,128)(2,1)}, u32[]{:S(2)}) copy-start(bf16[2,384,2,32]{1,3,2,0:T(8,128)(2,1)} %param.26) | copy-start | bytes 294916
  131.0 14.7 %copy-start.20 = (bf16[2,32,32,128]{3,2,1,0:T(8,128)(2,1)S(1)}, bf16[2,32,32,128]{3,2,1,0:T(8,128)(2,1)}, u32[]{:S(2)}) copy-start(bf16[2,32,32,128]{3,2,1,0:T(8,128)(2,1)} %param.27) | copy-start | bytes 1572868
  145.7 4.1 %copy-start.16 = (bf16[2,128,4]{1,2,0:T(4,128)(2,1)S(1)}, bf16[2,128,4]{1,2,0:T(4,128)(2,1)}, u32[]{:S(2)}) copy-start(bf16[2,128,4]{1,2,0:T(4,128)(2,1)} %param.28) | copy-start | bytes 6148
  145.7 9.9 %copy-start.11 = (bf16[2,128,4,4,32]{1,4,3,2,0:T(8,128)(2,1)S(1)}, bf16[2,128,4,4,32]{1,4,3,2,0:T(8,128)(2,1)}, u32[]{:S(2)}) copy-start(bf16[2,128,4,4,32]{1,4,3,2,0:T(8,128)(2,1)} %param.29) | copy-start | bytes 786436
  156.5 2.4 copy-start.24
  162.0 39.9 %all-to-all-start.2 = ((bf16[16,64,128]{2,0,1:T(8,128)(2,1)}), bf16[16,64,128]{2,0,1:T(8,128)(2,1)S(1)}, u32[]{:S(2)}, u32[]{:S(2)}) async-start(bf16[16,64,128]{2,0,1:T(8,128)(2,1)} %copy.116), calls=%async_computation.2 | async-start | bytes 524288 | tf_op jit(solution)/shard_map/all_to_all | solution.py:81
  165.8 12.9 %copy-start.5 = (bf16[128,16,384]{2,0,1:T(8,128)(2,1)S(1)}, bf16[128,16,384]{2,0,1:T(8,128)(2,1)}, u32[]{:S(2)}) copy-start(bf16[128,16,384]{2,0,1:T(8,128)(2,1)} %get-tuple-element.16) | copy-start | bytes 4718596
  187.4 3.0 copy-start.23
  189.5 9.8 %copy-start.21 = (bf16[2,32,32,128]{3,2,1,0:T(8,128)(2,1)S(1)}, bf16[2,32,32,128]{3,2,1,0:T(8,128)(2,1)}, u32[]{:S(2)}) copy-start(bf16[2,32,32,128]{3,2,1,0:T(8,128)(2,1)} %param.27) | copy-start | bytes 1572868
  199.3 3.7 %copy-start.17 = (bf16[2,128,4]{1,2,0:T(4,128)(2,1)S(1)}, bf16[2,128,4]{1,2,0:T(4,128)(2,1)}, u32[]{:S(2)}) copy-start(bf16[2,128,4]{1,2,0:T(4,128)(2,1)} %param.31) | copy-start | bytes 6148
  201.9 8.9 %copy-start.10 = (bf16[2,128,4,4,32]{1,4,3,2,0:T(8,128)(2,1)S(1)}, bf16[2,128,4,4,32]{1,4,3,2,0:T(8,128)(2,1)}, u32[]{:S(2)}) copy-start(bf16[2,128,4,4,32]{1,4,3,2,0:T(8,128)(2,1)} %param.32) | copy-start | bytes 786436
  212.1 1.9 copy-start
  223.8 2.2 copy-start.7
  226.0 0.8 copy-start.8
  250.0 6.1 %copy-start.9 = (f32[64,16,128]{2,1,0:T(8,128)S(1)}, f32[64,16,128]{2,1,0:T(8,128)}, u32[]{:S(2)}) copy-start(f32[64,16,128]{2,1,0:T(8,128)} %copy-done.8) | copy-start | bytes 1572868
  250.0 6.1 %copy-start.27 = (bf16[2,128,16]{1,2,0:T(8,128)(2,1)S(1)}, bf16[2,128,16]{1,2,0:T(8,128)(2,1)}, u32[]{:S(2)}) copy-start(bf16[2,128,16]{1,2,0:T(8,128)(2,1)} %param.21) | copy-start | bytes 24580
  252.7 12.7 %all-to-all-start.3 = ((bf16[64,16,128]{2,1,0:T(8,128)(2,1)}), bf16[64,16,128]{2,1,0:T(8,128)(2,1)S(1)}, u32[]{:S(2)}, u32[]{:S(2)}) async-start(bf16[64,16,128]{2,1,0:T(8,128)(2,1)} %fusion.114), calls=%async_computation.3 | async-start | bytes 524288 | tf_op jit(solution)/shard_map/all_to_all | solution.py:96
  265.4 24.9 %copy-start.12 = (bf16[2,128,4,4,32]{1,4,3,2,0:T(8,128)(2,1)S(1)}, bf16[2,128,4,4,32]{1,4,3,2,0:T(8,128)(2,1)}, u32[]{:S(2)}) copy-start(bf16[2,128,4,4,32]{1,4,3,2,0:T(8,128)(2,1)} %param.29) | copy-start | bytes 786436
  265.4 33.7 %all-to-all-start.1 = ((bf16[128,16,384]{2,1,0:T(8,128)(2,1)}), bf16[128,16,384]{2,1,0:T(8,128)(2,1)S(1)}, u32[]{:S(2)}, u32[]{:S(2)}) async-start(bf16[128,16,384]{2,1,0:T(8,128)(2,1)} %copy.110), calls=%async_computation.1 | async-start | bytes 3145728 | tf_op jit(solution)/shard_map/all_to_all | solution.py:91
  292.4 3.6 %copy-start.25 = (bf16[2,4,32,128]{3,2,1,0:T(8,128)(2,1)S(1)}, bf16[2,4,32,128]{3,2,1,0:T(8,128)(2,1)}, u32[]{:S(2)}) copy-start(bf16[2,4,32,128]{3,2,1,0:T(8,128)(2,1)} %param.30) | copy-start | bytes 196612
  300.5 2.8 copy-start.19
  303.4 9.2 %copy-start.15 = (pred[32,64]{1,0:T(8,128)(4,1)S(1)}, pred[32,64]{1,0:T(8,128)(4,1)}, u32[]{:S(2)}) copy-start(pred[32,64]{1,0:T(8,128)(4,1)} %copy-done.14) | copy-start | bytes 6148
  312.6 13.7 %copy-start.3 = (f32[4,32,16,384]{3,2,0,1:T(8,128)S(1)}, f32[4,32,16,384]{3,2,0,1:T(8,128)}, u32[]{:S(2)}) copy-start(f32[4,32,16,384]{3,2,0,1:T(8,128)} %copy.111) | copy-start | bytes 9437188
where the time goes:
time: 341 us; the launch traced here: 338 us
  matrix products  183 us (54%)
  blocking collectives  65.2 us (19%)
  local copies, waits for them, and re-layouts  37 us (11%)
  waiting for transfers between devices  19.5 us (6%)
  other arithmetic  16.6 us (5%)
  starting transfers between devices  14.6 us (4%)
    sub x8, matrix products, gated_attention(): attn_probs = jax.nn.softmax(logits, axis=-1).astype(jnp.bfloat16)  69.8 us
    dot_general x8, matrix products, gated_attention(): jnp.einsum('abhd,hdc->abc', gated, w_out, preferred_element_type=jnp.floa...  49.7 us
    dot_general x8, matrix products, gated_attention(): jnp.einsum('abc,cfhd->abfhd', x_ln, w_in, preferred_element_type=jnp.floa...  39.9 us
    all_gather x1, blocking collectives, local_step(): lax.all_gather(pair_bias(pair_ln, w_ts_bias[1], 'ijc,ch->hij'), 'dap', ax...  19.7 us
    all_to_all x1, waiting for transfers between devices, local_step(): value_a7 = lax.all_to_all(value_a7, 'dap', 1, 0, tiled=True)  19.5 us
    convert_element_type x1, local copies, waits for them, and re-layouts, opm_update(): jnp.einsum('sip,sjq->ijpq', left, right, preferred_element_type=jnp.float32)  14.7 us
    convert_element_type x7, local copies, waits for them, and re-layouts, add_residual(): return (current.astype(jnp.float32) + update).astype(jnp.bfloat16)  10.1 us
    reduce_sum x10, other arithmetic, layer_norm(): row_var = jnp.mean(centered * centered, axis=-1, keepdims=True)  8.46 us
  transfers between devices with their start and end apart: 4, of which 1 were waited for; matrix products, arithmetic and copies ran while one was open for 12% of the time, Pallas kernels for 0%

commit v1 on v0

v1 whole, which is shorter than its diff:
```python
import functools

import jax
import jax.numpy as jnp
from jax import lax
from jax.experimental import pallas as pl
from jax.experimental.pallas import tpu as pltpu
from jax.sharding import PartitionSpec as P

LOG2E = 1.4426950408889634
NEG = -1e9 * LOG2E
F32 = jnp.float32
BF16 = jnp.bfloat16
NT = (((1,), (1,)), ((), ()))


def layer_norm(values):
    flat = values.astype(F32)
    row_mean = jnp.mean(flat, axis=-1, keepdims=True)
    centered = flat - row_mean
    row_var = jnp.mean(centered * centered, axis=-1, keepdims=True)
    return (centered * lax.rsqrt(row_var + 1e-5)).astype(BF16)


def half_masks(rows, split):
    index = lax.broadcasted_iota(jnp.int32, (rows, 128), 0)
    upper = (index < split).astype(F32).astype(BF16)
    lower = (index >= split).astype(F32).astype(BF16)
    return upper, lower


def attend(x, w_ref, wo_ref, pt_ref, gt_ref, heads, dim, keep, bias_ref):
    width = heads * dim
    rows = 2 * dim
    x_ln = layer_norm(x)
    for part in range(4):
        sl = pl.ds(part * width, width)
        pt_ref[sl, :] = lax.dot_general(w_ref[sl, :], x_ln, NT, preferred_element_type=F32).astype(BF16)
    up, low = half_masks(rows, dim)
    scale = dim ** -0.5 * LOG2E
    if bias_ref is not None:
        left = lax.broadcasted_iota(jnp.int32, (64, 128), 1) < 64
        left_b = left.astype(F32).astype(BF16)
        right_b = (1.0 - left.astype(F32)).astype(BF16)
    for blk in range(2):
        ln = pl.ds(blk * 128, 128)
        for hp in range(heads // 2):
            r = rows * hp
            q = pt_ref[pl.ds(r, rows), ln]
            k = pt_ref[pl.ds(width + r, rows), ln]
            v = pt_ref[pl.ds(2 * width + r, rows), ln]
            g = pt_ref[pl.ds(3 * width + r, rows), ln]
            rhs = jnp.concatenate([q * up, q * low], axis=1)
            logits2 = jnp.dot(k.T, rhs, preferred_element_type=F32)
            probs = []
            for half in range(2):
                lg = logits2[:, 128 * half:128 * half + 128]
                if bias_ref is not None:
                    lg = jnp.where(left, lg[0:64], lg[64:128]) * scale + bias_ref[2 * hp + half]
                else:
                    lg = lg * scale
                lg = jnp.where(keep[blk], lg, NEG)
                e = jnp.exp2(lg - jnp.max(lg, axis=0, keepdims=True))
                p = (e * (1.0 / jnp.sum(e, axis=0, keepdims=True))).astype(BF16)
                if bias_ref is not None:
                    probs += [p * left_b, p * right_b]
                else:
                    probs += [p]
            att = jnp.dot(jnp.concatenate([v * up, v * low], axis=1), jnp.concatenate(probs, axis=0),
                          preferred_element_type=F32)
            gt_ref[pl.ds(r, rows), ln] = (att * jax.nn.sigmoid(g.astype(F32))).astype(BF16)
    update = jnp.dot(gt_ref[...].T, wo_ref[...], preferred_element_type=F32)
    return (x + update).astype(BF16)


def pick_column(table, col):
    lane = lax.broadcasted_iota(jnp.int32, table.shape, 1)
    return jnp.sum(jnp.where(lane == col, table, 0.0), axis=1, keepdims=True)


def row_kernel(heads, dim, per_row, x_ref, keys_ref, bias_ref, w_ref, wo_ref, out_ref, pt_ref, gt_ref):
    step = pl.program_id(0)
    x = x_ref[...].astype(F32).reshape(256, x_ref.shape[-1])
    left = lax.broadcasted_iota(jnp.int32, (64, 128), 1) < 64
    keep = []
    for blk in range(2):
        if per_row:
            keys = keys_ref[...]
            first = pick_column(keys, step * 4 + 2 * blk)
            second = pick_column(keys, step * 4 + 2 * blk + 1)
            keep.append(jnp.where(left, first, second) > 0.5)
        else:
            keep.append(jnp.broadcast_to(keys_ref[...], (64, 128)) > 0.5)
    out = attend(x, w_ref, wo_ref, pt_ref, gt_ref, heads, dim, keep, bias_ref)
    out_ref[...] = out.reshape(out_ref.shape)


def row_attention(x, keys, bias_t, w, wo, heads, dim, per_row):
    groups, length, width = x.shape
    inner = heads * dim
    bias_t = bias_t.astype(F32) * LOG2E
    bias_t = jnp.concatenate([bias_t, bias_t], axis=2)
    return pl.pallas_call(
        functools.partial(row_kernel, heads, dim, per_row),
        grid=(groups // 4,),
        in_specs=[
            pl.BlockSpec((4, length, width), lambda i: (i, 0, 0)),
            pl.BlockSpec(keys.shape, lambda i: (0, 0)),
            pl.BlockSpec(bias_t.shape, lambda i: (0, 0, 0)),
            pl.BlockSpec(w.shape, lambda i: (0, 0)),
            pl.BlockSpec(wo.shape, lambda i: (0, 0)),
        ],
        out_specs=pl.BlockSpec((4, length, width), lambda i: (i, 0, 0)),
        out_shape=jax.ShapeDtypeStruct(x.shape, BF16),
        scratch_shapes=[pltpu.VMEM((4 * inner, 256), BF16), pltpu.VMEM((inner, 256), BF16)],
        cost_estimate=pl.CostEstimate(flops=groups * length * width * inner * 10, bytes_accessed=x.size * 4, transcendentals=0),
        name="row_att" if per_row else "tri_att",
    )(x, keys, bias_t, w, wo)


def col_kernel(x_ref, keys_ref, lanes_ref, w1_ref, wo1_ref, wp1_ref, w2_ref, wo2_ref, wp2_ref,
               out_ref, ac1_ref, ac2_ref, pt_ref, gt_ref):
    step = pl.program_id(0)
    x = x_ref[...].astype(F32).reshape(256, 384)
    keep = [jnp.broadcast_to(pick_column(keys_ref[...], step * 2 + blk), (128, 128)) > 0.5 for blk in range(2)]
    lane_mask = jnp.concatenate([lanes_ref[0], lanes_ref[1]], axis=1)
    for w_ref, wo_ref, wp_ref, ac_ref in ((w1_ref, wo1_ref, wp1_ref, ac1_ref), (w2_ref, wo2_ref, wp2_ref, ac2_ref)):
        out = attend(x, w_ref, wo_ref, pt_ref, gt_ref, 16, 24, keep, None)
        x = out.astype(F32)
        ac = lax.dot_general(wp_ref[...], layer_norm(x), NT, preferred_element_type=F32)
        ac_ref[0] = (ac * lane_mask).astype(BF16)
    out_ref[...] = out.reshape(out_ref.shape)


def column_pair(x, keys, lanes, weights):
    whole = lambda a: pl.BlockSpec(a.shape, lambda i: (0,) * a.ndim)
    return pl.pallas_call(
        col_kernel,
        grid=(8,),
        in_specs=[
            pl.BlockSpec((2, 128, 384), lambda i: (i, 0, 0)),
            whole(keys),
            pl.BlockSpec((2, 1, 128), lambda i: (i, 0, 0)),
        ] + [whole(a) for a in weights],
        out_specs=[
            pl.BlockSpec((2, 128, 384), lambda i: (i, 0, 0)),
            pl.BlockSpec((1, 64, 256), lambda i: (i, 0, 0)),
            pl.BlockSpec((1, 64, 256), lambda i: (i, 0, 0)),
        ],
        out_shape=[
            jax.ShapeDtypeStruct(x.shape, BF16),
            jax.ShapeDtypeStruct((8, 64, 256), BF16),
            jax.ShapeDtypeStruct((8, 64, 256), BF16),
        ],
        scratch_shapes=[pltpu.VMEM((1536, 256), BF16), pltpu.VMEM((384, 256), BF16)],
        cost_estimate=pl.CostEstimate(flops=2048 * 384 * 384 * 20, bytes_accessed=x.size * 4, transcendentals=0),
        name="col_att",
    )(x, keys, lanes, *weights)


def opm_kernel(own_ref, full_ref, z_ref, norm_ref, w_ref, out_ref, full32_ref, o_ref):
    full32_ref[...] = full_ref[...].astype(F32)
    own = own_ref[...]
    zeros = jnp.zeros((64, 128), BF16)

    def one(q, carry):
        c_q = full32_ref[pl.ds(q, 64, stride=32), :].astype(BF16)
        rhs = jnp.concatenate([jnp.concatenate([c_q, zeros], axis=1), jnp.concatenate([zeros, c_q], axis=1)], axis=0)
        o = lax.dot_general(own, rhs, NT, preferred_element_type=F32).astype(BF16)
        for pair in range(8):
            o_ref[pair, pl.ds(pl.multiple_of(q * 32, 32), 32), :] = o[32 * pair:32 * pair + 32]
        return carry

    lax.fori_loop(0, 32, one, 0, unroll=4)
    w = w_ref[...]
    for pair in range(8):
        update = jnp.dot(w, o_ref[pair], preferred_element_type=F32).T
        z = z_ref[pl.ds(2 * pair, 2)].astype(F32).reshape(128, 128)
        norm = norm_ref[...]
        norm = jnp.concatenate([pick_column(norm, 2 * pair), pick_column(norm, 2 * pair + 1)], axis=0)
        out_ref[pl.ds(2 * pair, 2)] = (z + update / (1e-3 + norm)).astype(BF16).reshape(2, 64, 128)


def opm(own, full, z, norm, w):
    return pl.pallas_call(
        opm_kernel,
        out_shape=jax.ShapeDtypeStruct(z.shape, BF16),
        scratch_shapes=[pltpu.VMEM((2048, 128), F32), pltpu.VMEM((8, 1024, 128), BF16)],
        cost_estimate=pl.CostEstimate(flops=10 ** 9, bytes_accessed=2 ** 20, transcendentals=0),
        name="opm",
    )(own, full, z, norm, w)


def solution(mesh):
    def local_step(m, z, mask, res_mask, w_row_bias, w_row_in, w_row_out, w_col_in, w_col_out, w_opm_in, w_opm_out, w_ts_bias, w_ts_in, w_ts_out, w_te_bias, w_te_in, w_te_out):
        dev = lax.axis_index('dap')
        flat_in = lambda w: jnp.transpose(w, (0, 2, 3, 4, 1)).reshape(2, -1, w.shape[1])
        flat_out = lambda w: w.reshape(2, -1, w.shape[-1])
        w_row_in, w_col_in, w_ts_in, w_te_in = map(flat_in, (w_row_in, w_col_in, w_ts_in, w_te_in))
        w_row_out, w_col_out, w_ts_out, w_te_out = map(flat_out, (w_row_out, w_col_out, w_ts_out, w_te_out))
        w_opm_in = jnp.transpose(w_opm_in, (0, 2, 3, 1)).reshape(2, 64, 384)
        w_opm_1 = jnp.transpose(w_opm_out[0], (2, 1, 0)).reshape(128, 1024)
        w_opm_2 = jnp.transpose(w_opm_out[1], (2, 0, 1)).reshape(128, 1024)

        mask_f = mask.astype(F32)
        row_keys = lax.dynamic_slice_in_dim(mask_f, dev * 32, 32, 0).T
        col_keys = lax.dynamic_slice_in_dim(mask_f, dev * 16, 16, 1)
        lanes = col_keys.T.reshape(16, 1, 128)
        tri_keys = res_mask.astype(F32).reshape(64, 1)
        norm = jnp.dot(mask_f.T, col_keys)

        def bias(z_blk, w, form, axis):
            part = jnp.einsum(form, layer_norm(z_blk), w, preferred_element_type=F32).astype(BF16)
            return lax.all_gather(part, 'dap', axis=axis, tiled=True)

        def gather_full(half):
            full = lax.all_gather(half.reshape(8, 32, 2, 128).transpose(0, 2, 1, 3).reshape(512, 128), 'dap', axis=0, tiled=True)
            return full

        row_bias = bias(z, w_row_bias[0], 'ijc,ch->hji', 2)
        m = row_attention(m, row_keys, row_bias, w_row_in[0], w_row_out[0], 16, 24, True)
        m = lax.all_to_all(m, 'dap', 1, 0, tiled=True)
        m = jnp.transpose(m, (1, 0, 2))
        m, ac1, ac2 = column_pair(m, col_keys, lanes, (w_col_in[0], w_col_out[0], w_opm_in[0], w_col_in[1], w_col_out[1], w_opm_in[1]))
        z = opm(ac1[:, :32].reshape(256, 256), gather_full(ac1[:, 32:]), z, norm, w_opm_1)
        ts_bias = bias(z, w_ts_bias[0], 'ijc,ch->hji', 2)
        z = row_attention(z, tri_keys, ts_bias, w_ts_in[0], w_ts_out[0], 4, 32, False)
        z = jnp.transpose(lax.all_to_all(z, 'dap', 1, 0, tiled=True), (1, 0, 2))
        te_bias = bias(z, w_te_bias[0], 'ijc,ch->hji', 2)
        z = row_attention(z, tri_keys, te_bias, w_te_in[0], w_te_out[0], 4, 32, False)

        row_bias = bias(z, w_row_bias[1], 'jic,ch->hji', 1)
        z = opm(ac2[:, 32:].reshape(256, 256), gather_full(ac2[:, :32]), z, norm, w_opm_2)
        m = lax.all_to_all(jnp.transpose(m, (1, 0, 2)), 'dap', 0, 1, tiled=True)
        m = row_attention(m, row_keys, row_bias, w_row_in[1], w_row_out[1], 16, 24, True)
        te_bias = bias(z, w_te_bias[1], 'ijc,ch->hji', 2)
        z = row_attention(z, tri_keys, te_bias, w_te_in[1], w_te_out[1], 4, 32, False)
        z = lax.all_to_all(jnp.transpose(z, (1, 0, 2)), 'dap', 0, 1, tiled=True)
        ts_bias = bias(z, w_ts_bias[1], 'ijc,ch->hji', 2)
        z = row_attention(z, tri_keys, ts_bias, w_ts_in[1], w_ts_out[1], 4, 32, False)
        return m, z

    in_specs = (P(('data', 'dap')), P(('data', 'dap')), P('data'), P('data')) + (P(),) * 13
    out_specs = (P(('data', 'dap')), P(('data', 'dap')))
    return jax.shard_map(local_step, mesh=mesh, in_specs=in_specs, out_specs=out_specs, check_vma=False)
```

time: 341 us -> 345 us (1.012)
  Pallas kernels: 0 us -> 204 us
  matrix products: 183 us -> 6.46 us
  waiting for transfers between devices: 19.5 us -> 7.85 us
  local copies, waits for them, and re-layouts: 37 us -> 29.7 us
    pallas_call x0 -> x9, Pallas kernels: none -> 204 us  [the longest x6 110 us: row_attention(): pl.pallas_call(functools.partial(row_kernel, heads, dim, per_row), grid=(...]
    dot_general x30 -> x7, matrix products: 113 us -> 6.46 us  [the longest x6 5.72 us: bias(): jnp.einsum(form, layer_norm(z_blk), w, preferred_element_type=F32)]
    sub x8 -> x0, matrix products: 69.8 us -> none  [gated_attention(): attn_probs = jax.nn.softmax(logits, axis=-1).astype(jnp.bfloat16)]
    convert_element_type x18 -> x0, local copies, waits for them, and re-layouts: 28.2 us -> none  [the longest x1 14.7 us: opm_update(): jnp.einsum('sip,sjq->ijpq', left, right, preferred_element_type=jnp.float32)]
    all_to_all x4, waiting for transfers between devices: 19.5 us -> 7.85 us  [the longest x1 7.85 us: local_step(): m = lax.all_to_all(m, 'dap', 1, 0, tiled=True)]
    slice x2 -> x10, local copies, waits for them, and re-layouts: 0.02 us -> 10.2 us  [the longest x1 3.31 us: local_step(): w_col_in[1]]
    pallas_call x0 -> x2, local copies, waits for them, and re-layouts: none -> 5.32 us  [row_attention(): pl.pallas_call(functools.partial(row_kernel, heads, dim, per_row), grid=(...]
    concatenate x0 -> x6, other arithmetic: none -> 5.1 us  [row_attention(): bias_t = jnp.concatenate([bias_t, bias_t], axis=2)]
  transfers between devices with their start and end apart: 4 -> 4, of which waited for: 1 -> 1; matrix products, arithmetic and copies ran while one was open for 12% -> 5% of each run, Pallas kernels for 0% -> 2%
where the time goes in v1:
time: 345 us; the launch traced here: 344 us
  Pallas kernels  204 us (59%)
  blocking collectives  63.8 us (18%)
  local copies, waits for them, and re-layouts  29.7 us (9%)
  other arithmetic  16.7 us (5%)
  starting transfers between devices  14.3 us (4%)
  waiting for transfers between devices  7.85 us (2%)
  matrix products  6.46 us (2%)
    pallas_call x6, Pallas kernels, row_attention(): pl.pallas_call(functools.partial(row_kernel, heads, dim, per_row), grid=(...  110 us
    pallas_call x1, Pallas kernels, column_pair(): pl.pallas_call(col_kernel, grid=(8,), in_specs=[pl.BlockSpec((2, 128, 384...  82.1 us
    all_gather x6, blocking collectives, bias(): return lax.all_gather(part, 'dap', axis=axis, tiled=True)  49.3 us
    all_gather x2, blocking collectives, gather_full(): lax.all_gather(half.reshape(8, 32, 2, 128).transpose(0, 2, 1, 3).reshape(...  14.5 us
    pallas_call x2, Pallas kernels, opm(): pl.pallas_call(opm_kernel, out_shape=jax.ShapeDtypeStruct(z.shape, BF16),...  11.1 us
    all_to_all x1, waiting for transfers between devices, local_step(): m = lax.all_to_all(m, 'dap', 1, 0, tiled=True)  7.85 us
  transfers between devices with their start and end apart: 4, of which 1 were waited for; matrix products, arithmetic and copies ran while one was open for 5% of the time, Pallas kernels for 2%

profile of v1, /device:TPU:0, one launch (start us, length us, event | category | flops | bytes accessed | tf_op | source)
XLA Modules:
  0.0 343.5 jit_solution(8563261637340696243)
XLA Ops:
  1.4 1.2 convert_reduce_fusion.5
  2.6 1.3 fusion.27
  3.9 1.6 fusion
  5.5 7.5 %all_gather.24 = bf16[16,64,64]{1,0,2:T(8,128)(2,1)S(1)} all-gather(bf16[16,64,16]{1,0,2:T(8,128)(2,1)S(1)} %fusion), channel_id=1, replica_groups=mesh['data'=4,'dap'=4] {'dap'}, dimensions={2}, use_global_device_ids=true | all-gather | bytes 163840 | tf_op jit(solution)/shard_map/all_gather | solution.py:214
  13.3 1.0 pad_maximum_fusion.bias_ref
  14.3 1.7 fusion.59
  16.0 0.9 fusion.61
  17.6 39.2 %row_att.2 = bf16[32,64,384]{2,1,0:T(8,128)(2,1)} custom-call(bf16[32,64,384]{2,1,0:T(8,128)(2,1)} %x_ref.1, f32[64,32]{1,0:T(8,128)} %dynamic-slice_bitcast_fusion.keys_ref, f32[16,64,128]{2,1,0:T(8,128)} %pad_maximum_fusion.bias_ref, bf16[1536,384]{1,0:T(8,128)(2,1)} %bitcast.146, bf16[384,384]{1,0:T(8,128)(2,1)} %bitcast.162), custom_call_target="tpu_custom_call" | custom-call | flops 3019898880 | bytes 3145728 | tf_op jit(solution)/shard_map/row_att/pallas_call | solution.py:103
  56.8 3.5 %copy.63 = bf16[32,64,384]{2,0,1:T(8,128)(2,1)} copy(bf16[32,64,384]{2,1,0:T(8,128)(2,1)} %row_att.2) | data formatting | bytes 3145728 | tf_op jit(solution)/shard_map/row_att/pallas_call | solution.py:103
  60.3 3.9 %all-to-all-start = ((bf16[32,64,384]{2,0,1:T(8,128)(2,1)}), bf16[32,64,384]{2,0,1:T(8,128)(2,1)S(1)}, u32[]{:S(2)}, u32[]{:S(2)}) async-start(bf16[32,64,384]{2,0,1:T(8,128)(2,1)} %copy.63), calls=%async_computation | async-start | bytes 3145728 | tf_op jit(solution)/shard_map/all_to_all | solution.py:222
  65.8 0.9 copy.72.w_ref
  68.6 0.9 copy.81.w_ref
  71.7 0.9 fusion.62
  72.6 3.3 fusion.60
  76.0 7.8 %all-to-all-done = bf16[32,64,384]{2,0,1:T(8,128)(2,1)S(1)} async-done(((bf16[32,64,384]{2,0,1:T(8,128)(2,1)}), bf16[32,64,384]{2,0,1:T(8,128)(2,1)S(1)}, u32[]{:S(2)}, u32[]{:S(2)}) %all-to-all-start) | async-done | bytes 1572896 | tf_op jit(solution)/shard_map/all_to_all | solution.py:222
  83.8 1.4 copy.64
  85.2 82.1 %col_att.1 = (bf16[16,128,384]{2,1,0:T(8,128)(2,1)}, bf16[8,64,256]{2,1,0:T(8,128)(2,1)}, bf16[8,64,256]{2,1,0:T(8,128)(2,1)}) custom-call(bf16[16,128,384]{2,1,0:T(8,128)(2,1)} %bitcast.141, f32[128,16]{1,0:T(8,128)} %copy.65.keys_ref, f32[16,1,128]{2,1,0:T(1,128)} %bitcast.173, bf16[1536,384]{1,0:T(8,128)(2,1)} %bitcast.145, bf16[384,384]{1,0:T(8,128)(2,1)} %bitcast.161, ...), custom_call_target="tpu_custom_call" | custom-call | flops 6039797760 | bytes 3145728 | tf_op jit(solution)/shard_map/col_att/pallas_call | solution.py:137
  167.3 1.8 slice_bitcast_fusion
  169.2 6.5 %all_gather.25.full_ref = bf16[2048,128]{1,0:T(8,128)(2,1)} all-gather(bf16[512,128]{1,0:T(8,128)(2,1)S(1)} %bitcast.154), channel_id=1, replica_groups=mesh['data'=4,'dap'=4] {'dap'}, dimensions={0}, use_global_device_ids=true | all-gather | bytes 655360 | tf_op jit(solution)/shard_map/all_gather | solution.py:217
  175.7 5.5 %opm.2.x_ref = bf16[16,64,128]{2,1,0:T(8,128)(2,1)} custom-call(bf16[256,256]{1,0:T(8,128)(2,1)} %bitcast.167, bf16[2048,128]{1,0:T(8,128)(2,1)} %all_gather.25.full_ref, bf16[16,64,128]{2,1,0:T(8,128)(2,1)} %z_ref.1, f32[64,16]{1,0:T(8,128)} %convolution_bitcast_fusion.norm_ref, bf16[128,1024]{1,0:T(8,128)(2,1)} %copy.72.w_ref), custom_call_target="tpu_custom_call" | custom-call | flops 1000000000 | bytes 1048576 | tf_op jit(solution)/shard_map/opm/pallas_call | solution.py:185
  181.2 1.2 convert_reduce_fusion.4
  182.4 1.3 fusion.25
  183.8 1.5 fusion.1
  185.3 5.2 %all_gather.26 = bf16[4,64,64]{1,0,2:T(4,128)(2,1)S(1)} all-gather(bf16[4,64,16]{1,0,2:T(4,128)(2,1)S(1)} %fusion.1), channel_id=1, replica_groups=mesh['data'=4,'dap'=4] {'dap'}, dimensions={2}, use_global_device_ids=true | all-gather | bytes 40960 | tf_op jit(solution)/shard_map/all_gather | solution.py:214
  191.4 8.0 %tri_att.4 = bf16[16,64,128]{2,1,0:T(8,128)(2,1)} custom-call(bf16[16,64,128]{2,1,0:T(8,128)(2,1)} %opm.2.x_ref, f32[64,1]{1,0:T(8,128)} %copy.74.keys_ref, f32[4,64,128]{2,1,0:T(8,128)} %pad_maximum_fusion.2.bias_ref, bf16[512,128]{1,0:T(8,128)(2,1)} %bitcast.158, bf16[128,128]{1,0:T(8,128)(2,1)} %bitcast.171), custom_call_target="tpu_custom_call" | custom-call | flops 167772160 | bytes 524288 | tf_op jit(solution)/shard_map/tri_att/pallas_call | solution.py:103
  199.5 1.8 copy.75
  201.3 3.4 all-to-all-start.2
  204.7 2.1 copy.67
  206.8 8.0 %all_gather.29.full_ref = bf16[2048,128]{1,0:T(8,128)(2,1)} all-gather(bf16[512,128]{1,0:T(8,128)(2,1)S(1)} %bitcast.153), channel_id=1, replica_groups=mesh['data'=4,'dap'=4] {'dap'}, dimensions={0}, use_global_device_ids=true | all-gather | bytes 655360 | tf_op jit(solution)/shard_map/all_gather | solution.py:217
  215.9 5.2 %all_gather.27 = bf16[4,64,64]{1,0,2:T(4,128)(2,1)S(1)} all-gather(bf16[4,64,16]{1,0,2:T(4,128)(2,1)S(1)} %fusion.2), channel_id=1, replica_groups=mesh['data'=4,'dap'=4] {'dap'}, dimensions={2}, use_global_device_ids=true | all-gather | bytes 40960 | tf_op jit(solution)/shard_map/all_gather | solution.py:214
  222.1 8.0 %tri_att.5.z_ref = bf16[16,64,128]{2,1,0:T(8,128)(2,1)} custom-call(bf16[16,64,128]{2,1,0:T(8,128)(2,1)} %bitcast.137, f32[64,1]{1,0:T(8,128)} %copy.74.keys_ref, f32[4,64,128]{2,1,0:T(8,128)} %pad_maximum_fusion.3.bias_ref, bf16[512,128]{1,0:T(8,128)(2,1)} %bitcast.157, bf16[128,128]{1,0:T(8,128)(2,1)} %bitcast.170), custom_call_target="tpu_custom_call" | custom-call | flops 167772160 | bytes 524288 | tf_op jit(solution)/shard_map/tri_att/pallas_call | solution.py:103
  230.1 1.2 convert_reduce_fusion.2
  231.3 5.5 %opm.3.x_ref = bf16[16,64,128]{2,1,0:T(8,128)(2,1)} custom-call(bf16[256,256]{1,0:T(8,128)(2,1)} %bitcast.166, bf16[2048,128]{1,0:T(8,128)(2,1)} %all_gather.29.full_ref, bf16[16,64,128]{2,1,0:T(8,128)(2,1)} %tri_att.5.z_ref, f32[64,16]{1,0:T(8,128)} %convolution_bitcast_fusion.norm_ref, bf16[128,1024]{1,0:T(8,128)(2,1)} %copy.81.w_ref), custom_call_target="tpu_custom_call" | custom-call | flops 1000000000 | bytes 1048576 | tf_op jit(solution)/shard_map/opm/pallas_call | solution.py:185
  236.8 1.2 convert_reduce_fusion.1
  238.0 1.3 fusion.19
  239.3 1.4 fusion.3
  240.8 5.4 %all_gather.30 = bf16[4,64,64]{1,0,2:T(4,128)(2,1)S(1)} all-gather(bf16[4,64,16]{1,0,2:T(4,128)(2,1)S(1)} %fusion.3), channel_id=1, replica_groups=mesh['data'=4,'dap'=4] {'dap'}, dimensions={2}, use_global_device_ids=true | all-gather | bytes 40960 | tf_op jit(solution)/shard_map/all_gather | solution.py:214
  247.0 8.0 %tri_att.6 = bf16[16,64,128]{2,1,0:T(8,128)(2,1)} custom-call(bf16[16,64,128]{2,1,0:T(8,128)(2,1)} %opm.3.x_ref, f32[64,1]{1,0:T(8,128)} %copy.74.keys_ref, f32[4,64,128]{2,1,0:T(8,128)} %pad_maximum_fusion.4.bias_ref, bf16[512,128]{1,0:T(8,128)(2,1)} %bitcast.156, bf16[128,128]{1,0:T(8,128)(2,1)} %bitcast.169), custom_call_target="tpu_custom_call" | custom-call | flops 167772160 | bytes 524288 | tf_op jit(solution)/shard_map/tri_att/pallas_call | solution.py:103
  255.1 1.8 copy.84
  256.9 3.4 all-to-all-start.3
  261.2 7.1 %all_gather.28 = bf16[16,64,64]{2,1,0:T(8,128)(2,1)S(1)} all-gather(bf16[16,16,64]{2,1,0:T(8,128)(2,1)S(1)} %bitcast.163), channel_id=1, replica_groups=mesh['data'=4,'dap'=4] {'dap'}, dimensions={1}, use_global_device_ids=true | all-gather | bytes 163840 | tf_op jit(solution)/shard_map/all_gather | solution.py:214
  268.4 1.0 pad_maximum_fusion.1.bias_ref
  269.4 3.6 %all-to-all-start.1 = ((bf16[128,16,384]{2,1,0:T(8,128)(2,1)}), bf16[128,16,384]{2,1,0:T(8,128)(2,1)S(1)}, u32[]{:S(2)}, u32[]{:S(2)}) async-start(bf16[128,16,384]{2,1,0:T(8,128)(2,1)} %copy.67), calls=%async_computation.1 | async-start | bytes 3145728 | tf_op jit(solution)/shard_map/all_to_all | solution.py:234
  275.0 18.9 %all_gather.31 = bf16[4,64,64]{1,0,2:T(4,128)(2,1)S(1)} all-gather(bf16[4,64,16]{1,0,2:T(4,128)(2,1)S(1)} %fusion.4), channel_id=1, replica_groups=mesh['data'=4,'dap'=4] {'dap'}, dimensions={2}, use_global_device_ids=true | all-gather | bytes 40960 | tf_op jit(solution)/shard_map/all_gather | solution.py:214
  294.1 0.8 pad_maximum_fusion.5.bias_ref
  294.8 8.0 %tri_att.7 = bf16[16,64,128]{2,1,0:T(8,128)(2,1)} custom-call(bf16[16,64,128]{2,1,0:T(8,128)(2,1)} %bitcast.147, f32[64,1]{1,0:T(8,128)} %copy.74.keys_ref, f32[4,64,128]{2,1,0:T(8,128)} %pad_maximum_fusion.5.bias_ref, bf16[512,128]{1,0:T(8,128)(2,1)} %bitcast.155, bf16[128,128]{1,0:T(8,128)(2,1)} %bitcast.168), custom_call_target="tpu_custom_call" | custom-call | flops 167772160 | bytes 524288 | tf_op jit(solution)/shard_map/tri_att/pallas_call | solution.py:103
  302.9 1.5 copy.68
  304.3 39.2 %row_att.3 = bf16[32,64,384]{2,1,0:T(8,128)(2,1)} custom-call(bf16[32,64,384]{2,1,0:T(8,128)(2,1)} %bitcast.142, f32[64,32]{1,0:T(8,128)} %dynamic-slice_bitcast_fusion.keys_ref, f32[16,64,128]{2,1,0:T(8,128)} %pad_maximum_fusion.1.bias_ref, bf16[1536,384]{1,0:T(8,128)(2,1)} %bitcast.143, bf16[384,384]{1,0:T(8,128)(2,1)} %bitcast.159), custom_call_target="tpu_custom_call" | custom-call | flops 3019898880 | bytes 3145728 | tf_op jit(solution)/shard_map/row_att/pallas_call | solution.py:103
  (93 shorter events, 14.5 us)
Async XLA Ops:
  3.9 10.4 %copy-start.1 = (bf16[2,384,4,16,24]{1,4,3,2,0:T(8,128)(2,1)S(1)}, bf16[2,384,4,16,24]{1,4,3,2,0:T(8,128)(2,1)}, u32[]{:S(2)}) copy-start(bf16[2,384,4,16,24]{1,4,3,2,0:T(8,128)(2,1)} %param.22) | copy-start | bytes 7077892
  14.3 1.7 copy-start.4
  60.3 4.7 %copy-start.10 = (bf16[2,384,2,32]{1,3,2,0:T(8,128)(2,1)S(1)}, bf16[2,384,2,32]{1,3,2,0:T(8,128)(2,1)}, u32[]{:S(2)}) copy-start(bf16[2,384,2,32]{1,3,2,0:T(8,128)(2,1)} %param.26) | copy-start | bytes 294916
  60.3 5.3 %copy-start.6 = (bf16[2,32,32,128]{3,2,1,0:T(8,128)(2,1)S(1)}, bf16[2,32,32,128]{3,2,1,0:T(8,128)(2,1)}, u32[]{:S(2)}) copy-start(bf16[2,32,32,128]{3,2,1,0:T(8,128)(2,1)} %param.27) | copy-start | bytes 1572868
  60.3 23.5 %all-to-all-start = ((bf16[32,64,384]{2,0,1:T(8,128)(2,1)}), bf16[32,64,384]{2,0,1:T(8,128)(2,1)S(1)}, u32[]{:S(2)}, u32[]{:S(2)}) async-start(bf16[32,64,384]{2,0,1:T(8,128)(2,1)} %copy.63), calls=%async_computation | async-start | bytes 3145728 | tf_op jit(solution)/shard_map/all_to_all | solution.py:222
  64.2 2.5 copy-start.17
  64.2 3.2 copy-start.12
  64.2 3.8 %copy-start.13 = (bf16[2,4,32,128]{3,2,1,0:T(8,128)(2,1)S(1)}, bf16[2,4,32,128]{3,2,1,0:T(8,128)(2,1)}, u32[]{:S(2)}) copy-start(bf16[2,4,32,128]{3,2,1,0:T(8,128)(2,1)} %param.33) | copy-start | bytes 196612
  64.2 5.3 %copy-start.11 = (f32[128,16]{0,1:T(8,128)}, f32[128,16]{0,1:T(8,128)S(1)}, u32[]{:S(2)}) copy-start(f32[128,16]{0,1:T(8,128)S(1)} %constant_dynamic-slice_fusion) | copy-start | bytes 24580
  65.0 4.5 %copy-start.9 = (s32[128,64]{0,1:T(8,128)S(1)}, s32[128,64]{0,1:T(8,128)}, u32[]{:S(2)}) copy-start(s32[128,64]{0,1:T(8,128)} %param.19) | copy-start | bytes 98308
  65.0 5.3 %copy-start.7 = (bf16[2,128,4,4,32]{1,4,3,2,0:T(8,128)(2,1)S(1)}, bf16[2,128,4,4,32]{1,4,3,2,0:T(8,128)(2,1)}, u32[]{:S(2)}) copy-start(bf16[2,128,4,4,32]{1,4,3,2,0:T(8,128)(2,1)} %param.29) | copy-start | bytes 786436
  65.6 5.4 %copy-start.8 = (bf16[2,128,4,4,32]{1,4,3,2,0:T(8,128)(2,1)S(1)}, bf16[2,128,4,4,32]{1,4,3,2,0:T(8,128)(2,1)}, u32[]{:S(2)}) copy-start(bf16[2,128,4,4,32]{1,4,3,2,0:T(8,128)(2,1)} %param.32) | copy-start | bytes 786436
  65.7 6.1 %copy-start.5 = (bf16[2,16,24,384]{3,2,1,0:T(8,128)(2,1)S(1)}, bf16[2,16,24,384]{3,2,1,0:T(8,128)(2,1)}, u32[]{:S(2)}) copy-start(bf16[2,16,24,384]{3,2,1,0:T(8,128)(2,1)} %param.25) | copy-start | bytes 1769476
  175.7 8.1 %copy-start.14 = (bf16[2,128,4]{1,2,0:T(4,128)(2,1)S(1)}, bf16[2,128,4]{1,2,0:T(4,128)(2,1)}, u32[]{:S(2)}) copy-start(bf16[2,128,4]{1,2,0:T(4,128)(2,1)} %param.28) | copy-start | bytes 6148
  183.8 21.0 %copy-start.3 = (bf16[16,128,384]{2,1,0:T(8,128)(2,1)S(1)}, bf16[16,128,384]{2,1,0:T(8,128)(2,1)}, u32[]{:S(2)}) copy-start(bf16[16,128,384]{2,1,0:T(8,128)(2,1)} %get-tuple-element.5) | copy-start | bytes 4718596
  201.3 13.5 %all-to-all-start.2 = ((bf16[16,64,128]{2,0,1:T(8,128)(2,1)}), bf16[16,64,128]{2,0,1:T(8,128)(2,1)S(1)}, u32[]{:S(2)}, u32[]{:S(2)}) async-start(bf16[16,64,128]{2,0,1:T(8,128)(2,1)} %copy.75), calls=%async_computation.2 | async-start | bytes 524288 | tf_op jit(solution)/shard_map/all_to_all | solution.py:228
  206.8 8.7 %copy-start.16 = (bf16[2,128,4]{1,2,0:T(4,128)(2,1)S(1)}, bf16[2,128,4]{1,2,0:T(4,128)(2,1)}, u32[]{:S(2)}) copy-start(bf16[2,128,4]{1,2,0:T(4,128)(2,1)} %param.31) | copy-start | bytes 6148
  214.8 7.2 %copy-start = (bf16[16,4,16,128]{3,0,1,2:T(8,128)(2,1)}, bf16[16,4,16,128]{3,0,1,2:T(8,128)(2,1)S(1)}, u32[]{:S(2)}) copy-start(bf16[16,4,16,128]{3,0,1,2:T(8,128)(2,1)S(1)} %copy.76) | copy-start | bytes 786436
  239.3 21.0 %copy-start.2 = (bf16[16,64,128]{2,1,0:T(8,128)(2,1)S(1)}, bf16[16,64,128]{2,1,0:T(8,128)(2,1)}, u32[]{:S(2)}) copy-start(bf16[16,64,128]{2,1,0:T(8,128)(2,1)} %tri_att.5.z_ref) | copy-start | bytes 786436
  240.8 20.0 %copy-start.15 = (bf16[2,128,16]{1,2,0:T(8,128)(2,1)S(1)}, bf16[2,128,16]{1,2,0:T(8,128)(2,1)}, u32[]{:S(2)}) copy-start(bf16[2,128,16]{1,2,0:T(8,128)(2,1)} %param.21) | copy-start | bytes 24580
  256.9 12.5 %all-to-all-start.3 = ((bf16[64,16,128]{2,1,0:T(8,128)(2,1)}), bf16[64,16,128]{2,1,0:T(8,128)(2,1)S(1)}, u32[]{:S(2)}, u32[]{:S(2)}) async-start(bf16[64,16,128]{2,1,0:T(8,128)(2,1)} %copy.84), calls=%async_computation.3 | async-start | bytes 524288 | tf_op jit(solution)/shard_map/all_to_all | solution.py:238
  269.4 33.5 %all-to-all-start.1 = ((bf16[128,16,384]{2,1,0:T(8,128)(2,1)}), bf16[128,16,384]{2,1,0:T(8,128)(2,1)S(1)}, u32[]{:S(2)}, u32[]{:S(2)}) async-start(bf16[128,16,384]{2,1,0:T(8,128)(2,1)} %copy.67), calls=%async_computation.1 | async-start | bytes 3145728 | tf_op jit(solution)/shard_map/all_to_all | solution.py:234

commit v2 on v1

--- a/solution.py
+++ b/solution.py
@@ -11,6 +11,7 @@
 NEG = -1e9 * LOG2E
 F32 = jnp.float32
 BF16 = jnp.bfloat16
+LAG = 3
 NT = (((1,), (1,)), ((), ()))
 
 
@@ -29,9 +30,10 @@
     return upper, lower
 
 
-def attend(x, w_ref, wo_ref, pt_ref, gt_ref, heads, dim, keep, bias_ref):
+def attend(x, w_ref, wo_ref, pt_ref, gt_ref, kt_ref, lg_ref, pr_ref, heads, dim, keep, bias_ref):
     width = heads * dim
     rows = 2 * dim
+    pairs = heads // 2
     x_ln = layer_norm(x)
     for part in range(4):
         sl = pl.ds(part * width, width)
@@ -42,35 +44,64 @@
         left = lax.broadcasted_iota(jnp.int32, (64, 128), 1) < 64
         left_b = left.astype(F32).astype(BF16)
         right_b = (1.0 - left.astype(F32)).astype(BF16)
-    for blk in range(2):
-        ln = pl.ds(blk * 128, 128)
-        for hp in range(heads // 2):
-            r = rows * hp
-            q = pt_ref[pl.ds(r, rows), ln]
-            k = pt_ref[pl.ds(width + r, rows), ln]
-            v = pt_ref[pl.ds(2 * width + r, rows), ln]
-            g = pt_ref[pl.ds(3 * width + r, rows), ln]
-            rhs = jnp.concatenate([q * up, q * low], axis=1)
-            logits2 = jnp.dot(k.T, rhs, preferred_element_type=F32)
-            probs = []
-            for half in range(2):
-                lg = logits2[:, 128 * half:128 * half + 128]
-                if bias_ref is not None:
-                    lg = jnp.where(left, lg[0:64], lg[64:128]) * scale + bias_ref[2 * hp + half]
-                else:
-                    lg = lg * scale
-                lg = jnp.where(keep[blk], lg, NEG)
-                e = jnp.exp2(lg - jnp.max(lg, axis=0, keepdims=True))
-                p = (e * (1.0 / jnp.sum(e, axis=0, keepdims=True))).astype(BF16)
-                if bias_ref is not None:
-                    probs += [p * left_b, p * right_b]
-                else:
-                    probs += [p]
-            att = jnp.dot(jnp.concatenate([v * up, v * low], axis=1), jnp.concatenate(probs, axis=0),
-                          preferred_element_type=F32)
-            gt_ref[pl.ds(r, rows), ln] = (att * jax.nn.sigmoid(g.astype(F32))).astype(BF16)
+
+    def place(unit):
+        return pl.ds(unit // pairs * 128, 128), rows * (unit % pairs)
+
+    def turn_keys(unit):
+        ln, r = place(unit)
+        kt_ref[unit % 8] = pt_ref[pl.ds(width + r, rows), ln].T
+
+    def make_logits(unit):
+        ln, r = place(unit)
+        q = pt_ref[pl.ds(r, rows), ln]
+        rhs = jnp.concatenate([q * up, q * low], axis=1)
+        logits2 = jnp.dot(kt_ref[unit % 8], rhs, preferred_element_type=F32)
+        for half in range(2):
+            lg = logits2[:, 128 * half:128 * half + 128]
+            if bias_ref is not None:
+                lg = jnp.where(left, lg[0:64], lg[64:128])
+            lg_ref[unit % 8, half] = lg
+
+    def soften(unit):
+        blk, hp = unit // pairs, unit % pairs
+        for half in range(2):
+            lg = lg_ref[unit % 8, half] * scale
+            if bias_ref is not None:
+                lg = lg + bias_ref[2 * hp + half]
+            lg = jnp.where(keep[blk], lg, NEG)
+            e = jnp.exp2(lg - jnp.max(lg, axis=0, keepdims=True))
+            p = (e * (1.0 / jnp.sum(e, axis=0, keepdims=True))).astype(BF16)
+            if bias_ref is not None:
+                pr_ref[unit % 8, pl.ds(128 * half, 64)] = p * left_b
+                pr_ref[unit % 8, pl.ds(128 * half + 64, 64)] = p * right_b
+            else:
+                pr_ref[unit % 8, pl.ds(128 * half, 128)] = p
+
+    def mix(unit):
+        ln, r = place(unit)
+        v = pt_ref[pl.ds(2 * width + r, rows), ln]
+        g = pt_ref[pl.ds(3 * width + r, rows), ln]
+        att = jnp.dot(jnp.concatenate([v * up, v * low], axis=1), pr_ref[unit % 8], preferred_element_type=F32)
+        gt_ref[pl.ds(r, rows), ln] = (att * jax.nn.sigmoid(g.astype(F32))).astype(BF16)
+
+    stages = ((turn_keys, 0), (make_logits, LAG), (soften, 2 * LAG), (mix, 3 * LAG))
+    for tick in range(2 * pairs + 3 * LAG):
+        for stage, lag in stages:
+            if 0 <= tick - lag < 2 * pairs:
+                stage(tick - lag)
     update = jnp.dot(gt_ref[...].T, wo_ref[...], preferred_element_type=F32)
     return (x + update).astype(BF16)
+
+
+def attend_scratch(heads, dim, keys):
+    return [
+        pltpu.VMEM((4 * heads * dim, 256), BF16),
+        pltpu.VMEM((heads * dim, 256), BF16),
+        pltpu.VMEM((8, 128, 2 * dim), BF16),
+        pltpu.VMEM((8, 2, keys, 128), F32),
+        pltpu.VMEM((8, 256, 128), BF16),
+    ]
 
 
 def pick_column(table, col):
@@ -78,7 +109,7 @@
     return jnp.sum(jnp.where(lane == col, table, 0.0), axis=1, keepdims=True)
 
 
-def row_kernel(heads, dim, per_row, x_ref, keys_ref, bias_ref, w_ref, wo_ref, out_ref, pt_ref, gt_ref):
+def row_kernel(heads, dim, per_row, x_ref, keys_ref, bias_ref, w_ref, wo_ref, out_ref, *scratch):
     step = pl.program_id(0)
     x = x_ref[...].astype(F32).reshape(256, x_ref.shape[-1])
     left = lax.broadcasted_iota(jnp.int32, (64, 128), 1) < 64
@@ -91,13 +122,12 @@
             keep.append(jnp.where(left, first, second) > 0.5)
         else:
             keep.append(jnp.broadcast_to(keys_ref[...], (64, 128)) > 0.5)
-    out = attend(x, w_ref, wo_ref, pt_ref, gt_ref, heads, dim, keep, bias_ref)
+    out = attend(x, w_ref, wo_ref, *scratch, heads, dim, keep, bias_ref)
     out_ref[...] = out.reshape(out_ref.shape)
 
 
 def row_attention(x, keys, bias_t, w, wo, heads, dim, per_row):
     groups, length, width = x.shape
-    inner = heads * dim
     bias_t = bias_t.astype(F32) * LOG2E
     bias_t = jnp.concatenate([bias_t, bias_t], axis=2)
     return pl.pallas_call(
@@ -112,20 +142,20 @@
         ],
         out_specs=pl.BlockSpec((4, length, width), lambda i: (i, 0, 0)),
         out_shape=jax.ShapeDtypeStruct(x.shape, BF16),
-        scratch_shapes=[pltpu.VMEM((4 * inner, 256), BF16), pltpu.VMEM((inner, 256), BF16)],
-        cost_estimate=pl.CostEstimate(flops=groups * length * width * inner * 10, bytes_accessed=x.size * 4, transcendentals=0),
+        scratch_shapes=attend_scratch(heads, dim, 64),
+        cost_estimate=pl.CostEstimate(flops=groups * length * width * heads * dim * 10, bytes_accessed=x.size * 4, transcendentals=0),
         name="row_att" if per_row else "tri_att",
     )(x, keys, bias_t, w, wo)
 
 
 def col_kernel(x_ref, keys_ref, lanes_ref, w1_ref, wo1_ref, wp1_ref, w2_ref, wo2_ref, wp2_ref,
-               out_ref, ac1_ref, ac2_ref, pt_ref, gt_ref):
+               out_ref, ac1_ref, ac2_ref, *scratch):
     step = pl.program_id(0)
     x = x_ref[...].astype(F32).reshape(256, 384)
     keep = [jnp.broadcast_to(pick_column(keys_ref[...], step * 2 + blk), (128, 128)) > 0.5 for blk in range(2)]
     lane_mask = jnp.concatenate([lanes_ref[0], lanes_ref[1]], axis=1)
     for w_ref, wo_ref, wp_ref, ac_ref in ((w1_ref, wo1_ref, wp1_ref, ac1_ref), (w2_ref, wo2_ref, wp2_ref, ac2_ref)):
-        out = attend(x, w_ref, wo_ref, pt_ref, gt_ref, 16, 24, keep, None)
+        out = attend(x, w_ref, wo_ref, *scratch, 16, 24, keep, None)
         x = out.astype(F32)
         ac = lax.dot_general(wp_ref[...], layer_norm(x), NT, preferred_element_type=F32)
         ac_ref[0] = (ac * lane_mask).astype(BF16)
@@ -152,7 +182,7 @@
             jax.ShapeDtypeStruct((8, 64, 256), BF16),
             jax.ShapeDtypeStruct((8, 64, 256), BF16),
         ],
-        scratch_shapes=[pltpu.VMEM((1536, 256), BF16), pltpu.VMEM((384, 256), BF16)],
+        scratch_shapes=attend_scratch(16, 24, 128),
         cost_estimate=pl.CostEstimate(flops=2048 * 384 * 384 * 20, bytes_accessed=x.size * 4, transcendentals=0),
         name="col_att",
     )(x, keys, lanes, *weights)

time: 345 us -> 252 us (0.73)
  Pallas kernels: 204 us -> 111 us
    pallas_call x6, Pallas kernels: 110 us -> 60.8 us  [row_attention(): pl.pallas_call(functools.partial(row_kernel, heads, dim, per_row), grid=(...]
    pallas_call x1, Pallas kernels: 82.1 us -> 39.3 us  [column_pair(): pl.pallas_call(col_kernel, grid=(8,), in_specs=[pl.BlockSpec((2, 128, 384...]
  transfers between devices with their start and end apart: 4 -> 4, of which waited for: 1 -> 1; matrix products, arithmetic and copies ran while one was open for 5% -> 7% of each run, Pallas kernels for 2% -> 2%
where the time goes in v2:
time: 252 us; the launch traced here: 251 us
  Pallas kernels  111 us (44%)
  blocking collectives  63.8 us (25%)
  local copies, waits for them, and re-layouts  29.7 us (12%)
  other arithmetic  16.7 us (7%)
  starting transfers between devices  14.1 us (6%)
  waiting for transfers between devices  8.03 us (3%)
  matrix products  6.46 us (3%)
    pallas_call x6, Pallas kernels, row_attention(): pl.pallas_call(functools.partial(row_kernel, heads, dim, per_row), grid=(...  60.8 us
    all_gather x6, blocking collectives, bias(): return lax.all_gather(part, 'dap', axis=axis, tiled=True)  49.5 us
    pallas_call x1, Pallas kernels, column_pair(): pl.pallas_call(col_kernel, grid=(8,), in_specs=[pl.BlockSpec((2, 128, 384...  39.3 us
    all_gather x2, blocking collectives, gather_full(): lax.all_gather(half.reshape(8, 32, 2, 128).transpose(0, 2, 1, 3).reshape(...  14.3 us
    pallas_call x2, Pallas kernels, opm(): pl.pallas_call(opm_kernel, out_shape=jax.ShapeDtypeStruct(z.shape, BF16),...  11.1 us
    all_to_all x1, waiting for transfers between devices, local_step(): m = lax.all_to_all(m, 'dap', 1, 0, tiled=True)  8.03 us
    dot_general x6, matrix products, bias(): jnp.einsum(form, layer_norm(z_blk), w, preferred_element_type=F32)  5.72 us
    pallas_call x2, local copies, waits for them, and re-layouts, row_attention(): pl.pallas_call(functools.partial(row_kernel, heads, dim, per_row), grid=(...  5.32 us
  transfers between devices with their start and end apart: 4, of which 1 were waited for; matrix products, arithmetic and copies ran while one was open for 7% of the time, Pallas kernels for 2%

profile of v2, /device:TPU:0, one launch (start us, length us, event | category | flops | bytes accessed | tf_op | source)
XLA Modules:
  0.0 251.0 jit_solution(14825072259521062710)
XLA Ops:
  1.4 1.2 convert_reduce_fusion.5
  2.6 1.3 fusion.27
  3.9 1.6 fusion
  5.5 7.5 %all_gather.24 = bf16[16,64,64]{1,0,2:T(8,128)(2,1)S(1)} all-gather(bf16[16,64,16]{1,0,2:T(8,128)(2,1)S(1)} %fusion), channel_id=1, replica_groups=mesh['data'=4,'dap'=4] {'dap'}, dimensions={2}, use_global_device_ids=true | all-gather | bytes 163840 | tf_op jit(solution)/shard_map/all_gather | solution.py:244
  13.3 1.0 pad_maximum_fusion.bias_ref
  14.3 1.7 fusion.59
  16.0 0.9 fusion.61
  17.6 18.5 %row_att.2 = bf16[32,64,384]{2,1,0:T(8,128)(2,1)} custom-call(bf16[32,64,384]{2,1,0:T(8,128)(2,1)} %x_ref.1, f32[64,32]{1,0:T(8,128)} %dynamic-slice_bitcast_fusion.keys_ref, f32[16,64,128]{2,1,0:T(8,128)} %pad_maximum_fusion.bias_ref, bf16[1536,384]{1,0:T(8,128)(2,1)} %bitcast.146, bf16[384,384]{1,0:T(8,128)(2,1)} %bitcast.162), custom_call_target="tpu_custom_call" | custom-call | flops 3019898880 | bytes 3145728 | tf_op jit(solution)/shard_map/row_att/pallas_call | solution.py:133
  36.1 3.5 %copy.63 = bf16[32,64,384]{2,0,1:T(8,128)(2,1)} copy(bf16[32,64,384]{2,1,0:T(8,128)(2,1)} %row_att.2) | data formatting | bytes 3145728 | tf_op jit(solution)/shard_map/row_att/pallas_call | solution.py:133
  39.6 3.7 %all-to-all-start = ((bf16[32,64,384]{2,0,1:T(8,128)(2,1)}), bf16[32,64,384]{2,0,1:T(8,128)(2,1)S(1)}, u32[]{:S(2)}, u32[]{:S(2)}) async-start(bf16[32,64,384]{2,0,1:T(8,128)(2,1)} %copy.63), calls=%async_computation | async-start | bytes 3145728 | tf_op jit(solution)/shard_map/all_to_all | solution.py:252
  44.9 0.9 copy.72.w_ref
  47.7 0.9 copy.81.w_ref
  50.8 0.9 fusion.62
  51.8 3.3 %fusion.60 = (bf16[1,4,16,24,384]{4,3,2,1,0:T(8,128)(2,1)}, bf16[1,4,16,24,384]{4,3,2,1,0:T(8,128)(2,1)}) fusion(bf16[2,4,16,24,384]{4,3,2,1,0:T(8,128)(2,1)} %bitcast.139), kind=kLoop, calls=%fused_computation.105 | loop fusion | bytes 4718592 | tf_op jit(solution)/shard_map/slice | solution.py:254
  55.1 8.0 %all-to-all-done = bf16[32,64,384]{2,0,1:T(8,128)(2,1)S(1)} async-done(((bf16[32,64,384]{2,0,1:T(8,128)(2,1)}), bf16[32,64,384]{2,0,1:T(8,128)(2,1)S(1)}, u32[]{:S(2)}, u32[]{:S(2)}) %all-to-all-start) | async-done | bytes 1572896 | tf_op jit(solution)/shard_map/all_to_all | solution.py:252
  63.1 1.4 copy.64
  64.5 39.3 %col_att.1 = (bf16[16,128,384]{2,1,0:T(8,128)(2,1)}, bf16[8,64,256]{2,1,0:T(8,128)(2,1)}, bf16[8,64,256]{2,1,0:T(8,128)(2,1)}) custom-call(bf16[16,128,384]{2,1,0:T(8,128)(2,1)} %bitcast.141, f32[128,16]{1,0:T(8,128)} %copy.65.keys_ref, f32[16,1,128]{2,1,0:T(1,128)} %bitcast.173, bf16[1536,384]{1,0:T(8,128)(2,1)} %bitcast.145, bf16[384,384]{1,0:T(8,128)(2,1)} %bitcast.161, ...), custom_call_target="tpu_custom_call" | custom-call | flops 6039797760 | bytes 3145728 | tf_op jit(solution)/shard_map/col_att/pallas_call | solution.py:167
  103.8 1.8 slice_bitcast_fusion
  105.7 6.5 %all_gather.25.full_ref = bf16[2048,128]{1,0:T(8,128)(2,1)} all-gather(bf16[512,128]{1,0:T(8,128)(2,1)S(1)} %bitcast.154), channel_id=1, replica_groups=mesh['data'=4,'dap'=4] {'dap'}, dimensions={0}, use_global_device_ids=true | all-gather | bytes 655360 | tf_op jit(solution)/shard_map/all_gather | solution.py:247
  112.2 5.5 %opm.2.x_ref = bf16[16,64,128]{2,1,0:T(8,128)(2,1)} custom-call(bf16[256,256]{1,0:T(8,128)(2,1)} %bitcast.167, bf16[2048,128]{1,0:T(8,128)(2,1)} %all_gather.25.full_ref, bf16[16,64,128]{2,1,0:T(8,128)(2,1)} %z_ref.1, f32[64,16]{1,0:T(8,128)} %convolution_bitcast_fusion.norm_ref, bf16[128,1024]{1,0:T(8,128)(2,1)} %copy.72.w_ref), custom_call_target="tpu_custom_call" | custom-call | flops 1000000000 | bytes 1048576 | tf_op jit(solution)/shard_map/opm/pallas_call | solution.py:215
  117.7 1.2 convert_reduce_fusion.4
  118.9 1.3 fusion.25
  120.3 1.5 fusion.1
  121.8 5.4 %all_gather.26 = bf16[4,64,64]{1,0,2:T(4,128)(2,1)S(1)} all-gather(bf16[4,64,16]{1,0,2:T(4,128)(2,1)S(1)} %fusion.1), channel_id=1, replica_groups=mesh['data'=4,'dap'=4] {'dap'}, dimensions={2}, use_global_device_ids=true | all-gather | bytes 40960 | tf_op jit(solution)/shard_map/all_gather | solution.py:244
  128.1 6.0 %tri_att.4 = bf16[16,64,128]{2,1,0:T(8,128)(2,1)} custom-call(bf16[16,64,128]{2,1,0:T(8,128)(2,1)} %opm.2.x_ref, f32[64,1]{1,0:T(8,128)} %copy.74.keys_ref, f32[4,64,128]{2,1,0:T(8,128)} %pad_maximum_fusion.2.bias_ref, bf16[512,128]{1,0:T(8,128)(2,1)} %bitcast.158, bf16[128,128]{1,0:T(8,128)(2,1)} %bitcast.171), custom_call_target="tpu_custom_call" | custom-call | flops 167772160 | bytes 524288 | tf_op jit(solution)/shard_map/tri_att/pallas_call | solution.py:133
  134.1 1.8 copy.75
  135.9 3.4 %all-to-all-start.2 = ((bf16[16,64,128]{2,0,1:T(8,128)(2,1)}), bf16[16,64,128]{2,0,1:T(8,128)(2,1)S(1)}, u32[]{:S(2)}, u32[]{:S(2)}) async-start(bf16[16,64,128]{2,0,1:T(8,128)(2,1)} %copy.75), calls=%async_computation.2 | async-start | bytes 524288 | tf_op jit(solution)/shard_map/all_to_all | solution.py:258
  139.4 2.1 copy.67
  141.4 7.8 %all_gather.29.full_ref = bf16[2048,128]{1,0:T(8,128)(2,1)} all-gather(bf16[512,128]{1,0:T(8,128)(2,1)S(1)} %bitcast.153), channel_id=1, replica_groups=mesh['data'=4,'dap'=4] {'dap'}, dimensions={0}, use_global_device_ids=true | all-gather | bytes 655360 | tf_op jit(solution)/shard_map/all_gather | solution.py:247
  150.4 5.2 %all_gather.27 = bf16[4,64,64]{1,0,2:T(4,128)(2,1)S(1)} all-gather(bf16[4,64,16]{1,0,2:T(4,128)(2,1)S(1)} %fusion.2), channel_id=1, replica_groups=mesh['data'=4,'dap'=4] {'dap'}, dimensions={2}, use_global_device_ids=true | all-gather | bytes 40960 | tf_op jit(solution)/shard_map/all_gather | solution.py:244
  156.5 6.0 %tri_att.5.z_ref = bf16[16,64,128]{2,1,0:T(8,128)(2,1)} custom-call(bf16[16,64,128]{2,1,0:T(8,128)(2,1)} %bitcast.137, f32[64,1]{1,0:T(8,128)} %copy.74.keys_ref, f32[4,64,128]{2,1,0:T(8,128)} %pad_maximum_fusion.3.bias_ref, bf16[512,128]{1,0:T(8,128)(2,1)} %bitcast.157, bf16[128,128]{1,0:T(8,128)(2,1)} %bitcast.170), custom_call_target="tpu_custom_call" | custom-call | flops 167772160 | bytes 524288 | tf_op jit(solution)/shard_map/tri_att/pallas_call | solution.py:133
  162.5 1.2 convert_reduce_fusion.2
  163.6 5.5 %opm.3.x_ref = bf16[16,64,128]{2,1,0:T(8,128)(2,1)} custom-call(bf16[256,256]{1,0:T(8,128)(2,1)} %bitcast.166, bf16[2048,128]{1,0:T(8,128)(2,1)} %all_gather.29.full_ref, bf16[16,64,128]{2,1,0:T(8,128)(2,1)} %tri_att.5.z_ref, f32[64,16]{1,0:T(8,128)} %convolution_bitcast_fusion.norm_ref, bf16[128,1024]{1,0:T(8,128)(2,1)} %copy.81.w_ref), custom_call_target="tpu_custom_call" | custom-call | flops 1000000000 | bytes 1048576 | tf_op jit(solution)/shard_map/opm/pallas_call | solution.py:215
  169.2 1.2 convert_reduce_fusion.1
  170.3 1.3 fusion.19
  171.7 1.4 fusion.3
  173.1 5.4 %all_gather.30 = bf16[4,64,64]{1,0,2:T(4,128)(2,1)S(1)} all-gather(bf16[4,64,16]{1,0,2:T(4,128)(2,1)S(1)} %fusion.3), channel_id=1, replica_groups=mesh['data'=4,'dap'=4] {'dap'}, dimensions={2}, use_global_device_ids=true | all-gather | bytes 40960 | tf_op jit(solution)/shard_map/all_gather | solution.py:244
  179.4 6.0 %tri_att.6 = bf16[16,64,128]{2,1,0:T(8,128)(2,1)} custom-call(bf16[16,64,128]{2,1,0:T(8,128)(2,1)} %opm.3.x_ref, f32[64,1]{1,0:T(8,128)} %copy.74.keys_ref, f32[4,64,128]{2,1,0:T(8,128)} %pad_maximum_fusion.4.bias_ref, bf16[512,128]{1,0:T(8,128)(2,1)} %bitcast.156, bf16[128,128]{1,0:T(8,128)(2,1)} %bitcast.169), custom_call_target="tpu_custom_call" | custom-call | flops 167772160 | bytes 524288 | tf_op jit(solution)/shard_map/tri_att/pallas_call | solution.py:133
  185.4 1.8 copy.84
  187.2 3.4 %all-to-all-start.3 = ((bf16[64,16,128]{2,1,0:T(8,128)(2,1)}), bf16[64,16,128]{2,1,0:T(8,128)(2,1)S(1)}, u32[]{:S(2)}, u32[]{:S(2)}) async-start(bf16[64,16,128]{2,1,0:T(8,128)(2,1)} %copy.84), calls=%async_computation.3 | async-start | bytes 524288 | tf_op jit(solution)/shard_map/all_to_all | solution.py:268
  191.5 7.1 %all_gather.28 = bf16[16,64,64]{2,1,0:T(8,128)(2,1)S(1)} all-gather(bf16[16,16,64]{2,1,0:T(8,128)(2,1)S(1)} %bitcast.163), channel_id=1, replica_groups=mesh['data'=4,'dap'=4] {'dap'}, dimensions={1}, use_global_device_ids=true | all-gather | bytes 163840 | tf_op jit(solution)/shard_map/all_gather | solution.py:244
  198.7 1.0 pad_maximum_fusion.1.bias_ref
  199.7 3.6 %all-to-all-start.1 = ((bf16[128,16,384]{2,1,0:T(8,128)(2,1)}), bf16[128,16,384]{2,1,0:T(8,128)(2,1)S(1)}, u32[]{:S(2)}, u32[]{:S(2)}) async-start(bf16[128,16,384]{2,1,0:T(8,128)(2,1)} %copy.67), calls=%async_computation.1 | async-start | bytes 3145728 | tf_op jit(solution)/shard_map/all_to_all | solution.py:264
  205.3 18.9 %all_gather.31 = bf16[4,64,64]{1,0,2:T(4,128)(2,1)S(1)} all-gather(bf16[4,64,16]{1,0,2:T(4,128)(2,1)S(1)} %fusion.4), channel_id=1, replica_groups=mesh['data'=4,'dap'=4] {'dap'}, dimensions={2}, use_global_device_ids=true | all-gather | bytes 40960 | tf_op jit(solution)/shard_map/all_gather | solution.py:244
  224.4 0.8 pad_maximum_fusion.5.bias_ref
  225.1 6.0 %tri_att.7 = bf16[16,64,128]{2,1,0:T(8,128)(2,1)} custom-call(bf16[16,64,128]{2,1,0:T(8,128)(2,1)} %bitcast.147, f32[64,1]{1,0:T(8,128)} %copy.74.keys_ref, f32[4,64,128]{2,1,0:T(8,128)} %pad_maximum_fusion.5.bias_ref, bf16[512,128]{1,0:T(8,128)(2,1)} %bitcast.155, bf16[128,128]{1,0:T(8,128)(2,1)} %bitcast.168), custom_call_target="tpu_custom_call" | custom-call | flops 167772160 | bytes 524288 | tf_op jit(solution)/shard_map/tri_att/pallas_call | solution.py:133
  231.1 1.5 copy.68
  232.6 18.5 %row_att.3 = bf16[32,64,384]{2,1,0:T(8,128)(2,1)} custom-call(bf16[32,64,384]{2,1,0:T(8,128)(2,1)} %bitcast.142, f32[64,32]{1,0:T(8,128)} %dynamic-slice_bitcast_fusion.keys_ref, f32[16,64,128]{2,1,0:T(8,128)} %pad_maximum_fusion.1.bias_ref, bf16[1536,384]{1,0:T(8,128)(2,1)} %bitcast.143, bf16[384,384]{1,0:T(8,128)(2,1)} %bitcast.159), custom_call_target="tpu_custom_call" | custom-call | flops 3019898880 | bytes 3145728 | tf_op jit(solution)/shard_map/row_att/pallas_call | solution.py:133
  (93 shorter events, 14.5 us)
Async XLA Ops:
  3.9 10.4 %copy-start.1 = (bf16[2,384,4,16,24]{1,4,3,2,0:T(8,128)(2,1)S(1)}, bf16[2,384,4,16,24]{1,4,3,2,0:T(8,128)(2,1)}, u32[]{:S(2)}) copy-start(bf16[2,384,4,16,24]{1,4,3,2,0:T(8,128)(2,1)} %param.22) | copy-start | bytes 7077892
  14.3 1.7 copy-start.4
  39.6 4.5 %copy-start.10 = (bf16[2,384,2,32]{1,3,2,0:T(8,128)(2,1)S(1)}, bf16[2,384,2,32]{1,3,2,0:T(8,128)(2,1)}, u32[]{:S(2)}) copy-start(bf16[2,384,2,32]{1,3,2,0:T(8,128)(2,1)} %param.26) | copy-start | bytes 294916
  39.6 5.1 %copy-start.6 = (bf16[2,32,32,128]{3,2,1,0:T(8,128)(2,1)S(1)}, bf16[2,32,32,128]{3,2,1,0:T(8,128)(2,1)}, u32[]{:S(2)}) copy-start(bf16[2,32,32,128]{3,2,1,0:T(8,128)(2,1)} %param.27) | copy-start | bytes 1572868
  39.6 23.5 %all-to-all-start = ((bf16[32,64,384]{2,0,1:T(8,128)(2,1)}), bf16[32,64,384]{2,0,1:T(8,128)(2,1)S(1)}, u32[]{:S(2)}, u32[]{:S(2)}) async-start(bf16[32,64,384]{2,0,1:T(8,128)(2,1)} %copy.63), calls=%async_computation | async-start | bytes 3145728 | tf_op jit(solution)/shard_map/all_to_all | solution.py:252
  43.3 2.5 copy-start.17
  43.3 3.2 %copy-start.12 = (bf16[2,4,32,128]{3,2,1,0:T(8,128)(2,1)S(1)}, bf16[2,4,32,128]{3,2,1,0:T(8,128)(2,1)}, u32[]{:S(2)}) copy-start(bf16[2,4,32,128]{3,2,1,0:T(8,128)(2,1)} %param.30) | copy-start | bytes 196612
  43.3 3.8 %copy-start.13 = (bf16[2,4,32,128]{3,2,1,0:T(8,128)(2,1)S(1)}, bf16[2,4,32,128]{3,2,1,0:T(8,128)(2,1)}, u32[]{:S(2)}) copy-start(bf16[2,4,32,128]{3,2,1,0:T(8,128)(2,1)} %param.33) | copy-start | bytes 196612
  43.3 5.3 %copy-start.11 = (f32[128,16]{0,1:T(8,128)}, f32[128,16]{0,1:T(8,128)S(1)}, u32[]{:S(2)}) copy-start(f32[128,16]{0,1:T(8,128)S(1)} %constant_dynamic-slice_fusion) | copy-start | bytes 24580
  44.1 4.5 %copy-start.9 = (s32[128,64]{0,1:T(8,128)S(1)}, s32[128,64]{0,1:T(8,128)}, u32[]{:S(2)}) copy-start(s32[128,64]{0,1:T(8,128)} %param.19) | copy-start | bytes 98308
  44.1 5.3 %copy-start.7 = (bf16[2,128,4,4,32]{1,4,3,2,0:T(8,128)(2,1)S(1)}, bf16[2,128,4,4,32]{1,4,3,2,0:T(8,128)(2,1)}, u32[]{:S(2)}) copy-start(bf16[2,128,4,4,32]{1,4,3,2,0:T(8,128)(2,1)} %param.29) | copy-start | bytes 786436
  44.7 5.4 %copy-start.8 = (bf16[2,128,4,4,32]{1,4,3,2,0:T(8,128)(2,1)S(1)}, bf16[2,128,4,4,32]{1,4,3,2,0:T(8,128)(2,1)}, u32[]{:S(2)}) copy-start(bf16[2,128,4,4,32]{1,4,3,2,0:T(8,128)(2,1)} %param.32) | copy-start | bytes 786436
  44.8 6.1 %copy-start.5 = (bf16[2,16,24,384]{3,2,1,0:T(8,128)(2,1)S(1)}, bf16[2,16,24,384]{3,2,1,0:T(8,128)(2,1)}, u32[]{:S(2)}) copy-start(bf16[2,16,24,384]{3,2,1,0:T(8,128)(2,1)} %param.25) | copy-start | bytes 1769476
  112.2 8.1 %copy-start.14 = (bf16[2,128,4]{1,2,0:T(4,128)(2,1)S(1)}, bf16[2,128,4]{1,2,0:T(4,128)(2,1)}, u32[]{:S(2)}) copy-start(bf16[2,128,4]{1,2,0:T(4,128)(2,1)} %param.28) | copy-start | bytes 6148
  120.3 19.1 %copy-start.3 = (bf16[16,128,384]{2,1,0:T(8,128)(2,1)S(1)}, bf16[16,128,384]{2,1,0:T(8,128)(2,1)}, u32[]{:S(2)}) copy-start(bf16[16,128,384]{2,1,0:T(8,128)(2,1)} %get-tuple-element.5) | copy-start | bytes 4718596
  135.9 13.3 %all-to-all-start.2 = ((bf16[16,64,128]{2,0,1:T(8,128)(2,1)}), bf16[16,64,128]{2,0,1:T(8,128)(2,1)S(1)}, u32[]{:S(2)}, u32[]{:S(2)}) async-start(bf16[16,64,128]{2,0,1:T(8,128)(2,1)} %copy.75), calls=%async_computation.2 | async-start | bytes 524288 | tf_op jit(solution)/shard_map/all_to_all | solution.py:258
  141.4 8.5 %copy-start.16 = (bf16[2,128,4]{1,2,0:T(4,128)(2,1)S(1)}, bf16[2,128,4]{1,2,0:T(4,128)(2,1)}, u32[]{:S(2)}) copy-start(bf16[2,128,4]{1,2,0:T(4,128)(2,1)} %param.31) | copy-start | bytes 6148
  149.2 7.2 %copy-start = (bf16[16,4,16,128]{3,0,1,2:T(8,128)(2,1)}, bf16[16,4,16,128]{3,0,1,2:T(8,128)(2,1)S(1)}, u32[]{:S(2)}) copy-start(bf16[16,4,16,128]{3,0,1,2:T(8,128)(2,1)S(1)} %copy.76) | copy-start | bytes 786436
  171.7 18.9 %copy-start.2 = (bf16[16,64,128]{2,1,0:T(8,128)(2,1)S(1)}, bf16[16,64,128]{2,1,0:T(8,128)(2,1)}, u32[]{:S(2)}) copy-start(bf16[16,64,128]{2,1,0:T(8,128)(2,1)} %tri_att.5.z_ref) | copy-start | bytes 786436
  173.1 17.9 %copy-start.15 = (bf16[2,128,16]{1,2,0:T(8,128)(2,1)S(1)}, bf16[2,128,16]{1,2,0:T(8,128)(2,1)}, u32[]{:S(2)}) copy-start(bf16[2,128,16]{1,2,0:T(8,128)(2,1)} %param.21) | copy-start | bytes 24580
  187.2 12.5 %all-to-all-start.3 = ((bf16[64,16,128]{2,1,0:T(8,128)(2,1)}), bf16[64,16,128]{2,1,0:T(8,128)(2,1)S(1)}, u32[]{:S(2)}, u32[]{:S(2)}) async-start(bf16[64,16,128]{2,1,0:T(8,128)(2,1)} %copy.84), calls=%async_computation.3 | async-start | bytes 524288 | tf_op jit(solution)/shard_map/all_to_all | solution.py:268
  199.7 31.4 %all-to-all-start.1 = ((bf16[128,16,384]{2,1,0:T(8,128)(2,1)}), bf16[128,16,384]{2,1,0:T(8,128)(2,1)S(1)}, u32[]{:S(2)}, u32[]{:S(2)}) async-start(bf16[128,16,384]{2,1,0:T(8,128)(2,1)} %copy.67), calls=%async_computation.1 | async-start | bytes 3145728 | tf_op jit(solution)/shard_map/all_to_all | solution.py:264

commit v3 on v2

--- a/solution.py
+++ b/solution.py
@@ -11,7 +11,8 @@
 NEG = -1e9 * LOG2E
 F32 = jnp.float32
 BF16 = jnp.bfloat16
-LAG = 3
+LAG = 2
+SLOTS = 4
 NT = (((1,), (1,)), ((), ()))
 
 
@@ -30,14 +31,11 @@
     return upper, lower
 
 
-def attend(x, w_ref, wo_ref, pt_ref, gt_ref, kt_ref, lg_ref, pr_ref, heads, dim, keep, bias_ref):
+def attend_units(pt_ref, gt_ref, kt_ref, lg_ref, pr_ref, heads, dim, keep, bias_ref, work):
     width = heads * dim
     rows = 2 * dim
     pairs = heads // 2
-    x_ln = layer_norm(x)
-    for part in range(4):
-        sl = pl.ds(part * width, width)
-        pt_ref[sl, :] = lax.dot_general(w_ref[sl, :], x_ln, NT, preferred_element_type=F32).astype(BF16)
+    units = 2 * pairs
     up, low = half_masks(rows, dim)
     scale = dim ** -0.5 * LOG2E
     if bias_ref is not None:
@@ -50,57 +48,84 @@
 
     def turn_keys(unit):
         ln, r = place(unit)
-        kt_ref[unit % 8] = pt_ref[pl.ds(width + r, rows), ln].T
+        kt_ref[unit % SLOTS] = pt_ref[pl.ds(width + r, rows), ln].T
 
     def make_logits(unit):
         ln, r = place(unit)
         q = pt_ref[pl.ds(r, rows), ln]
         rhs = jnp.concatenate([q * up, q * low], axis=1)
-        logits2 = jnp.dot(kt_ref[unit % 8], rhs, preferred_element_type=F32)
+        logits2 = jnp.dot(kt_ref[unit % SLOTS], rhs, preferred_element_type=F32)
         for half in range(2):
             lg = logits2[:, 128 * half:128 * half + 128]
             if bias_ref is not None:
                 lg = jnp.where(left, lg[0:64], lg[64:128])
-            lg_ref[unit % 8, half] = lg
+            lg_ref[unit % SLOTS, half] = lg
 
     def soften(unit):
         blk, hp = unit // pairs, unit % pairs
         for half in range(2):
-            lg = lg_ref[unit % 8, half] * scale
+            lg = lg_ref[unit % SLOTS, half] * scale
             if bias_ref is not None:
                 lg = lg + bias_ref[2 * hp + half]
             lg = jnp.where(keep[blk], lg, NEG)
             e = jnp.exp2(lg - jnp.max(lg, axis=0, keepdims=True))
             p = (e * (1.0 / jnp.sum(e, axis=0, keepdims=True))).astype(BF16)
-            if bias_ref is not None:
-                pr_ref[unit % 8, pl.ds(128 * half, 64)] = p * left_b
-                pr_ref[unit % 8, pl.ds(128 * half + 64, 64)] = p * right_b
-            else:
-                pr_ref[unit % 8, pl.ds(128 * half, 128)] = p
+            pr_ref[unit % SLOTS, half] = p
 
     def mix(unit):
         ln, r = place(unit)
         v = pt_ref[pl.ds(2 * width + r, rows), ln]
         g = pt_ref[pl.ds(3 * width + r, rows), ln]
-        att = jnp.dot(jnp.concatenate([v * up, v * low], axis=1), pr_ref[unit % 8], preferred_element_type=F32)
+        probs = []
+        for half in range(2):
+            p = pr_ref[unit % SLOTS, half]
+            probs += [p] if bias_ref is None else [p * left_b, p * right_b]
+        att = jnp.dot(jnp.concatenate([v * up, v * low], axis=1), jnp.concatenate(probs, axis=0), preferred_element_type=F32)
         gt_ref[pl.ds(r, rows), ln] = (att * jax.nn.sigmoid(g.astype(F32))).astype(BF16)
 
     stages = ((turn_keys, 0), (make_logits, LAG), (soften, 2 * LAG), (mix, 3 * LAG))
-    for tick in range(2 * pairs + 3 * LAG):
+    ticks = units + 3 * LAG
+    for tick in range(ticks):
         for stage, lag in stages:
-            if 0 <= tick - lag < 2 * pairs:
+            if 0 <= tick - lag < units:
                 stage(tick - lag)
-    update = jnp.dot(gt_ref[...].T, wo_ref[...], preferred_element_type=F32)
-    return (x + update).astype(BF16)
-
-
-def attend_scratch(heads, dim, keys):
+        for job in work[len(work) * tick // ticks:len(work) * (tick + 1) // ticks]:
+            job()
+
+
+def attend_step(half, scratch, heads, dim, x_new, w, keep, bias_ref, x_old, wo, finish):
+    ln_ref, pt_refs, gt_refs, others = scratch[0], scratch[1:3], scratch[3:5], scratch[5:8]
+    width = heads * dim
+    chunk = 256 if width > 256 else 128
+
+    def norm():
+        ln_ref[...] = layer_norm(x_new())
+
+    def project(part):
+        def job():
+            sl = pl.ds(part * chunk, chunk)
+            pt_refs[half][sl, :] = lax.dot_general(w(sl), ln_ref[...], NT, preferred_element_type=F32).astype(BF16)
+        return job
+
+    def leave():
+        update = jnp.dot(gt_refs[half][...].T, wo(), preferred_element_type=F32)
+        finish((x_old() + update).astype(BF16))
+
+    work = [norm, leave] + [project(part) for part in range(4 * width // chunk)]
+    attend_units(pt_refs[1 - half], gt_refs[1 - half], *others, heads, dim, keep, bias_ref, work)
+
+
+def attend_scratch(heads, dim, keys, channels):
+    inner = heads * dim
     return [
-        pltpu.VMEM((4 * heads * dim, 256), BF16),
-        pltpu.VMEM((heads * dim, 256), BF16),
-        pltpu.VMEM((8, 128, 2 * dim), BF16),
-        pltpu.VMEM((8, 2, keys, 128), F32),
-        pltpu.VMEM((8, 256, 128), BF16),
+        pltpu.VMEM((256, channels), BF16),
+        pltpu.VMEM((4 * inner, 256), BF16),
+        pltpu.VMEM((4 * inner, 256), BF16),
+        pltpu.VMEM((inner, 256), BF16),
+        pltpu.VMEM((inner, 256), BF16),
+        pltpu.VMEM((SLOTS, 128, 2 * dim), BF16),
+        pltpu.VMEM((SLOTS, 2, keys, 128), F32),
+        pltpu.VMEM((SLOTS, 2, keys, 128), BF16),
     ]
 
 
@@ -109,21 +134,34 @@
     return jnp.sum(jnp.where(lane == col, table, 0.0), axis=1, keepdims=True)
 
 
-def row_kernel(heads, dim, per_row, x_ref, keys_ref, bias_ref, w_ref, wo_ref, out_ref, *scratch):
-    step = pl.program_id(0)
-    x = x_ref[...].astype(F32).reshape(256, x_ref.shape[-1])
+def row_kernel(heads, dim, per_row, blocks, x_ref, keys_ref, bias_ref, w_ref, wo_ref, out_ref, *scratch):
+    channels = x_ref.shape[-1]
     left = lax.broadcasted_iota(jnp.int32, (64, 128), 1) < 64
-    keep = []
-    for blk in range(2):
-        if per_row:
-            keys = keys_ref[...]
-            first = pick_column(keys, step * 4 + 2 * blk)
-            second = pick_column(keys, step * 4 + 2 * blk + 1)
-            keep.append(jnp.where(left, first, second) > 0.5)
-        else:
-            keep.append(jnp.broadcast_to(keys_ref[...], (64, 128)) > 0.5)
-    out = attend(x, w_ref, wo_ref, *scratch, heads, dim, keep, bias_ref)
-    out_ref[...] = out.reshape(out_ref.shape)
+
+    def body(turn, carry):
+        for half in range(2):
+            i = 2 * turn + half
+            new = jnp.minimum(i, blocks - 1)
+            mid = jnp.clip(i - 1, 0, blocks - 1)
+            old = jnp.clip(i - 2, 0, blocks - 1)
+            keep = []
+            for blk in range(2):
+                if per_row:
+                    first = pick_column(keys_ref[...], mid * 4 + 2 * blk)
+                    second = pick_column(keys_ref[...], mid * 4 + 2 * blk + 1)
+                    keep.append(jnp.where(left, first, second) > 0.5)
+                else:
+                    keep.append(jnp.broadcast_to(keys_ref[...], (64, 128)) > 0.5)
+            read = lambda at: x_ref[pl.ds(at * 4, 4)].astype(F32).reshape(256, channels)
+
+            def finish(out):
+                out_ref[pl.ds(old * 4, 4)] = out.reshape(4, 64, channels)
+
+            attend_step(half, scratch, heads, dim, lambda: read(new), lambda sl: w_ref[sl, :], keep, bias_ref,
+                        lambda: read(old), lambda: wo_ref[...], finish)
+        return carry
+
+    lax.fori_loop(0, blocks // 2 + 1, body, 0)
 
 
 def row_attention(x, keys, bias_t, w, wo, heads, dim, per_row):
@@ -131,61 +169,51 @@
     bias_t = bias_t.astype(F32) * LOG2E
     bias_t = jnp.concatenate([bias_t, bias_t], axis=2)
     return pl.pallas_call(
-        functools.partial(row_kernel, heads, dim, per_row),
-        grid=(groups // 4,),
-        in_specs=[
-            pl.BlockSpec((4, length, width), lambda i: (i, 0, 0)),
-            pl.BlockSpec(keys.shape, lambda i: (0, 0)),
-            pl.BlockSpec(bias_t.shape, lambda i: (0, 0, 0)),
-            pl.BlockSpec(w.shape, lambda i: (0, 0)),
-            pl.BlockSpec(wo.shape, lambda i: (0, 0)),
-        ],
-        out_specs=pl.BlockSpec((4, length, width), lambda i: (i, 0, 0)),
+        functools.partial(row_kernel, heads, dim, per_row, groups // 4),
         out_shape=jax.ShapeDtypeStruct(x.shape, BF16),
-        scratch_shapes=attend_scratch(heads, dim, 64),
+        scratch_shapes=attend_scratch(heads, dim, 64, width),
         cost_estimate=pl.CostEstimate(flops=groups * length * width * heads * dim * 10, bytes_accessed=x.size * 4, transcendentals=0),
         name="row_att" if per_row else "tri_att",
     )(x, keys, bias_t, w, wo)
 
 
-def col_kernel(x_ref, keys_ref, lanes_ref, w1_ref, wo1_ref, wp1_ref, w2_ref, wo2_ref, wp2_ref,
-               out_ref, ac1_ref, ac2_ref, *scratch):
-    step = pl.program_id(0)
-    x = x_ref[...].astype(F32).reshape(256, 384)
-    keep = [jnp.broadcast_to(pick_column(keys_ref[...], step * 2 + blk), (128, 128)) > 0.5 for blk in range(2)]
-    lane_mask = jnp.concatenate([lanes_ref[0], lanes_ref[1]], axis=1)
-    for w_ref, wo_ref, wp_ref, ac_ref in ((w1_ref, wo1_ref, wp1_ref, ac1_ref), (w2_ref, wo2_ref, wp2_ref, ac2_ref)):
-        out = attend(x, w_ref, wo_ref, *scratch, 16, 24, keep, None)
-        x = out.astype(F32)
-        ac = lax.dot_general(wp_ref[...], layer_norm(x), NT, preferred_element_type=F32)
-        ac_ref[0] = (ac * lane_mask).astype(BF16)
-    out_ref[...] = out.reshape(out_ref.shape)
-
-
-def column_pair(x, keys, lanes, weights):
-    whole = lambda a: pl.BlockSpec(a.shape, lambda i: (0,) * a.ndim)
+def col_kernel(x_ref, keys_ref, lanes_ref, w_ref, wo_ref, wp_ref, out_ref, ac_ref, m_ref, *scratch):
+    m_ref[0] = x_ref[...]
+
+    def body(turn, carry):
+        for half in range(2):
+            i = 2 * turn + half
+            new = jnp.minimum(i, 15)
+            mid = jnp.clip(i - 1, 0, 15)
+            old = jnp.clip(i - 2, 0, 15)
+            keep = [jnp.broadcast_to(pick_column(keys_ref[...], mid % 8 * 2 + blk), (128, 128)) > 0.5 for blk in range(2)]
+            read = lambda at: m_ref[at // 8, pl.ds(at % 8 * 2, 2)].astype(F32).reshape(256, 384)
+
+            def finish(out):
+                m_ref[old // 8 + 1, pl.ds(old % 8 * 2, 2)] = out.reshape(2, 128, 384)
+                ac = lax.dot_general(wp_ref[old // 8], layer_norm(out), NT, preferred_element_type=F32)
+                lane_mask = jnp.concatenate([lanes_ref[old % 8 * 2], lanes_ref[old % 8 * 2 + 1]], axis=1)
+                ac_ref[old // 8, old % 8] = (ac * lane_mask).astype(BF16)
+
+            attend_step(half, scratch, 16, 24, lambda: read(new), lambda sl: w_ref[new // 8, sl, :], keep, None,
+                        lambda: read(old), lambda: wo_ref[old // 8], finish)
+        return carry
+
+    lax.fori_loop(0, 9, body, 0)
+    out_ref[...] = m_ref[2]
+
+
+def column_pair(x, keys, lanes, w, wo, wp):
     return pl.pallas_call(
         col_kernel,
-        grid=(8,),
-        in_specs=[
-            pl.BlockSpec((2, 128, 384), lambda i: (i, 0, 0)),
-            whole(keys),
-            pl.BlockSpec((2, 1, 128), lambda i: (i, 0, 0)),
-        ] + [whole(a) for a in weights],
-        out_specs=[
-            pl.BlockSpec((2, 128, 384), lambda i: (i, 0, 0)),
-            pl.BlockSpec((1, 64, 256), lambda i: (i, 0, 0)),
-            pl.BlockSpec((1, 64, 256), lambda i: (i, 0, 0)),
-        ],
         out_shape=[
             jax.ShapeDtypeStruct(x.shape, BF16),
-            jax.ShapeDtypeStruct((8, 64, 256), BF16),
-            jax.ShapeDtypeStruct((8, 64, 256), BF16),
+            jax.ShapeDtypeStruct((2, 8, 64, 256), BF16),
         ],
-        scratch_shapes=attend_scratch(16, 24, 128),
+        scratch_shapes=[pltpu.VMEM((3, 16, 128, 384), BF16)] + attend_scratch(16, 24, 128, 384),
         cost_estimate=pl.CostEstimate(flops=2048 * 384 * 384 * 20, bytes_accessed=x.size * 4, transcendentals=0),
         name="col_att",
-    )(x, keys, lanes, *weights)
+    )(x, keys, lanes, w, wo, wp)
 
 
 def opm_kernel(own_ref, full_ref, z_ref, norm_ref, w_ref, out_ref, full32_ref, o_ref):
@@ -251,7 +279,7 @@
         m = row_attention(m, row_keys, row_bias, w_row_in[0], w_row_out[0], 16, 24, True)
         m = lax.all_to_all(m, 'dap', 1, 0, tiled=True)
         m = jnp.transpose(m, (1, 0, 2))
-        m, ac1, ac2 = column_pair(m, col_keys, lanes, (w_col_in[0], w_col_out[0], w_opm_in[0], w_col_in[1], w_col_out[1], w_opm_in[1]))
+        m, (ac1, ac2) = column_pair(m, col_keys, lanes, w_col_in, w_col_out, w_opm_in)
         z = opm(ac1[:, :32].reshape(256, 256), gather_full(ac1[:, 32:]), z, norm, w_opm_1)
         ts_bias = bias(z, w_ts_bias[0], 'ijc,ch->hji', 2)
         z = row_attention(z, tri_keys, ts_bias, w_ts_in[0], w_ts_out[0], 4, 32, False)

time: 252 us -> 242 us (0.960)
  Pallas kernels: 111 us -> 101 us
  local copies, waits for them, and re-layouts: 29.7 us -> 25.4 us
  waiting for transfers between devices: 8.03 us -> 12.2 us
    pallas_call x7, Pallas kernels: 100 us -> 90 us  [the longest x6 52.4 us: row_attention(): pl.pallas_call(functools.partial(row_kernel, heads, dim, per_row, groups...]
    slice x3 -> x0, local copies, waits for them, and re-layouts: 4.85 us -> none  [the longest x1 3.31 us: local_step(): w_col_in[1]]
    all_to_all x1, waiting for transfers between devices: 8.03 us -> 12.2 us  [local_step(): m = lax.all_to_all(m, 'dap', 1, 0, tiled=True)]
  transfers between devices with their start and end apart: 4 -> 4, of which waited for: 1 -> 1; matrix products, arithmetic and copies ran while one was open for 7% -> 6% of each run, Pallas kernels for 2% -> 2%
where the time goes in v3:
time: 242 us; the launch traced here: 241 us
  Pallas kernels  101 us (42%)
  blocking collectives  63.8 us (26%)
  local copies, waits for them, and re-layouts  25.4 us (10%)
  other arithmetic  16.7 us (7%)
  starting transfers between devices  14.3 us (6%)
  waiting for transfers between devices  12.2 us (5%)
  matrix products  6.45 us (3%)
    pallas_call x6, Pallas kernels, row_attention(): pl.pallas_call(functools.partial(row_kernel, heads, dim, per_row, groups...  52.4 us
    all_gather x6, blocking collectives, bias(): return lax.all_gather(part, 'dap', axis=axis, tiled=True)  49.3 us
    pallas_call x1, Pallas kernels, column_pair(): pl.pallas_call(col_kernel, out_shape=[jax.ShapeDtypeStruct(x.shape, BF16)...  37.6 us
    all_gather x2, blocking collectives, gather_full(): lax.all_gather(half.reshape(8, 32, 2, 128).transpose(0, 2, 1, 3).reshape(...  14.5 us
    all_to_all x1, waiting for transfers between devices, local_step(): m = lax.all_to_all(m, 'dap', 1, 0, tiled=True)  12.2 us
    pallas_call x2, Pallas kernels, opm(): pl.pallas_call(opm_kernel, out_shape=jax.ShapeDtypeStruct(z.shape, BF16),...  11.1 us
    dot_general x6, matrix products, bias(): jnp.einsum(form, layer_norm(z_blk), w, preferred_element_type=F32)  5.72 us
    pallas_call x2, local copies, waits for them, and re-layouts, row_attention(): pl.pallas_call(functools.partial(row_kernel, heads, dim, per_row, groups...  5.31 us
  transfers between devices with their start and end apart: 4, of which 1 were waited for; matrix products, arithmetic and copies ran while one was open for 6% of the time, Pallas kernels for 2%

profile of v3, /device:TPU:0, one launch (start us, length us, event | category | flops | bytes accessed | tf_op | source)
XLA Modules:
  0.0 240.9 jit_solution(9600038268457411413)
XLA Ops:
  0.6 0.8 convert_element_type.102
  1.4 1.2 convert_reduce_fusion.5
  2.6 1.3 fusion.27
  3.9 1.6 fusion
  5.5 7.5 %all_gather.24 = bf16[16,64,64]{1,0,2:T(8,128)(2,1)S(1)} all-gather(bf16[16,64,16]{1,0,2:T(8,128)(2,1)S(1)} %fusion), channel_id=1, replica_groups=mesh['data'=4,'dap'=4] {'dap'}, dimensions={2}, use_global_device_ids=true | all-gather | bytes 163840 | tf_op jit(solution)/shard_map/all_gather | solution.py:272
  13.3 1.0 pad_maximum_fusion.bias_ref
  14.3 1.7 fusion.59
  16.0 0.9 fusion.60
  17.6 16.3 %row_att.2 = bf16[32,64,384]{2,1,0:T(8,128)(2,1)} custom-call(bf16[32,64,384]{2,1,0:T(8,128)(2,1)} %x_ref.1, f32[64,32]{1,0:T(8,128)} %dynamic-slice_bitcast_fusion.keys_ref, f32[16,64,128]{2,1,0:T(8,128)} %pad_maximum_fusion.bias_ref, bf16[1536,384]{1,0:T(8,128)(2,1)} %bitcast.146, bf16[384,384]{1,0:T(8,128)(2,1)} %bitcast.160), custom_call_target="tpu_custom_call" | custom-call | flops 3019898880 | bytes 3145728 | tf_op jit(solution)/shard_map/row_att/pallas_call | solution.py:171
  33.9 3.5 %copy.63 = bf16[32,64,384]{2,0,1:T(8,128)(2,1)} copy(bf16[32,64,384]{2,1,0:T(8,128)(2,1)} %row_att.2) | data formatting | bytes 3145728 | tf_op jit(solution)/shard_map/row_att/pallas_call | solution.py:171
  37.4 3.7 %all-to-all-start = ((bf16[32,64,384]{2,0,1:T(8,128)(2,1)}), bf16[32,64,384]{2,0,1:T(8,128)(2,1)S(1)}, u32[]{:S(2)}, u32[]{:S(2)}) async-start(bf16[32,64,384]{2,0,1:T(8,128)(2,1)} %copy.63), calls=%async_computation | async-start | bytes 3145728 | tf_op jit(solution)/shard_map/all_to_all | solution.py:280
  42.1 0.9 copy.72.w_ref
  43.6 0.8 copy.81.w_ref
  45.8 1.4 fusion.65
  48.6 12.2 %all-to-all-done = bf16[32,64,384]{2,0,1:T(8,128)(2,1)S(1)} async-done(((bf16[32,64,384]{2,0,1:T(8,128)(2,1)}), bf16[32,64,384]{2,0,1:T(8,128)(2,1)S(1)}, u32[]{:S(2)}, u32[]{:S(2)}) %all-to-all-start) | async-done | bytes 1572896 | tf_op jit(solution)/shard_map/all_to_all | solution.py:280
  60.9 1.4 copy.64
  62.3 37.6 %col_att.1 = (bf16[16,128,384]{2,1,0:T(8,128)(2,1)}, bf16[2,8,64,256]{3,2,1,0:T(8,128)(2,1)}) custom-call(bf16[16,128,384]{2,1,0:T(8,128)(2,1)} %bitcast.144, f32[128,16]{1,0:T(8,128)} %copy.65.keys_ref, f32[16,1,128]{2,1,0:T(1,128)} %bitcast.170, bf16[2,1536,384]{2,1,0:T(8,128)(2,1)} %bitcast.171, bf16[2,384,384]{2,1,0:T(8,128)(2,1)} %bitcast.172, ...), custom_call_target="tpu_custom_call" | custom-call | flops 6039797760 | bytes 3145728 | tf_op jit(solution)/shard_map/col_att/pallas_call | solution.py:207
  99.9 1.1 slice_bitcast_fusion
  101.7 6.7 %all_gather.25.full_ref = bf16[2048,128]{1,0:T(8,128)(2,1)} all-gather(bf16[512,128]{1,0:T(8,128)(2,1)S(1)} %bitcast.154), channel_id=1, replica_groups=mesh['data'=4,'dap'=4] {'dap'}, dimensions={0}, use_global_device_ids=true | all-gather | bytes 655360 | tf_op jit(solution)/shard_map/all_gather | solution.py:275
  108.4 5.5 %opm.2.x_ref = bf16[16,64,128]{2,1,0:T(8,128)(2,1)} custom-call(bf16[256,256]{1,0:T(8,128)(2,1)} %bitcast.165, bf16[2048,128]{1,0:T(8,128)(2,1)} %all_gather.25.full_ref, bf16[16,64,128]{2,1,0:T(8,128)(2,1)} %z_ref.1, f32[64,16]{1,0:T(8,128)} %convolution_bitcast_fusion.norm_ref, bf16[128,1024]{1,0:T(8,128)(2,1)} %copy.72.w_ref), custom_call_target="tpu_custom_call" | custom-call | flops 1000000000 | bytes 1048576 | tf_op jit(solution)/shard_map/opm/pallas_call | solution.py:243
  113.9 1.2 convert_reduce_fusion.4
  115.1 1.3 fusion.25
  116.5 1.5 fusion.1
  118.0 5.2 %all_gather.26 = bf16[4,64,64]{1,0,2:T(4,128)(2,1)S(1)} all-gather(bf16[4,64,16]{1,0,2:T(4,128)(2,1)S(1)} %fusion.1), channel_id=1, replica_groups=mesh['data'=4,'dap'=4] {'dap'}, dimensions={2}, use_global_device_ids=true | all-gather | bytes 40960 | tf_op jit(solution)/shard_map/all_gather | solution.py:272
  123.4 0.8 pad_maximum_fusion.2.bias_ref
  124.1 4.9 %tri_att.4 = bf16[16,64,128]{2,1,0:T(8,128)(2,1)} custom-call(bf16[16,64,128]{2,1,0:T(8,128)(2,1)} %opm.2.x_ref, f32[64,1]{1,0:T(8,128)} %copy.74.keys_ref, f32[4,64,128]{2,1,0:T(8,128)} %pad_maximum_fusion.2.bias_ref, bf16[512,128]{1,0:T(8,128)(2,1)} %bitcast.158, bf16[128,128]{1,0:T(8,128)(2,1)} %bitcast.169), custom_call_target="tpu_custom_call" | custom-call | flops 167772160 | bytes 524288 | tf_op jit(solution)/shard_map/tri_att/pallas_call | solution.py:171
  129.1 1.8 copy.75
  130.9 3.4 %all-to-all-start.2 = ((bf16[16,64,128]{2,0,1:T(8,128)(2,1)}), bf16[16,64,128]{2,0,1:T(8,128)(2,1)S(1)}, u32[]{:S(2)}, u32[]{:S(2)}) async-start(bf16[16,64,128]{2,0,1:T(8,128)(2,1)} %copy.75), calls=%async_computation.2 | async-start | bytes 524288 | tf_op jit(solution)/shard_map/all_to_all | solution.py:286
  134.3 2.1 copy.67
  136.4 7.8 %all_gather.29.full_ref = bf16[2048,128]{1,0:T(8,128)(2,1)} all-gather(bf16[512,128]{1,0:T(8,128)(2,1)S(1)} %bitcast.153), channel_id=1, replica_groups=mesh['data'=4,'dap'=4] {'dap'}, dimensions={0}, use_global_device_ids=true | all-gather | bytes 655360 | tf_op jit(solution)/shard_map/all_gather | solution.py:275
  145.3 5.2 %all_gather.27 = bf16[4,64,64]{1,0,2:T(4,128)(2,1)S(1)} all-gather(bf16[4,64,16]{1,0,2:T(4,128)(2,1)S(1)} %fusion.2), channel_id=1, replica_groups=mesh['data'=4,'dap'=4] {'dap'}, dimensions={2}, use_global_device_ids=true | all-gather | bytes 40960 | tf_op jit(solution)/shard_map/all_gather | solution.py:272
  151.4 4.9 %tri_att.5.z_ref = bf16[16,64,128]{2,1,0:T(8,128)(2,1)} custom-call(bf16[16,64,128]{2,1,0:T(8,128)(2,1)} %bitcast.140, f32[64,1]{1,0:T(8,128)} %copy.74.keys_ref, f32[4,64,128]{2,1,0:T(8,128)} %pad_maximum_fusion.3.bias_ref, bf16[512,128]{1,0:T(8,128)(2,1)} %bitcast.157, bf16[128,128]{1,0:T(8,128)(2,1)} %bitcast.168), custom_call_target="tpu_custom_call" | custom-call | flops 167772160 | bytes 524288 | tf_op jit(solution)/shard_map/tri_att/pallas_call | solution.py:171
  156.4 1.2 convert_reduce_fusion.2
  157.5 5.5 %opm.3.x_ref = bf16[16,64,128]{2,1,0:T(8,128)(2,1)} custom-call(bf16[256,256]{1,0:T(8,128)(2,1)} %bitcast.164, bf16[2048,128]{1,0:T(8,128)(2,1)} %all_gather.29.full_ref, bf16[16,64,128]{2,1,0:T(8,128)(2,1)} %tri_att.5.z_ref, f32[64,16]{1,0:T(8,128)} %convolution_bitcast_fusion.norm_ref, bf16[128,1024]{1,0:T(8,128)(2,1)} %copy.81.w_ref), custom_call_target="tpu_custom_call" | custom-call | flops 1000000000 | bytes 1048576 | tf_op jit(solution)/shard_map/opm/pallas_call | solution.py:243
  163.1 1.2 convert_reduce_fusion.1
  164.2 1.3 fusion.19
  165.6 1.4 fusion.3
  167.1 5.4 %all_gather.30 = bf16[4,64,64]{1,0,2:T(4,128)(2,1)S(1)} all-gather(bf16[4,64,16]{1,0,2:T(4,128)(2,1)S(1)} %fusion.3), channel_id=1, replica_groups=mesh['data'=4,'dap'=4] {'dap'}, dimensions={2}, use_global_device_ids=true | all-gather | bytes 40960 | tf_op jit(solution)/shard_map/all_gather | solution.py:272
  173.3 4.9 %tri_att.6 = bf16[16,64,128]{2,1,0:T(8,128)(2,1)} custom-call(bf16[16,64,128]{2,1,0:T(8,128)(2,1)} %opm.3.x_ref, f32[64,1]{1,0:T(8,128)} %copy.74.keys_ref, f32[4,64,128]{2,1,0:T(8,128)} %pad_maximum_fusion.4.bias_ref, bf16[512,128]{1,0:T(8,128)(2,1)} %bitcast.156, bf16[128,128]{1,0:T(8,128)(2,1)} %bitcast.167), custom_call_target="tpu_custom_call" | custom-call | flops 167772160 | bytes 524288 | tf_op jit(solution)/shard_map/tri_att/pallas_call | solution.py:171
  178.2 1.8 copy.84
  180.1 3.4 %all-to-all-start.3 = ((bf16[64,16,128]{2,1,0:T(8,128)(2,1)}), bf16[64,16,128]{2,1,0:T(8,128)(2,1)S(1)}, u32[]{:S(2)}, u32[]{:S(2)}) async-start(bf16[64,16,128]{2,1,0:T(8,128)(2,1)} %copy.84), calls=%async_computation.3 | async-start | bytes 524288 | tf_op jit(solution)/shard_map/all_to_all | solution.py:296
  184.4 7.1 %all_gather.28 = bf16[16,64,64]{2,1,0:T(8,128)(2,1)S(1)} all-gather(bf16[16,16,64]{2,1,0:T(8,128)(2,1)S(1)} %bitcast.161), channel_id=1, replica_groups=mesh['data'=4,'dap'=4] {'dap'}, dimensions={1}, use_global_device_ids=true | all-gather | bytes 163840 | tf_op jit(solution)/shard_map/all_gather | solution.py:272
  191.6 1.0 pad_maximum_fusion.1.bias_ref
  192.6 3.8 %all-to-all-start.1 = ((bf16[128,16,384]{2,1,0:T(8,128)(2,1)}), bf16[128,16,384]{2,1,0:T(8,128)(2,1)S(1)}, u32[]{:S(2)}, u32[]{:S(2)}) async-start(bf16[128,16,384]{2,1,0:T(8,128)(2,1)} %copy.67), calls=%async_computation.1 | async-start | bytes 3145728 | tf_op jit(solution)/shard_map/all_to_all | solution.py:292
  198.4 18.9 %all_gather.31 = bf16[4,64,64]{1,0,2:T(4,128)(2,1)S(1)} all-gather(bf16[4,64,16]{1,0,2:T(4,128)(2,1)S(1)} %fusion.4), channel_id=1, replica_groups=mesh['data'=4,'dap'=4] {'dap'}, dimensions={2}, use_global_device_ids=true | all-gather | bytes 40960 | tf_op jit(solution)/shard_map/all_gather | solution.py:272
  218.2 4.9 %tri_att.7 = bf16[16,64,128]{2,1,0:T(8,128)(2,1)} custom-call(bf16[16,64,128]{2,1,0:T(8,128)(2,1)} %bitcast.147, f32[64,1]{1,0:T(8,128)} %copy.74.keys_ref, f32[4,64,128]{2,1,0:T(8,128)} %pad_maximum_fusion.5.bias_ref, bf16[512,128]{1,0:T(8,128)(2,1)} %bitcast.155, bf16[128,128]{1,0:T(8,128)(2,1)} %bitcast.166), custom_call_target="tpu_custom_call" | custom-call | flops 167772160 | bytes 524288 | tf_op jit(solution)/shard_map/tri_att/pallas_call | solution.py:171
  223.2 1.4 copy.68
  224.6 16.3 %row_att.3 = bf16[32,64,384]{2,1,0:T(8,128)(2,1)} custom-call(bf16[32,64,384]{2,1,0:T(8,128)(2,1)} %bitcast.143, f32[64,32]{1,0:T(8,128)} %dynamic-slice_bitcast_fusion.keys_ref, f32[16,64,128]{2,1,0:T(8,128)} %pad_maximum_fusion.1.bias_ref, bf16[1536,384]{1,0:T(8,128)(2,1)} %bitcast.145, bf16[384,384]{1,0:T(8,128)(2,1)} %bitcast.159), custom_call_target="tpu_custom_call" | custom-call | flops 3019898880 | bytes 3145728 | tf_op jit(solution)/shard_map/row_att/pallas_call | solution.py:171
  (85 shorter events, 13.1 us)
Async XLA Ops:
  3.9 10.4 %copy-start.1 = (bf16[2,384,4,16,24]{1,4,3,2,0:T(8,128)(2,1)S(1)}, bf16[2,384,4,16,24]{1,4,3,2,0:T(8,128)(2,1)}, u32[]{:S(2)}) copy-start(bf16[2,384,4,16,24]{1,4,3,2,0:T(8,128)(2,1)} %param.22) | copy-start | bytes 7077892
  14.3 1.7 copy-start.4
  37.4 3.7 %copy-start.5 = (bf16[2,32,32,128]{3,2,1,0:T(8,128)(2,1)S(1)}, bf16[2,32,32,128]{3,2,1,0:T(8,128)(2,1)}, u32[]{:S(2)}) copy-start(bf16[2,32,32,128]{3,2,1,0:T(8,128)(2,1)} %param.27) | copy-start | bytes 1572868
  37.4 3.8 %copy-start.14 = (s32[64]{0:T(128)S(1)}, s32[64]{0:T(128)}, u32[]{:S(2)}) copy-start(s32[64]{0:T(128)} %param.20) | copy-start | bytes 772
  37.4 23.5 %all-to-all-start = ((bf16[32,64,384]{2,0,1:T(8,128)(2,1)}), bf16[32,64,384]{2,0,1:T(8,128)(2,1)S(1)}, u32[]{:S(2)}, u32[]{:S(2)}) async-start(bf16[32,64,384]{2,0,1:T(8,128)(2,1)} %copy.63), calls=%async_computation | async-start | bytes 3145728 | tf_op jit(solution)/shard_map/all_to_all | solution.py:280
  41.1 3.4 %copy-start.8 = (s32[128,64]{0,1:T(8,128)S(1)}, s32[128,64]{0,1:T(8,128)}, u32[]{:S(2)}) copy-start(s32[128,64]{0,1:T(8,128)} %param.19) | copy-start | bytes 98308
  41.1 4.1 %copy-start.10 = (bf16[2,4,32,128]{3,2,1,0:T(8,128)(2,1)S(1)}, bf16[2,4,32,128]{3,2,1,0:T(8,128)(2,1)}, u32[]{:S(2)}) copy-start(bf16[2,4,32,128]{3,2,1,0:T(8,128)(2,1)} %param.30) | copy-start | bytes 196612
  41.1 6.1 %copy-start.6 = (bf16[2,128,4,4,32]{1,4,3,2,0:T(8,128)(2,1)S(1)}, bf16[2,128,4,4,32]{1,4,3,2,0:T(8,128)(2,1)}, u32[]{:S(2)}) copy-start(bf16[2,128,4,4,32]{1,4,3,2,0:T(8,128)(2,1)} %param.29) | copy-start | bytes 786436
  41.1 6.8 %copy-start.7 = (bf16[2,128,4,4,32]{1,4,3,2,0:T(8,128)(2,1)S(1)}, bf16[2,128,4,4,32]{1,4,3,2,0:T(8,128)(2,1)}, u32[]{:S(2)}) copy-start(bf16[2,128,4,4,32]{1,4,3,2,0:T(8,128)(2,1)} %param.32) | copy-start | bytes 786436
  41.2 21.1 %copy-start.9 = (f32[128,16]{0,1:T(8,128)}, f32[128,16]{0,1:T(8,128)S(1)}, u32[]{:S(2)}) copy-start(f32[128,16]{0,1:T(8,128)S(1)} %constant_dynamic-slice_fusion) | copy-start | bytes 24580
  108.4 8.1 %copy-start.11 = (bf16[2,128,4]{1,2,0:T(4,128)(2,1)S(1)}, bf16[2,128,4]{1,2,0:T(4,128)(2,1)}, u32[]{:S(2)}) copy-start(bf16[2,128,4]{1,2,0:T(4,128)(2,1)} %param.28) | copy-start | bytes 6148
  116.5 17.9 %copy-start.3 = (bf16[16,128,384]{2,1,0:T(8,128)(2,1)S(1)}, bf16[16,128,384]{2,1,0:T(8,128)(2,1)}, u32[]{:S(2)}) copy-start(bf16[16,128,384]{2,1,0:T(8,128)(2,1)} %get-tuple-element.4) | copy-start | bytes 4718596
  130.9 13.3 %all-to-all-start.2 = ((bf16[16,64,128]{2,0,1:T(8,128)(2,1)}), bf16[16,64,128]{2,0,1:T(8,128)(2,1)S(1)}, u32[]{:S(2)}, u32[]{:S(2)}) async-start(bf16[16,64,128]{2,0,1:T(8,128)(2,1)} %copy.75), calls=%async_computation.2 | async-start | bytes 524288 | tf_op jit(solution)/shard_map/all_to_all | solution.py:286
  136.4 8.5 %copy-start.13 = (bf16[2,128,4]{1,2,0:T(4,128)(2,1)S(1)}, bf16[2,128,4]{1,2,0:T(4,128)(2,1)}, u32[]{:S(2)}) copy-start(bf16[2,128,4]{1,2,0:T(4,128)(2,1)} %param.31) | copy-start | bytes 6148
  144.2 7.2 %copy-start = (bf16[16,4,16,128]{3,0,1,2:T(8,128)(2,1)}, bf16[16,4,16,128]{3,0,1,2:T(8,128)(2,1)S(1)}, u32[]{:S(2)}) copy-start(bf16[16,4,16,128]{3,0,1,2:T(8,128)(2,1)S(1)} %copy.76) | copy-start | bytes 786436
  165.6 17.9 %copy-start.2 = (bf16[16,64,128]{2,1,0:T(8,128)(2,1)S(1)}, bf16[16,64,128]{2,1,0:T(8,128)(2,1)}, u32[]{:S(2)}) copy-start(bf16[16,64,128]{2,1,0:T(8,128)(2,1)} %tri_att.5.z_ref) | copy-start | bytes 786436
  167.1 16.9 %copy-start.12 = (bf16[2,128,16]{1,2,0:T(8,128)(2,1)S(1)}, bf16[2,128,16]{1,2,0:T(8,128)(2,1)}, u32[]{:S(2)}) copy-start(bf16[2,128,16]{1,2,0:T(8,128)(2,1)} %param.21) | copy-start | bytes 24580
  180.1 12.5 %all-to-all-start.3 = ((bf16[64,16,128]{2,1,0:T(8,128)(2,1)}), bf16[64,16,128]{2,1,0:T(8,128)(2,1)S(1)}, u32[]{:S(2)}, u32[]{:S(2)}) async-start(bf16[64,16,128]{2,1,0:T(8,128)(2,1)} %copy.84), calls=%async_computation.3 | async-start | bytes 524288 | tf_op jit(solution)/shard_map/all_to_all | solution.py:296
  192.6 30.6 %all-to-all-start.1 = ((bf16[128,16,384]{2,1,0:T(8,128)(2,1)}), bf16[128,16,384]{2,1,0:T(8,128)(2,1)S(1)}, u32[]{:S(2)}, u32[]{:S(2)}) async-start(bf16[128,16,384]{2,1,0:T(8,128)(2,1)} %copy.67), calls=%async_computation.1 | async-start | bytes 3145728 | tf_op jit(solution)/shard_map/all_to_all | solution.py:292

commit v4 on v3

v4 whole, which is shorter than its diff:
```python
import functools

import jax
import jax.numpy as jnp
from jax import lax
from jax.experimental import pallas as pl
from jax.experimental.pallas import tpu as pltpu
from jax.sharding import PartitionSpec as P

LOG2E = 1.4426950408889634
NEG = -1e9 * LOG2E
F32 = jnp.float32
BF16 = jnp.bfloat16
LAG = 2
SLOTS = 4
NT = (((1,), (1,)), ((), ()))
LANES = 128
RES = 64
BLOCK = 256
HELD = 16
WIDE = 384
CELLS = 1024


def layer_norm(values):
    flat = values.astype(F32)
    row_mean = jnp.mean(flat, axis=-1, keepdims=True)
    centered = flat - row_mean
    row_var = jnp.mean(centered * centered, axis=-1, keepdims=True)
    return (centered * lax.rsqrt(row_var + 1e-5)).astype(BF16)


def half_masks(rows, split):
    index = lax.broadcasted_iota(jnp.int32, (rows, LANES), 0)
    upper = (index < split).astype(F32).astype(BF16)
    lower = (index >= split).astype(F32).astype(BF16)
    return upper, lower


def attend_units(pt_ref, gt_ref, kt_ref, lg_ref, pr_ref, heads, dim, keep, bias_ref, work):
    width = heads * dim
    rows = 2 * dim
    pairs = heads // 2
    units = 2 * pairs
    up, low = half_masks(rows, dim)
    scale = dim ** -0.5 * LOG2E
    if bias_ref is not None:
        left = lax.broadcasted_iota(jnp.int32, (RES, LANES), 1) < RES
        left_b = left.astype(F32).astype(BF16)
        right_b = (1.0 - left.astype(F32)).astype(BF16)

    def place(unit):
        return pl.ds(unit // pairs * LANES, LANES), rows * (unit % pairs)

    def turn_keys(unit):
        ln, r = place(unit)
        kt_ref[unit % SLOTS] = pt_ref[pl.ds(width + r, rows), ln].T

    def make_logits(unit):
        ln, r = place(unit)
        q = pt_ref[pl.ds(r, rows), ln]
        rhs = jnp.concatenate([q * up, q * low], axis=1)
        logits2 = jnp.dot(kt_ref[unit % SLOTS], rhs, preferred_element_type=F32)
        for half in range(2):
            lg = logits2[:, LANES * half:LANES * half + LANES]
            if bias_ref is not None:
                lg = jnp.where(left, lg[0:RES], lg[RES:LANES])
            lg_ref[unit % SLOTS, half] = lg

    def soften(unit):
        blk, hp = unit // pairs, unit % pairs
        for half in range(2):
            lg = lg_ref[unit % SLOTS, half] * scale
            if bias_ref is not None:
                lg = lg + bias_ref[2 * hp + half]
            lg = jnp.where(keep[blk], lg, NEG)
            e = jnp.exp2(lg - jnp.max(lg, axis=0, keepdims=True))
            p = (e * (1.0 / jnp.sum(e, axis=0, keepdims=True))).astype(BF16)
            pr_ref[unit % SLOTS, half] = p

    def mix(unit):
        ln, r = place(unit)
        v = pt_ref[pl.ds(2 * width + r, rows), ln]
        g = pt_ref[pl.ds(3 * width + r, rows), ln]
        probs = []
        for half in range(2):
            p = pr_ref[unit % SLOTS, half]
            probs += [p] if bias_ref is None else [p * left_b, p * right_b]
        att = jnp.dot(jnp.concatenate([v * up, v * low], axis=1), jnp.concatenate(probs, axis=0), preferred_element_type=F32)
        gt_ref[pl.ds(r, rows), ln] = (att * jax.nn.sigmoid(g.astype(F32))).astype(BF16)

    stages = ((turn_keys, 0), (make_logits, LAG), (soften, 2 * LAG), (mix, 3 * LAG))
    ticks = units + 3 * LAG
    for tick in range(ticks):
        for stage, lag in stages:
            if 0 <= tick - lag < units:
                stage(tick - lag)
        for job in work[len(work) * tick // ticks:len(work) * (tick + 1) // ticks]:
            job()


def attend_step(half, scratch, heads, dim, x_new, w, keep, bias_ref, x_old, wo, finish):
    ln_ref, pt_refs, gt_refs, others = scratch[0], scratch[1:3], scratch[3:5], scratch[5:8]
    width = heads * dim
    chunk = BLOCK if width > BLOCK else LANES

    def norm():
        ln_ref[...] = layer_norm(x_new())

    def project(part):
        def job():
            sl = pl.ds(part * chunk, chunk)
            pt_refs[half][sl, :] = lax.dot_general(w(sl), ln_ref[...], NT, preferred_element_type=F32).astype(BF16)
        return job

    def leave():
        update = jnp.dot(gt_refs[half][...].T, wo(), preferred_element_type=F32)
        finish((x_old() + update).astype(BF16))

    work = [norm, leave] + [project(part) for part in range(4 * width // chunk)]
    attend_units(pt_refs[1 - half], gt_refs[1 - half], *others, heads, dim, keep, bias_ref, work)


def attend_scratch(heads, dim, keys, channels):
    inner = heads * dim
    return [
        pltpu.VMEM((BLOCK, channels), BF16),
        pltpu.VMEM((4 * inner, BLOCK), BF16),
        pltpu.VMEM((4 * inner, BLOCK), BF16),
        pltpu.VMEM((inner, BLOCK), BF16),
        pltpu.VMEM((inner, BLOCK), BF16),
        pltpu.VMEM((SLOTS, LANES, 2 * dim), BF16),
        pltpu.VMEM((SLOTS, 2, keys, LANES), F32),
        pltpu.VMEM((SLOTS, 2, keys, LANES), BF16),
    ]


def pick_column(table, col):
    lane = lax.broadcasted_iota(jnp.int32, table.shape, 1)
    return jnp.sum(jnp.where(lane == col, table, 0.0), axis=1, keepdims=True)


def row_kernel(heads, dim, per_row, blocks, x_ref, keys_ref, bias_ref, w_ref, wo_ref, out_ref, *scratch):
    channels = x_ref.shape[-1]
    left = lax.broadcasted_iota(jnp.int32, (RES, LANES), 1) < RES

    def body(turn, carry):
        for half in range(2):
            i = 2 * turn + half
            new = jnp.minimum(i, blocks - 1)
            mid = jnp.clip(i - 1, 0, blocks - 1)
            old = jnp.clip(i - 2, 0, blocks - 1)
            keep = []
            for blk in range(2):
                if per_row:
                    first = pick_column(keys_ref[...], mid * 4 + 2 * blk)
                    second = pick_column(keys_ref[...], mid * 4 + 2 * blk + 1)
                    keep.append(jnp.where(left, first, second) > 0.5)
                else:
                    keep.append(jnp.broadcast_to(keys_ref[...], (RES, LANES)) > 0.5)
            read = lambda at: x_ref[pl.ds(at * 4, 4)].astype(F32).reshape(BLOCK, channels)

            def finish(out):
                out_ref[pl.ds(old * 4, 4)] = out.reshape(4, RES, channels)

            attend_step(half, scratch, heads, dim, lambda: read(new), lambda sl: w_ref[sl, :], keep, bias_ref,
                        lambda: read(old), lambda: wo_ref[...], finish)
        return carry

    lax.fori_loop(0, blocks // 2 + 1, body, 0)


def row_attention(x, keys, bias_t, w, wo, heads, dim, per_row):
    groups, length, width = x.shape
    bias_t = bias_t.astype(F32) * LOG2E
    return pl.pallas_call(
        functools.partial(row_kernel, heads, dim, per_row, groups // 4),
        out_shape=jax.ShapeDtypeStruct(x.shape, BF16),
        scratch_shapes=attend_scratch(heads, dim, RES, width),
        cost_estimate=pl.CostEstimate(flops=groups * length * width * heads * dim * 10, bytes_accessed=x.size * 4, transcendentals=0),
        name="row_att" if per_row else "tri_att",
    )(x, keys, bias_t, w, wo)


def col_kernel(x_ref, keys_ref, lanes_ref, w_ref, wo_ref, wp_ref, out_ref, pairs_ref, singles_ref, m_ref, *scratch):
    m_ref[0] = x_ref[...]

    def body(turn, carry):
        for half in range(2):
            i = 2 * turn + half
            new = jnp.minimum(i, 15)
            mid = jnp.clip(i - 1, 0, 15)
            old = jnp.clip(i - 2, 0, 15)
            keep = [jnp.broadcast_to(pick_column(keys_ref[...], mid % 8 * 2 + blk), (LANES, LANES)) > 0.5 for blk in range(2)]
            read = lambda at: m_ref[at // 8, pl.ds(at % 8 * 2, 2)].astype(F32).reshape(BLOCK, WIDE)

            def finish(out):
                m_ref[old // 8 + 1, pl.ds(old % 8 * 2, 2)] = out.reshape(2, LANES, WIDE)
                ac = lax.dot_general(wp_ref[old // 8], layer_norm(out), NT, preferred_element_type=F32)
                lane_mask = jnp.concatenate([lanes_ref[old % 8 * 2], lanes_ref[old % 8 * 2 + 1]], axis=1)
                ac = (ac * lane_mask).astype(BF16)
                own, part = ac[:32], ac[32:]
                pairs_ref[old // 8, 0, old % 8] = own
                pairs_ref[old // 8, 1, old % 8] = part
                for blk in range(2):
                    singles_ref[old // 8, 0, old % 8 * 2 + blk] = own[:, LANES * blk:LANES * blk + LANES]
                    singles_ref[old // 8, 1, old % 8 * 2 + blk] = part[:, LANES * blk:LANES * blk + LANES]

            attend_step(half, scratch, HELD, 24, lambda: read(new), lambda sl: w_ref[new // 8, sl, :], keep, None,
                        lambda: read(old), lambda: wo_ref[old // 8], finish)
        return carry

    lax.fori_loop(0, 9, body, 0)
    out_ref[...] = m_ref[2]


def column_pair(x, keys, lanes, w, wo, wp):
    return pl.pallas_call(
        col_kernel,
        out_shape=[
            jax.ShapeDtypeStruct(x.shape, BF16),
            jax.ShapeDtypeStruct((2, 2, 8, 32, BLOCK), BF16),
            jax.ShapeDtypeStruct((2, 2, HELD, 32, LANES), BF16),
        ],
        scratch_shapes=[pltpu.VMEM((3, HELD, LANES, WIDE), BF16)] + attend_scratch(HELD, 24, LANES, WIDE),
        cost_estimate=pl.CostEstimate(flops=2048 * WIDE * WIDE * 20, bytes_accessed=x.size * 4, transcendentals=0),
        name="col_att",
    )(x, keys, lanes, w, wo, wp)


def greet(me):
    barrier = pltpu.get_barrier_semaphore()
    for o in range(1, 4):
        pl.semaphore_signal(barrier, inc=1, device_id={'dap': lax.rem(me + o, 4)}, device_id_type=pl.DeviceIdType.MESH)
    pl.semaphore_wait(barrier, 3)


def push(me, kind, send_sem, recv_sem, source, target):
    copies = []
    for o in range(1, 4):
        peer = lax.rem(me + o, 4)
        copy = pltpu.make_async_remote_copy(
            src_ref=source(peer), dst_ref=target, send_sem=send_sem.at[3 * kind + o - 1],
            recv_sem=recv_sem.at[3 * kind + o - 1], device_id={'dap': peer}, device_id_type=pl.DeviceIdType.MESH)
        copy.start()
        copies.append(copy)
    return copies


def finish_all(copies):
    for copy in copies:
        copy.wait()


def local_bias_rows(ln_ref, w_ref):
    rows = w_ref.shape[0]
    index = lax.broadcasted_iota(jnp.int32, (rows, LANES), 0) % HELD
    total = jnp.zeros((rows, LANES), F32)
    for b in range(HELD):
        mine = w_ref[...] * (index == b).astype(F32).astype(BF16)
        part = ln_ref[pl.ds(RES * b, RES), :]
        total += lax.dot_general(mine, jnp.concatenate([part, part], axis=0), NT, preferred_element_type=F32)
    return total.astype(BF16)


def local_bias_lanes(me, ln_ref, w_ref):
    lane = lax.broadcasted_iota(jnp.int32, (1, BLOCK), 1) % RES
    total = jnp.zeros((RES, BLOCK), F32)
    for q in range(HELD):
        mine = w_ref[...] * (lane == HELD * me + q).astype(F32).astype(BF16)
        total += jnp.dot(ln_ref[pl.ds(RES * q, RES), :], mine, preferred_element_type=F32)
    return total.astype(BF16)


def triangle(zf_ref, ln_ref, w_ref, wo_ref, keep, bias_ref, pt_refs, gt_refs, others, ready):
    def project(block, part):
        def job():
            pt_refs[block % 2][pl.ds(LANES * part, LANES), :] = lax.dot_general(
                w_ref[pl.ds(LANES * part, LANES), :], ln_ref[pl.ds(BLOCK * block, BLOCK), :], NT,
                preferred_element_type=F32).astype(BF16)
        return job

    def leave(block):
        def job():
            update = jnp.dot(gt_refs[block % 2][...].T, wo_ref[...], preferred_element_type=F32)
            rows = pl.ds(BLOCK * block, BLOCK)
            zf_ref[rows, :] = (zf_ref[rows, :] + update).astype(BF16).astype(F32)
        return job

    for part in range(4):
        project(0, part)()
    ready()
    for block in range(4):
        work = [leave(block - 1)] if block else []
        if block < 3:
            work += [project(block + 1, part) for part in range(4)]
        attend_units(pt_refs[block % 2], gt_refs[block % 2], *others, 4, 32, [keep, keep], bias_ref, work)
    leave(3)()


def pair_kernel(has_next, own_ref, part_ref, z_ref, norm_ref, keys_ref, wm_ref, wba_ref, wa_ref, woa_ref, wbb_ref, wb_ref, wob_ref, *rest):
    if has_next:
        wn_ref, out_ref, next_ref = rest[:3]
        rest = rest[3:]
    else:
        out_ref = rest[0]
        rest = rest[1:]
    (full_ref, full32_ref, o_ref, zf_ref, zt_ref, ln_ref, lanes_ref, bias_ref, rows_ref, all_rows_ref, zs_ref, zr_ref,
     send_sem, recv_sem) = rest[:14]
    nl_ref = rest[14]
    att = rest[15:]
    pt_refs, gt_refs, others = att[0:2], att[2:4], att[4:7]
    me = lax.axis_index('dap')
    mine = pl.ds(pl.multiple_of(HELD * me, HELD), HELD)
    greet(me)
    copies = push(me, 0, send_sem, recv_sem, lambda peer: part_ref, full_ref.at[mine])
    full_ref[mine] = part_ref[...]
    keep = jnp.broadcast_to(keys_ref[...], (RES, LANES)) > 0.5
    left = lax.broadcasted_iota(jnp.int32, (RES, LANES), 1) < RES
    finish_all(copies)

    full32_ref[...] = full_ref[...].astype(F32).reshape(2048, LANES)
    own = own_ref[...].reshape(BLOCK, BLOCK)
    zeros = jnp.zeros((RES, LANES), BF16)

    def one(q, carry):
        c_q = full32_ref[pl.ds(q, RES, stride=32), :].astype(BF16)
        rhs = jnp.concatenate([jnp.concatenate([c_q, zeros], axis=1), jnp.concatenate([zeros, c_q], axis=1)], axis=0)
        o = lax.dot_general(own, rhs, NT, preferred_element_type=F32).astype(BF16)
        for pair in range(8):
            o_ref[pair, pl.ds(pl.multiple_of(q * 32, 32), 32), :] = o[32 * pair:32 * pair + 32]
        return carry

    lax.fori_loop(0, 32, one, 0, unroll=4)
    for pair in range(8):
        update = jnp.dot(wm_ref[...], o_ref[pair], preferred_element_type=F32).T
        z = z_ref[pl.ds(2 * pair, 2)].astype(F32).reshape(LANES, LANES)
        norm = jnp.concatenate([pick_column(norm_ref[...], 2 * pair), pick_column(norm_ref[...], 2 * pair + 1)], axis=0)
        z = (z + update / (1e-3 + norm)).astype(BF16).astype(F32)
        rows = pl.ds(LANES * pair, LANES)
        zf_ref[rows, :] = z
        ln_ref[rows, :] = layer_norm(z)

    lanes_ref[me] = local_bias_lanes(me, ln_ref, wba_ref)
    copies = push(me, 1, send_sem, recv_sem, lambda peer: lanes_ref.at[me], lanes_ref.at[me])

    def lanes_ready():
        finish_all(copies)
        total = (lanes_ref[0].astype(F32) + lanes_ref[1].astype(F32) + lanes_ref[2].astype(F32) + lanes_ref[3].astype(F32)) * LOG2E
        for two in range(2):
            value = total[:, LANES * two:LANES * two + LANES]
            turned = pltpu.roll(value, RES, 1)
            bias_ref[2 * two] = jnp.where(left, value, turned)
            bias_ref[2 * two + 1] = jnp.where(left, turned, value)

    triangle(zf_ref, ln_ref, wa_ref, woa_ref, keep, bias_ref, pt_refs, gt_refs, others, lanes_ready)

    zs_ref[...] = zf_ref[...].astype(BF16).reshape(HELD, RES, LANES)
    for block in range(8):
        rows = pl.ds(LANES * block, LANES)
        ln_ref[rows, :] = layer_norm(zf_ref[rows, :])
    rows_ref[...] = local_bias_rows(ln_ref, wbb_ref).reshape(4, HELD, LANES)
    moved = push(me, 2, send_sem, recv_sem, lambda peer: zs_ref.at[:, pl.ds(pl.multiple_of(HELD * peer, HELD), HELD), :], zr_ref.at[mine])
    copies = push(me, 3, send_sem, recv_sem, lambda peer: rows_ref, all_rows_ref.at[:, mine, :])
    zr_ref[mine] = zs_ref[:, mine, :]
    all_rows_ref[:, mine, :] = rows_ref[...]
    finish_all(moved)
    zt_ref[...] = zr_ref[...].astype(F32).reshape(CELLS, LANES)
    for row in range(HELD):
        value = zt_ref[pl.ds(row, RES, stride=HELD), :]
        zf_ref[pl.ds(RES * row, RES), :] = value
        ln_ref[pl.ds(RES * row, RES), :] = layer_norm(value)

    def rows_ready():
        finish_all(copies)
        bias_ref[...] = all_rows_ref[...].astype(F32) * LOG2E

    triangle(zf_ref, ln_ref, wb_ref, wob_ref, keep, bias_ref, pt_refs, gt_refs, others, rows_ready)
    out_ref[...] = zf_ref[...].astype(BF16).reshape(HELD, RES, LANES)
    if has_next:
        for block in range(8):
            rows = pl.ds(LANES * block, LANES)
            ln_ref[rows, :] = layer_norm(zf_ref[rows, :])
        nl_ref[...] = local_bias_rows(ln_ref, wn_ref).reshape(HELD, HELD, LANES)
        copies = push(me, 4, send_sem, recv_sem, lambda peer: nl_ref, next_ref.at[:, mine, :])
        next_ref[:, mine, :] = nl_ref[...]
        finish_all(copies)


def pair_block(ident, own, part, z, norm, keys, weights, w_next):
    has_next = w_next is not None
    out_shape = [jax.ShapeDtypeStruct(z.shape, BF16)]
    if has_next:
        weights = weights + (w_next,)
        out_shape.append(jax.ShapeDtypeStruct((HELD, RES, LANES), BF16))
    vmem = pl.BlockSpec(memory_space=pltpu.VMEM)
    args = (own, part, z, norm, keys) + weights
    return pl.pallas_call(
        functools.partial(pair_kernel, has_next),
        out_shape=out_shape,
        in_specs=[vmem] * len(args),
        out_specs=[vmem] * len(out_shape),
        scratch_shapes=[
            pltpu.VMEM((RES, 32, LANES), BF16),
            pltpu.VMEM((2048, LANES), F32),
            pltpu.VMEM((8, CELLS, LANES), BF16),
            pltpu.VMEM((CELLS, LANES), F32),
            pltpu.VMEM((CELLS, LANES), F32),
            pltpu.VMEM((CELLS, LANES), BF16),
            pltpu.VMEM((4, RES, BLOCK), BF16),
            pltpu.VMEM((4, RES, LANES), F32),
            pltpu.VMEM((4, HELD, LANES), BF16),
            pltpu.VMEM((4, RES, LANES), BF16),
            pltpu.VMEM((HELD, RES, LANES), BF16),
            pltpu.VMEM((RES, HELD, LANES), BF16),
            pltpu.SemaphoreType.DMA((15,)),
            pltpu.SemaphoreType.DMA((15,)),
            pltpu.VMEM((HELD, HELD, LANES), BF16),
        ] + attend_scratch(4, 32, RES, LANES)[1:],
        compiler_params=pltpu.CompilerParams(collective_id=ident, has_side_effects=True),
        cost_estimate=pl.CostEstimate(flops=10 ** 10, bytes_accessed=2 ** 22, transcendentals=0),
        name="pair_block",
    )(*args)


def solution(mesh):
    def local_step(m, z, mask, res_mask, w_row_bias, w_row_in, w_row_out, w_col_in, w_col_out, w_opm_in, w_opm_out, w_ts_bias, w_ts_in, w_ts_out, w_te_bias, w_te_in, w_te_out):
        dev = lax.axis_index('dap')
        flat_in = lambda w: jnp.transpose(w, (0, 2, 3, 4, 1)).reshape(2, -1, w.shape[1])
        flat_out = lambda w: w.reshape(2, -1, w.shape[-1])
        w_row_in, w_col_in, w_ts_in, w_te_in = map(flat_in, (w_row_in, w_col_in, w_ts_in, w_te_in))
        w_row_out, w_col_out, w_ts_out, w_te_out = map(flat_out, (w_row_out, w_col_out, w_ts_out, w_te_out))
        w_opm_in = jnp.transpose(w_opm_in, (0, 2, 3, 1)).reshape(2, RES, WIDE)
        w_opm_1 = jnp.transpose(w_opm_out[0], (2, 1, 0)).reshape(LANES, CELLS)
        w_opm_2 = jnp.transpose(w_opm_out[1], (2, 0, 1)).reshape(LANES, CELLS)

        mask_f = mask.astype(F32)
        row_keys = lax.dynamic_slice_in_dim(mask_f, dev * 32, 32, 0).T
        col_keys = lax.dynamic_slice_in_dim(mask_f, dev * HELD, HELD, 1)
        lanes = col_keys.T.reshape(HELD, 1, LANES)
        tri_keys = res_mask.astype(F32).reshape(RES, 1)
        norm = jnp.dot(mask_f.T, col_keys)

        def bias(z_blk, w, form, axis):
            part = jnp.einsum(form, layer_norm(z_blk), w, preferred_element_type=F32).astype(BF16)
            return lax.all_gather(part, 'dap', axis=axis, tiled=True)

        def by_key(w):
            return jnp.repeat(w.T, HELD, axis=0)

        def by_query(w):
            return jnp.repeat(w, RES, axis=1)

        row_bias = bias(z, w_row_bias[0], 'ijc,ch->hji', 2)
        row_bias = jnp.concatenate([row_bias, row_bias], axis=2)
        m = row_attention(m, row_keys, row_bias, w_row_in[0], w_row_out[0], HELD, 24, True)
        m = lax.all_to_all(m, 'dap', 1, 0, tiled=True)
        m = jnp.transpose(m, (1, 0, 2))
        m, pairs, singles = column_pair(m, col_keys, lanes, w_col_in, w_col_out, w_opm_in)
        m = lax.all_to_all(jnp.transpose(m, (1, 0, 2)), 'dap', 0, 1, tiled=True)
        z, row_bias = pair_block(
            0, pairs[0, 0], singles[0, 1], z, norm, tri_keys,
            (w_opm_1, by_query(w_ts_bias[0]), w_ts_in[0], w_ts_out[0], by_key(w_te_bias[0]), w_te_in[0], w_te_out[0]),
            by_key(w_row_bias[1]))

        z, = pair_block(
            1, pairs[1, 1], singles[1, 0], z, norm, tri_keys,
            (w_opm_2, by_query(w_te_bias[1]), w_te_in[1], w_te_out[1], by_key(w_ts_bias[1]), w_ts_in[1], w_ts_out[1]),
            None)
        m = row_attention(m, row_keys, row_bias, w_row_in[1], w_row_out[1], HELD, 24, True)
        return m, z

    in_specs = (P(('data', 'dap')), P(('data', 'dap')), P('data'), P('data')) + (P(),) * 13
    out_specs = (P(('data', 'dap')), P(('data', 'dap')))
    return jax.shard_map(local_step, mesh=mesh, in_specs=in_specs, out_specs=out_specs, check_vma=False)
```

time: 242 us -> 208 us (0.86)
  blocking collectives: 63.8 us -> 7.48 us
  Pallas kernels: 101 us -> 146 us
  other arithmetic: 16.7 us -> 5.23 us
  starting transfers between devices: 14.3 us -> 7.45 us
  matrix products: 6.45 us -> 2.13 us
    pallas_call x2, Pallas kernels: 11.1 us -> 75.4 us  [pair_block(): pl.pallas_call(functools.partial(pair_kernel, has_next), out_shape=out_sh...]
    all_gather x6 -> x1, blocking collectives: 49.3 us -> 7.48 us  [bias(): return lax.all_gather(part, 'dap', axis=axis, tiled=True)]
    pallas_call x6 -> x2, Pallas kernels: 52.4 us -> 32.6 us  [row_attention(): pl.pallas_call(functools.partial(row_kernel, heads, dim, per_row, groups...]
    all_gather x2 -> x0, blocking collectives: 14.5 us -> none  [gather_full(): lax.all_gather(half.reshape(8, 32, 2, 128).transpose(0, 2, 1, 3).reshape(...]
    all_to_all x2 -> x0, starting transfers between devices: 6.81 us -> none  [the longest x1 3.41 us: local_step(): z = lax.all_to_all(jnp.transpose(z, (1, 0, 2)), 'dap', 0, 1, tiled=True)]
    concatenate x6 -> x0, other arithmetic: 5.03 us -> none  [row_attention(): bias_t = jnp.concatenate([bias_t, bias_t], axis=2)]
    dot_general x6 -> x1, matrix products: 5.72 us -> 1.41 us  [bias(): jnp.einsum(form, layer_norm(z_blk), w, preferred_element_type=F32)]
    reduce_sum x6 -> x1, other arithmetic: 5.07 us -> 1.16 us  [layer_norm(): row_mean = jnp.mean(flat, axis=-1, keepdims=True)]
  transfers between devices with their start and end apart: 4 -> 2, of which waited for: 1 -> 1; matrix products, arithmetic and copies ran while one was open for 6% -> 5% of each run, Pallas kernels for 2% -> 36%
where the time goes in v4:
time: 208 us; the launch traced here: 207 us
  Pallas kernels  146 us (70%)
  local copies, waits for them, and re-layouts  27 us (13%)
  waiting for transfers between devices  11.3 us (5%)
  blocking collectives  7.48 us (4%)
  starting transfers between devices  7.45 us (4%)
  other arithmetic  5.23 us (3%)
  matrix products  2.13 us (1%)
    pallas_call x2, Pallas kernels, pair_block(): pl.pallas_call(functools.partial(pair_kernel, has_next), out_shape=out_sh...  75.4 us
    pallas_call x1, Pallas kernels, column_pair(): pl.pallas_call(col_kernel, out_shape=[jax.ShapeDtypeStruct(x.shape, BF16)...  37.6 us
    pallas_call x2, Pallas kernels, row_attention(): pl.pallas_call(functools.partial(row_kernel, heads, dim, per_row, groups...  32.6 us
    all_to_all x1, waiting for transfers between devices, local_step(): m = lax.all_to_all(m, 'dap', 1, 0, tiled=True)  11.3 us
    all_gather x1, blocking collectives, bias(): return lax.all_gather(part, 'dap', axis=axis, tiled=True)  7.48 us
  transfers between devices with their start and end apart: 2, of which 1 were waited for; matrix products, arithmetic and copies ran while one was open for 5% of the time, Pallas kernels for 36%

profile of v4, /device:TPU:0, one launch (start us, length us, event | category | flops | bytes accessed | tf_op | source)
XLA Modules:
  0.0 207.1 jit_solution(11587626294107645418)
XLA Ops:
  0.6 0.9 convert_element_type.24
  1.6 1.2 convert_reduce_fusion
  2.7 1.3 fusion.3
  4.1 1.4 fusion
  5.5 7.5 %all_gather.3 = bf16[16,64,64]{1,0,2:T(8,128)(2,1)S(1)} all-gather(bf16[16,64,16]{1,0,2:T(8,128)(2,1)S(1)} %fusion), channel_id=1, replica_groups=mesh['data'=4,'dap'=4] {'dap'}, dimensions={2}, use_global_device_ids=true | all-gather | bytes 163840 | tf_op jit(solution)/shard_map/all_gather | solution.py:446
  13.0 0.3 copy.44
  13.3 1.0 convert_multiply_fusion.1.bias_ref
  14.2 1.7 fusion.11
  15.9 0.9 fusion.12
  16.8 0.7 dynamic-slice_bitcast_fusion.keys_ref
  17.5 16.3 %row_att.2 = bf16[32,64,384]{2,1,0:T(8,128)(2,1)} custom-call(bf16[32,64,384]{2,1,0:T(8,128)(2,1)} %x_ref.1, f32[64,32]{1,0:T(8,128)} %dynamic-slice_bitcast_fusion.keys_ref, f32[16,64,128]{2,1,0:T(8,128)} %convert_multiply_fusion.1.bias_ref, bf16[1536,384]{1,0:T(8,128)(2,1)} %bitcast.97, bf16[384,384]{1,0:T(8,128)(2,1)} %bitcast.101), custom_call_target="tpu_custom_call" | custom-call | flops 3019898880 | bytes 3145728 | tf_op jit(solution)/shard_map/row_att/pallas_call | solution.py:176
  33.8 3.5 %copy.46 = bf16[32,64,384]{2,0,1:T(8,128)(2,1)} copy(bf16[32,64,384]{2,1,0:T(8,128)(2,1)} %row_att.2) | data formatting | bytes 3145728 | tf_op jit(solution)/shard_map/row_att/pallas_call | solution.py:176
  37.3 0.0 copy-start.13
  37.3 3.7 %all-to-all-start = ((bf16[32,64,384]{2,0,1:T(8,128)(2,1)}), bf16[32,64,384]{2,0,1:T(8,128)(2,1)S(1)}, u32[]{:S(2)}, u32[]{:S(2)}) async-start(bf16[32,64,384]{2,0,1:T(8,128)(2,1)} %copy.46), calls=%async_computation | async-start | bytes 3145728 | tf_op jit(solution)/shard_map/all_to_all | solution.py:457
  41.1 0.0 copy-start.7
  41.1 0.0 copy-start.9
  41.1 0.0 copy-start.10
  41.1 0.0 copy-start.4
  41.2 0.0 copy-start.5
  41.3 0.7 copy.48.keys_ref
  42.0 0.1 copy.61
  42.1 0.9 copy.55.wm_ref
  43.0 0.7 copy.56.wba_ref
  43.7 0.7 copy.54.keys_ref
  44.4 0.9 copy.58.wm_ref
  45.3 0.8 copy.59.wba_ref
  46.1 0.7 convolution_bitcast_fusion.norm_ref
  46.8 0.6 fusion.16
  47.4 0.6 fusion.17
  48.1 0.8 fusion.14
  48.8 0.7 fusion.15
  49.6 11.3 %all-to-all-done = bf16[32,64,384]{2,0,1:T(8,128)(2,1)S(1)} async-done(((bf16[32,64,384]{2,0,1:T(8,128)(2,1)}), bf16[32,64,384]{2,0,1:T(8,128)(2,1)S(1)}, u32[]{:S(2)}, u32[]{:S(2)}) %all-to-all-start) | async-done | bytes 1572896 | tf_op jit(solution)/shard_map/all_to_all | solution.py:457
  60.9 1.4 copy.47
  62.3 37.6 %col_att.1 = (bf16[16,128,384]{2,1,0:T(8,128)(2,1)}, bf16[2,2,8,32,256]{4,3,2,1,0:T(8,128)(2,1)}, bf16[2,2,16,32,128]{4,3,2,1,0:T(8,128)(2,1)}) custom-call(bf16[16,128,384]{2,1,0:T(8,128)(2,1)} %bitcast.95, f32[128,16]{1,0:T(8,128)} %copy.48.keys_ref, f32[16,1,128]{2,1,0:T(1,128)} %bitcast.110, bf16[2,1536,384]{2,1,0:T(8,128)(2,1)} %bitcast.118, ...), custom_call_target="tpu_custom_call" | custom-call | flops 6039797760 | bytes 3145728 | tf_op jit(solution)/shard_map/col_att/pallas_call | solution.py:218
  99.9 1.7 slice_bitcast_fusion
  101.6 1.7 slice_bitcast_fusion.1
  103.3 3.5 %copy.50 = bf16[128,16,384]{2,1,0:T(8,128)(2,1)} copy(bf16[128,16,384]{2,0,1:T(8,128)(2,1)} %bitcast.93) | data formatting | bytes 3145728 | tf_op jit(solution)/shard_map/transpose | solution.py:460
  106.7 3.7 %all-to-all-start.1 = ((bf16[128,16,384]{2,1,0:T(8,128)(2,1)}), bf16[128,16,384]{2,1,0:T(8,128)(2,1)S(1)}, u32[]{:S(2)}, u32[]{:S(2)}) async-start(bf16[128,16,384]{2,1,0:T(8,128)(2,1)} %copy.50), calls=%async_computation.1 | async-start | bytes 3145728 | tf_op jit(solution)/shard_map/all_to_all | solution.py:460
  110.5 0.6 broadcast_in_dim.18
  111.1 0.6 broadcast_in_dim.19
  111.7 46.6 %pair_block.2 = (bf16[16,64,128]{2,1,0:T(8,128)(2,1)}, bf16[16,64,128]{2,1,0:T(8,128)(2,1)}) custom-call(bf16[8,32,256]{2,1,0:T(8,128)(2,1)} %get-tuple-element.21.own_ref, bf16[16,32,128]{2,1,0:T(8,128)(2,1)} %get-tuple-element.19.part_ref, bf16[16,64,128]{2,1,0:T(8,128)(2,1)} %z_ref.1, f32[64,16]{1,0:T(8,128)} %convolution_bitcast_fusion.norm_ref, ...), custom_call_target="tpu_custom_call" | custom-call | flops 10000000000 | bytes 4194304 | tf_op jit(solution)/shard_map/pair_block/pallas_call | solution.py:398
  158.3 0.6 broadcast_in_dim.21
  158.9 28.8 %pair_block.3 = bf16[16,64,128]{2,1,0:T(8,128)(2,1)} custom-call(bf16[8,32,256]{2,1,0:T(8,128)(2,1)} %get-tuple-element.20.own_ref, bf16[16,32,128]{2,1,0:T(8,128)(2,1)} %get-tuple-element.18.part_ref, bf16[16,64,128]{2,1,0:T(8,128)(2,1)} %get-tuple-element.11.z_ref, f32[64,16]{1,0:T(8,128)} %convolution_bitcast_fusion.norm_ref, f32[64,1]{1,0:T(8,128)} %copy.54.keys_ref, ...), custom_call_target="tpu_custom_call" | custom-call | flops 10000000000 | bytes 4194304 | tf_op jit(solution)/shard_map/pair_block/pallas_call | solution.py:398
  187.7 0.9 convert_multiply_fusion.bias_ref
  188.6 0.0 all-to-all-done.1
  188.6 1.5 copy.51
  190.0 16.3 %row_att.3 = bf16[32,64,384]{2,1,0:T(8,128)(2,1)} custom-call(bf16[32,64,384]{2,1,0:T(8,128)(2,1)} %bitcast.94, f32[64,32]{1,0:T(8,128)} %dynamic-slice_bitcast_fusion.keys_ref, f32[16,64,128]{2,1,0:T(8,128)} %convert_multiply_fusion.bias_ref, bf16[1536,384]{1,0:T(8,128)(2,1)} %bitcast.96, bf16[384,384]{1,0:T(8,128)(2,1)} %bitcast.100), custom_call_target="tpu_custom_call" | custom-call | flops 3019898880 | bytes 3145728 | tf_op jit(solution)/shard_map/row_att/pallas_call | solution.py:176
  206.4 0.7 copy.63
  (34 shorter events, 0.1 us)
Async XLA Ops:
  0.6 13.6 %copy-start = (bf16[2,384,4,16,24]{1,4,3,2,0:T(8,128)(2,1)S(1)}, bf16[2,384,4,16,24]{1,4,3,2,0:T(8,128)(2,1)}, u32[]{:S(2)}) copy-start(bf16[2,384,4,16,24]{1,4,3,2,0:T(8,128)(2,1)} %param.22) | copy-start | bytes 7077892
  14.2 1.7 copy-start.1
  37.3 3.7 %copy-start.11 = (bf16[2,128,16]{1,2,0:T(8,128)(2,1)S(1)}, bf16[2,128,16]{1,2,0:T(8,128)(2,1)}, u32[]{:S(2)}) copy-start(bf16[2,128,16]{1,2,0:T(8,128)(2,1)} %param.21) | copy-start | bytes 24580
  37.3 3.8 %copy-start.2 = (bf16[2,32,32,128]{3,2,1,0:T(8,128)(2,1)S(1)}, bf16[2,32,32,128]{3,2,1,0:T(8,128)(2,1)}, u32[]{:S(2)}) copy-start(bf16[2,32,32,128]{3,2,1,0:T(8,128)(2,1)} %param.27) | copy-start | bytes 1572868
  37.3 3.9 %copy-start.12 = (bf16[2,128,4]{1,2,0:T(4,128)(2,1)S(1)}, bf16[2,128,4]{1,2,0:T(4,128)(2,1)}, u32[]{:S(2)}) copy-start(bf16[2,128,4]{1,2,0:T(4,128)(2,1)} %param.28) | copy-start | bytes 6148
  37.3 3.9 %copy-start.14 = (s32[64]{0:T(128)S(1)}, s32[64]{0:T(128)}, u32[]{:S(2)}) copy-start(s32[64]{0:T(128)} %param.20) | copy-start | bytes 772
  37.3 3.9 %copy-start.13 = (bf16[2,128,4]{1,2,0:T(4,128)(2,1)S(1)}, bf16[2,128,4]{1,2,0:T(4,128)(2,1)}, u32[]{:S(2)}) copy-start(bf16[2,128,4]{1,2,0:T(4,128)(2,1)} %param.31) | copy-start | bytes 6148
  37.3 23.5 %all-to-all-start = ((bf16[32,64,384]{2,0,1:T(8,128)(2,1)}), bf16[32,64,384]{2,0,1:T(8,128)(2,1)S(1)}, u32[]{:S(2)}, u32[]{:S(2)}) async-start(bf16[32,64,384]{2,0,1:T(8,128)(2,1)} %copy.46), calls=%async_computation | async-start | bytes 3145728 | tf_op jit(solution)/shard_map/all_to_all | solution.py:457
  41.1 5.0 %copy-start.7 = (s32[128,64]{0,1:T(8,128)S(1)}, s32[128,64]{0,1:T(8,128)}, u32[]{:S(2)}) copy-start(s32[128,64]{0,1:T(8,128)} %param.19) | copy-start | bytes 98308
  41.1 5.7 %copy-start.9 = (bf16[2,4,32,128]{3,2,1,0:T(8,128)(2,1)S(1)}, bf16[2,4,32,128]{3,2,1,0:T(8,128)(2,1)}, u32[]{:S(2)}) copy-start(bf16[2,4,32,128]{3,2,1,0:T(8,128)(2,1)} %param.30) | copy-start | bytes 196612
  41.1 6.3 %copy-start.10 = (bf16[2,4,32,128]{3,2,1,0:T(8,128)(2,1)S(1)}, bf16[2,4,32,128]{3,2,1,0:T(8,128)(2,1)}, u32[]{:S(2)}) copy-start(bf16[2,4,32,128]{3,2,1,0:T(8,128)(2,1)} %param.33) | copy-start | bytes 196612
  41.1 7.0 %copy-start.4 = (bf16[2,128,4,4,32]{1,4,3,2,0:T(8,128)(2,1)S(1)}, bf16[2,128,4,4,32]{1,4,3,2,0:T(8,128)(2,1)}, u32[]{:S(2)}) copy-start(bf16[2,128,4,4,32]{1,4,3,2,0:T(8,128)(2,1)} %param.29) | copy-start | bytes 786436
  41.2 7.7 %copy-start.5 = (bf16[2,128,4,4,32]{1,4,3,2,0:T(8,128)(2,1)S(1)}, bf16[2,128,4,4,32]{1,4,3,2,0:T(8,128)(2,1)}, u32[]{:S(2)}) copy-start(bf16[2,128,4,4,32]{1,4,3,2,0:T(8,128)(2,1)} %param.32) | copy-start | bytes 786436
  41.3 8.3 %copy-start.8 = (f32[128,16]{0,1:T(8,128)}, f32[128,16]{0,1:T(8,128)S(1)}, u32[]{:S(2)}) copy-start(f32[128,16]{0,1:T(8,128)S(1)} %constant_dynamic-slice_fusion) | copy-start | bytes 24580
  106.7 81.8 %all-to-all-start.1 = ((bf16[128,16,384]{2,1,0:T(8,128)(2,1)}), bf16[128,16,384]{2,1,0:T(8,128)(2,1)S(1)}, u32[]{:S(2)}, u32[]{:S(2)}) async-start(bf16[128,16,384]{2,1,0:T(8,128)(2,1)} %copy.50), calls=%async_computation.1 | async-start | bytes 3145728 | tf_op jit(solution)/shard_map/all_to_all | solution.py:460
  158.9 28.8 %copy-start.3 = (bf16[16,64,128]{2,1,0:T(8,128)(2,1)S(1)}, bf16[16,64,128]{2,1,0:T(8,128)(2,1)}, u32[]{:S(2)}) copy-start(bf16[16,64,128]{2,1,0:T(8,128)(2,1)} %get-tuple-element.10) | copy-start | bytes 786436
  190.0 16.3 %copy-start.6 = (bf16[16,64,128]{2,1,0:T(8,128)(2,1)S(1)}, bf16[16,64,128]{2,1,0:T(8,128)(2,1)}, u32[]{:S(2)}) copy-start(bf16[16,64,128]{2,1,0:T(8,128)(2,1)} %pair_block.3) | copy-start | bytes 786436

commit v5 on v4

v5 whole, which is shorter than its diff:
```python
import functools

import jax
import jax.numpy as jnp
from jax import lax
from jax.experimental import pallas as pl
from jax.experimental.pallas import tpu as pltpu
from jax.sharding import PartitionSpec as P

LOG2E = 1.4426950408889634
NEG = -1e9 * LOG2E
F32 = jnp.float32
BF16 = jnp.bfloat16
LAG = 2
SLOTS = 4
NT = (((1,), (1,)), ((), ()))
LANES = 128
RES = 64
BLOCK = 256
HELD = 16
WIDE = 384
CELLS = 1024


def layer_norm(values):
    flat = values.astype(F32)
    row_mean = jnp.mean(flat, axis=-1, keepdims=True)
    centered = flat - row_mean
    row_var = jnp.mean(centered * centered, axis=-1, keepdims=True)
    return (centered * lax.rsqrt(row_var + 1e-5)).astype(BF16)


def half_masks(rows, split):
    index = lax.broadcasted_iota(jnp.int32, (rows, LANES), 0)
    upper = (index < split).astype(F32).astype(BF16)
    lower = (index >= split).astype(F32).astype(BF16)
    return upper, lower


def attend_units(pt_ref, gt_ref, kt_ref, lg_ref, pr_ref, heads, dim, keep, bias_ref, work):
    width = heads * dim
    rows = 2 * dim
    pairs = heads // 2
    units = 2 * pairs
    up, low = half_masks(rows, dim)
    scale = dim ** -0.5 * LOG2E
    if bias_ref is not None:
        left = lax.broadcasted_iota(jnp.int32, (RES, LANES), 1) < RES
        left_b = left.astype(F32).astype(BF16)
        right_b = (1.0 - left.astype(F32)).astype(BF16)

    def place(unit):
        return pl.ds(unit // pairs * LANES, LANES), rows * (unit % pairs)

    def turn_keys(unit):
        ln, r = place(unit)
        kt_ref[unit % SLOTS] = pt_ref[pl.ds(width + r, rows), ln].T

    def make_logits(unit):
        ln, r = place(unit)
        q = pt_ref[pl.ds(r, rows), ln]
        rhs = jnp.concatenate([q * up, q * low], axis=1)
        logits2 = jnp.dot(kt_ref[unit % SLOTS], rhs, preferred_element_type=F32)
        for half in range(2):
            lg = logits2[:, LANES * half:LANES * half + LANES]
            if bias_ref is not None:
                lg = jnp.where(left, lg[0:RES], lg[RES:LANES])
            lg_ref[unit % SLOTS, half] = lg

    def soften(unit):
        blk, hp = unit // pairs, unit % pairs
        for half in range(2):
            lg = lg_ref[unit % SLOTS, half] * scale
            if bias_ref is not None:
                lg = lg + bias_ref[2 * hp + half]
            lg = jnp.where(keep[blk], lg, NEG)
            e = jnp.exp2(lg - jnp.max(lg, axis=0, keepdims=True))
            p = (e * (1.0 / jnp.sum(e, axis=0, keepdims=True))).astype(BF16)
            pr_ref[unit % SLOTS, half] = p

    def mix(unit):
        ln, r = place(unit)
        v = pt_ref[pl.ds(2 * width + r, rows), ln]
        g = pt_ref[pl.ds(3 * width + r, rows), ln]
        probs = []
        for half in range(2):
            p = pr_ref[unit % SLOTS, half]
            probs += [p] if bias_ref is None else [p * left_b, p * right_b]
        att = jnp.dot(jnp.concatenate([v * up, v * low], axis=1), jnp.concatenate(probs, axis=0), preferred_element_type=F32)
        gt_ref[pl.ds(r, rows), ln] = (att * jax.nn.sigmoid(g.astype(F32))).astype(BF16)

    stages = ((turn_keys, 0), (make_logits, LAG), (soften, 2 * LAG), (mix, 3 * LAG))
    ticks = units + 3 * LAG
    for tick in range(ticks):
        for stage, lag in stages:
            if 0 <= tick - lag < units:
                stage(tick - lag)
        for job in work[len(work) * tick // ticks:len(work) * (tick + 1) // ticks]:
            job()


def project(ln_ref, pt_ref, w):
    rows = pt_ref.shape[0]
    chunk = BLOCK if rows > CELLS else LANES

    def job(part):
        sl = pl.ds(part * chunk, chunk)
        pt_ref[sl, :] = lax.dot_general(w(sl), ln_ref[...], NT, preferred_element_type=F32).astype(BF16)
    return [functools.partial(job, part) for part in range(rows // chunk)]


def leave(gt_ref, x_old, wo):
    return (x_old + jnp.dot(gt_ref[...].T, wo, preferred_element_type=F32)).astype(BF16)


def attend_blocks(blocks, scratch, read, w_in, w_out, keep, bias_ref, finish, ready, aside):
    ln_ref, pt_refs, gt_refs, others = scratch[0], scratch[1:3], scratch[3:5], scratch[5:8]
    ln_ref[...] = layer_norm(read(0))
    for job in project(ln_ref, pt_refs[0], w_in(0)):
        job()
    ready()

    def body(turn, carry):
        for half in (1, 0):
            i = 2 * turn + 2 - half
            new = jnp.minimum(i, blocks - 1)
            old = jnp.maximum(i - 2, 0)
            aside(i)

            def norm():
                ln_ref[...] = layer_norm(read(new))

            def done():
                finish(old, leave(gt_refs[half], read(old), w_out(old)))

            work = [norm, done] + project(ln_ref, pt_refs[half], w_in(new))
            attend_units(pt_refs[1 - half], gt_refs[1 - half], *others, 16, 24, keep(i - 1), bias_ref, work)
        return carry

    lax.fori_loop(0, blocks // 2, body, 0)
    finish(blocks - 1, leave(gt_refs[1], read(blocks - 1), w_out(blocks - 1)))


def attend_scratch(heads, dim, keys, channels):
    inner = heads * dim
    return [
        pltpu.VMEM((BLOCK, channels), BF16),
        pltpu.VMEM((4 * inner, BLOCK), BF16),
        pltpu.VMEM((4 * inner, BLOCK), BF16),
        pltpu.VMEM((inner, BLOCK), BF16),
        pltpu.VMEM((inner, BLOCK), BF16),
        pltpu.VMEM((SLOTS, LANES, 2 * dim), BF16),
        pltpu.VMEM((SLOTS, 2, keys, LANES), F32),
        pltpu.VMEM((SLOTS, 2, keys, LANES), BF16),
    ]


def pick_column(table, col):
    lane = lax.broadcasted_iota(jnp.int32, table.shape, 1)
    return jnp.sum(jnp.where(lane == col, table, 0.0), axis=1, keepdims=True)


def row_keep(mask_ref, seq):
    left = lax.broadcasted_iota(jnp.int32, (RES, LANES), 1) < RES
    table = mask_ref[...].astype(F32)
    column = [pick_column(table, seq + n) for n in range(4)]
    return [jnp.where(left, column[2 * blk], column[2 * blk + 1]) > 0.5 for blk in range(2)]


def row_first_kernel(x_ref, z_ref, mask_ref, wb_ref, w_ref, wo_ref, out_ref, mo_ref, lnz_ref, nl_ref, rows_ref, bias_ref,
                     send_sem, recv_sem, *scratch):
    me = lax.axis_index('dap')
    mine = pl.ds(pl.multiple_of(HELD * me, HELD), HELD)
    for part in range(4):
        lnz_ref[pl.ds(BLOCK * part, BLOCK), :] = layer_norm(z_ref[pl.ds(4 * part, 4)].reshape(BLOCK, LANES))
    nl_ref[...] = local_bias_rows(lnz_ref, wb_ref[...]).reshape(HELD, HELD, LANES)
    greet(me)
    copies = push(me, 8, send_sem, recv_sem, lambda peer: nl_ref, rows_ref.at[:, mine, :])
    rows_ref[:, mine, :] = nl_ref[...]

    def ready():
        finish_all(copies)
        bias_by_query(rows_ref, bias_ref)

    def emit(block):
        seqs = pl.ds(4 * block, 4)
        target = pl.ds(32 * me + 4 * block, 4)
        push(me, block, send_sem, recv_sem,
             lambda peer: mo_ref.at[seqs, pl.ds(pl.multiple_of(HELD * peer, HELD), HELD), :], out_ref.at[target])
        out_ref[target] = mo_ref[seqs, mine, :]

    def aside(i):
        @pl.when(i >= 3)
        def _():
            emit(i - 3)

    def finish(block, out):
        mo_ref[pl.ds(4 * block, 4)] = out.reshape(4, RES, WIDE)

    attend_blocks(8, scratch, lambda at: x_ref[pl.ds(at * 4, 4)].astype(F32).reshape(BLOCK, WIDE),
                  lambda at: lambda sl: w_ref[sl, :], lambda at: wo_ref[...],
                  lambda at: row_keep(mask_ref, 32 * me + 4 * at), bias_ref, finish, ready, aside)
    emit(6)
    emit(7)

    def drain(block, carry):
        seqs = pl.ds(4 * block, 4)
        for o in range(1, 4):
            peer = lax.rem(me + o, 4)
            pltpu.make_async_remote_copy(
                src_ref=mo_ref.at[seqs, pl.ds(pl.multiple_of(HELD * peer, HELD), HELD), :],
                dst_ref=out_ref.at[pl.ds(32 * me + 4 * block, 4)], send_sem=send_sem.at[3 * block + o - 1],
                recv_sem=recv_sem.at[3 * block + o - 1], device_id={'dap': peer},
                device_id_type=pl.DeviceIdType.MESH).wait()
        return carry

    lax.fori_loop(0, 8, drain, 0)


def bias_by_query(rows_ref, bias_ref):
    for head in range(rows_ref.shape[0]):
        turned = (rows_ref[head].astype(F32) * LOG2E).T[:RES]
        bias_ref[head] = jnp.concatenate([turned, turned], axis=1)


VMEM = pl.BlockSpec(memory_space=pltpu.VMEM)


def of_layer(array, layer):
    rank = array.ndim - 1
    return pl.BlockSpec((None,) + array.shape[1:], lambda i: (layer,) + (0,) * rank)


def whole(array):
    return pl.BlockSpec(array.shape, lambda i: (0,) * array.ndim)


def row_first(x, z, mask, wb, w, wo):
    return pl.pallas_call(
        row_first_kernel,
        grid=(1,),
        in_specs=[whole(x), whole(z), whole(mask)] + [of_layer(a, 0) for a in (wb, w, wo)],
        out_specs=VMEM,
        out_shape=jax.ShapeDtypeStruct((LANES, HELD, WIDE), BF16),
        scratch_shapes=[
            pltpu.VMEM((32, RES, WIDE), BF16),
            pltpu.VMEM((CELLS, LANES), BF16),
            pltpu.VMEM((HELD, HELD, LANES), BF16),
            pltpu.VMEM((HELD, RES, LANES), BF16),
            pltpu.VMEM((HELD, RES, LANES), F32),
            pltpu.SemaphoreType.DMA((27,)),
            pltpu.SemaphoreType.DMA((27,)),
        ] + attend_scratch(HELD, 24, RES, WIDE),
        compiler_params=pltpu.CompilerParams(collective_id=0, has_side_effects=True),
        cost_estimate=pl.CostEstimate(flops=10 ** 10, bytes_accessed=2 ** 22, transcendentals=0),
        name="row_first",
    )(x, z, mask, wb, w, wo)


def row_last_kernel(x_ref, rows_ref, mask_ref, w_ref, wo_ref, out_ref, wide_ref, m_ref, bias_ref, *scratch):
    me = lax.axis_index('dap')
    turn_tokens(x_ref, wide_ref, m_ref)
    bias_ref[...] = rows_ref[...].astype(F32) * LOG2E

    def finish(block, out):
        out_ref[pl.ds(4 * block, 4)] = out.reshape(4, RES, WIDE)

    attend_blocks(8, scratch, lambda at: m_ref[pl.ds(at * 4, 4)].astype(F32).reshape(BLOCK, WIDE),
                  lambda at: lambda sl: w_ref[sl, :], lambda at: wo_ref[...],
                  lambda at: row_keep(mask_ref, 32 * me + 4 * at), bias_ref, finish, lambda: None, lambda i: None)


def turn_tokens(x_ref, wide_ref, m_ref):
    outer, inner = x_ref.shape[:2]
    for part in range(3):
        lanes = pl.ds(LANES * part, LANES)
        wide_ref[part] = x_ref[:, :, lanes].astype(F32).reshape(outer * inner, LANES)

    def one(row, carry):
        for part in range(3):
            m_ref[row, :, pl.ds(LANES * part, LANES)] = wide_ref[part, pl.ds(row, outer, stride=inner), :].astype(BF16)
        return carry

    lax.fori_loop(0, inner, one, 0, unroll=2)


def row_last(x, rows, mask, w, wo):
    return pl.pallas_call(
        row_last_kernel,
        grid=(1,),
        in_specs=[whole(x), whole(rows), whole(mask)] + [of_layer(a, 1) for a in (w, wo)],
        out_specs=VMEM,
        out_shape=jax.ShapeDtypeStruct((32, RES, WIDE), BF16),
        scratch_shapes=[
            pltpu.VMEM((3, 2048, LANES), F32),
            pltpu.VMEM((32, RES, WIDE), BF16),
            pltpu.VMEM((HELD, RES, LANES), F32),
        ] + attend_scratch(HELD, 24, RES, WIDE),
        cost_estimate=pl.CostEstimate(flops=10 ** 10, bytes_accessed=2 ** 22, transcendentals=0),
        name="row_last",
    )(x, rows, mask, w, wo)


def col_kernel(x_ref, mask_ref, w_ref, wo_ref, wp_ref, out_ref, own1_ref, own2_ref, full1_ref, full2_ref,
               wide_ref, m_ref, part_ref, keys_ref, send_sem, recv_sem, *scratch):
    me = lax.axis_index('dap')
    greet(me)
    turn_tokens(x_ref, wide_ref, m_ref.at[0])
    mine = pl.ds(pl.multiple_of(HELD * me, HELD), HELD)
    keys_ref[...] = mask_ref[mine, :].astype(F32).T

    def keep(at):
        return [jnp.broadcast_to(pick_column(keys_ref[...], at % 8 * 2 + blk), (LANES, LANES)) > 0.5 for blk in range(2)]

    def finish(block, out):
        layer, pair = block // 8, block % 8
        m_ref[layer + 1, pl.ds(pair * 2, 2)] = out.reshape(2, LANES, WIDE)
        ac = lax.dot_general(wp_ref[layer], layer_norm(out), NT, preferred_element_type=F32)
        ac = (ac * jnp.concatenate([mask_ref[pl.ds(HELD * me + 2 * pair + blk, 1), :] for blk in range(2)], axis=1).astype(F32)).astype(BF16)
        parts = (ac[:32], ac[32:])
        own1_ref[pair] = jnp.where(layer == 0, parts[0].astype(F32), own1_ref[pair].astype(F32)).astype(BF16)
        own2_ref[pair] = parts[1]
        for blk in range(2):
            lanes = slice(LANES * blk, LANES * blk + LANES)
            part_ref[block, blk] = jnp.where(layer == 0, parts[1][:, lanes].astype(F32), parts[0][:, lanes].astype(F32)).astype(BF16)

    def part_copies(block, full_ref):
        target = full_ref.at[pl.ds(HELD * me + block % 8 * 2, 2)]
        return [pltpu.make_async_remote_copy(
            src_ref=part_ref.at[block], dst_ref=target, send_sem=send_sem.at[3 * block + o - 1],
            recv_sem=recv_sem.at[3 * block + o - 1], device_id={'dap': lax.rem(me + o, 4)},
            device_id_type=pl.DeviceIdType.MESH) for o in range(1, 4)]

    def seq_copies(pair):
        target = out_ref.at[pl.ds(HELD * me + 2 * pair, 2)]
        return [pltpu.make_async_remote_copy(
            src_ref=m_ref.at[2, pl.ds(2 * pair, 2), pl.ds(pl.multiple_of(32 * lax.rem(me + o, 4), 32), 32), :],
            dst_ref=target, send_sem=send_sem.at[48 + 3 * pair + o - 1], recv_sem=recv_sem.at[48 + 3 * pair + o - 1],
            device_id={'dap': lax.rem(me + o, 4)}, device_id_type=pl.DeviceIdType.MESH) for o in range(1, 4)]

    def emit_first(block):
        for copy in part_copies(block, full1_ref):
            copy.start()
        full1_ref[pl.ds(HELD * me + 2 * block, 2)] = part_ref[block]

    def emit_second(block):
        pair = block - 8
        for copy in part_copies(block, full2_ref) + seq_copies(pair):
            copy.start()
        full2_ref[pl.ds(HELD * me + 2 * pair, 2)] = part_ref[block]
        out_ref[pl.ds(HELD * me + 2 * pair, 2)] = m_ref[2, pl.ds(2 * pair, 2), pl.ds(pl.multiple_of(32 * me, 32), 32), :]

    def aside(i):
        @pl.when(jnp.logical_and(i >= 3, i < 11))
        def _():
            emit_first(i - 3)

        @pl.when(i >= 11)
        def _():
            emit_second(i - 3)

    attend_blocks(16, scratch, lambda at: m_ref[at // 8, pl.ds(at % 8 * 2, 2)].astype(F32).reshape(BLOCK, WIDE),
                  lambda at: lambda sl: w_ref[at // 8, sl, :], lambda at: wo_ref[at // 8],
                  keep, None, finish, lambda: None, aside)
    emit_second(14)
    emit_second(15)

    def drain(pair, carry):
        for copy in part_copies(pair, full1_ref) + part_copies(pair + 8, full2_ref) + seq_copies(pair):
            copy.wait()
        return carry

    lax.fori_loop(0, 8, drain, 0)


def column_pair(x, mask, w, wo, wp):
    return pl.pallas_call(
        col_kernel,
        in_specs=[VMEM] * 5,
        out_specs=[VMEM] * 5,
        out_shape=[
            jax.ShapeDtypeStruct((RES, 32, WIDE), BF16),
            jax.ShapeDtypeStruct((8, 32, BLOCK), BF16),
            jax.ShapeDtypeStruct((8, 32, BLOCK), BF16),
            jax.ShapeDtypeStruct((RES, 32, LANES), BF16),
            jax.ShapeDtypeStruct((RES, 32, LANES), BF16),
        ],
        scratch_shapes=[
            pltpu.VMEM((3, 2048, LANES), F32),
            pltpu.VMEM((3, HELD, LANES, WIDE), BF16),
            pltpu.VMEM((HELD, 2, 32, LANES), BF16),
            pltpu.VMEM((LANES, HELD), F32),
            pltpu.SemaphoreType.DMA((72,)),
            pltpu.SemaphoreType.DMA((72,)),
        ] + attend_scratch(HELD, 24, LANES, WIDE),
        compiler_params=pltpu.CompilerParams(collective_id=1, has_side_effects=True),
        cost_estimate=pl.CostEstimate(flops=10 ** 10, bytes_accessed=2 ** 22, transcendentals=0),
        name="col_pair",
    )(x, mask, w, wo, wp)


def greet(me):
    barrier = pltpu.get_barrier_semaphore()
    for o in range(1, 4):
        pl.semaphore_signal(barrier, inc=1, device_id={'dap': lax.rem(me + o, 4)}, device_id_type=pl.DeviceIdType.MESH)
    pl.semaphore_wait(barrier, 3)


def push(me, kind, send_sem, recv_sem, source, target):
    copies = []
    for o in range(1, 4):
        peer = lax.rem(me + o, 4)
        copy = pltpu.make_async_remote_copy(
            src_ref=source(peer), dst_ref=target, send_sem=send_sem.at[3 * kind + o - 1],
            recv_sem=recv_sem.at[3 * kind + o - 1], device_id={'dap': peer}, device_id_type=pl.DeviceIdType.MESH)
        copy.start()
        copies.append(copy)
    return copies


def finish_all(copies):
    for copy in copies:
        copy.wait()


def local_bias_rows(ln_ref, w):
    heads = w.shape[0]
    spread = jnp.concatenate([jnp.broadcast_to(w[head:head + 1], (HELD, LANES)) for head in range(heads)], axis=0)
    index = lax.broadcasted_iota(jnp.int32, spread.shape, 0) % HELD
    total = jnp.zeros(spread.shape, F32)
    for held in range(HELD):
        chosen = spread * (index == held).astype(F32).astype(BF16)
        part = ln_ref[pl.ds(RES * held, RES), :]
        total += lax.dot_general(chosen, jnp.concatenate([part, part], axis=0), NT, preferred_element_type=F32)
    return total.astype(BF16)


def triangle(zf_ref, ln_ref, w_ref, wo_ref, keep, bias_ref, pt_refs, gt_refs, others, ready):
    def project(block, part):
        def job():
            pt_refs[block % 2][pl.ds(LANES * part, LANES), :] = lax.dot_general(
                w_ref[pl.ds(LANES * part, LANES), :], ln_ref[pl.ds(BLOCK * block, BLOCK), :], NT,
                preferred_element_type=F32).astype(BF16)
        return job

    def leave(block):
        def job():
            update = jnp.dot(gt_refs[block % 2][...].T, wo_ref[...], preferred_element_type=F32)
            rows = pl.ds(BLOCK * block, BLOCK)
            zf_ref[rows, :] = (zf_ref[rows, :] + update).astype(BF16).astype(F32)
        return job

    for part in range(4):
        project(0, part)()
    ready()
    for block in range(4):
        work = [leave(block - 1)] if block else []
        if block < 3:
            work += [project(block + 1, part) for part in range(4)]
        attend_units(pt_refs[block % 2], gt_refs[block % 2], *others, 4, 32, [keep, keep], bias_ref, work)
    leave(3)()


def pair_kernel(has_next, own_ref, full_ref, z_ref, mask_ref, res_ref, wm_ref, wba_ref, wa_ref, woa_ref, wbb_ref, wb_ref, wob_ref, *rest):
    if has_next:
        wn_ref, out_ref, next_ref = rest[:3]
        rest = rest[3:]
    else:
        out_ref = rest[0]
        rest = rest[1:]
    (full32_ref, o_ref, wt_ref, zf_ref, zt_ref, ln_ref, bias_ref, la_ref, ra_ref, lb_ref, rb_ref, zs_ref, zr_ref, nl_ref,
     send_sem, recv_sem) = rest[:16]
    att = rest[16:]
    pt_refs, gt_refs, others = att[0:2], att[2:4], att[4:7]
    me = lax.axis_index('dap')
    mine = pl.ds(pl.multiple_of(HELD * me, HELD), HELD)
    greet(me)
    diagonal = lax.broadcasted_iota(jnp.int32, (RES, RES), 0) == lax.broadcasted_iota(jnp.int32, (RES, RES), 1)
    keys = jnp.sum(jnp.where(diagonal, jnp.broadcast_to(res_ref[...], (RES, RES)), 0).astype(F32), axis=1, keepdims=True)
    keep = jnp.broadcast_to(keys, (RES, LANES)) > 0.5
    mask = mask_ref[...].astype(F32).astype(BF16)
    norm = lax.dot_general(mask, mask_ref[mine, :].astype(F32).astype(BF16), NT, preferred_element_type=F32)

    full32_ref[:CELLS] = wm_ref[...].astype(F32).reshape(CELLS, LANES)
    if has_next:
        for q in range(32):
            wt_ref[pl.ds(32 * q, 32), :] = full32_ref[pl.ds(q, 32, stride=32), :].astype(BF16)
    else:
        wt_ref[...] = wm_ref[...].reshape(CELLS, LANES)
    w_turned = wt_ref[...].T
    full32_ref[...] = full_ref[...].astype(F32).reshape(2048, LANES)
    own = own_ref[...].reshape(BLOCK, BLOCK)
    zeros = jnp.zeros((RES, LANES), BF16)

    def one(q, carry):
        c_q = full32_ref[pl.ds(q, RES, stride=32), :].astype(BF16)
        rhs = jnp.concatenate([jnp.concatenate([c_q, zeros], axis=1), jnp.concatenate([zeros, c_q], axis=1)], axis=0)
        o = lax.dot_general(own, rhs, NT, preferred_element_type=F32).astype(BF16)
        for pair in range(8):
            o_ref[pair, pl.ds(pl.multiple_of(q * 32, 32), 32), :] = o[32 * pair:32 * pair + 32]
        return carry

    lax.fori_loop(0, 32, one, 0, unroll=4)
    for pair in range(8):
        update = jnp.dot(w_turned, o_ref[pair], preferred_element_type=F32).T
        z = z_ref[pl.ds(2 * pair, 2)].astype(F32).reshape(LANES, LANES)
        below = jnp.concatenate([pick_column(norm, 2 * pair), pick_column(norm, 2 * pair + 1)], axis=0)
        z = (z + update / (1e-3 + below)).astype(BF16).astype(F32)
        rows = pl.ds(LANES * pair, LANES)
        zf_ref[rows, :] = z
        ln_ref[rows, :] = layer_norm(z)

    la_ref[...] = local_bias_rows(ln_ref, wba_ref[...]).reshape(4, HELD, LANES)
    copies = push(me, 0, send_sem, recv_sem, lambda peer: la_ref, ra_ref.at[:, mine, :])
    ra_ref[:, mine, :] = la_ref[...]

    def queries_ready():
        finish_all(copies)
        bias_by_query(ra_ref, bias_ref)

    triangle(zf_ref, ln_ref, wa_ref, woa_ref, keep, bias_ref, pt_refs, gt_refs, others, queries_ready)

    zs_ref[...] = zf_ref[...].astype(BF16).reshape(HELD, RES, LANES)
    norm_all(zf_ref, ln_ref)
    moved = push(me, 1, send_sem, recv_sem, lambda peer: zs_ref.at[:, pl.ds(pl.multiple_of(HELD * peer, HELD), HELD), :], zr_ref.at[mine])
    zr_ref[mine] = zs_ref[:, mine, :]
    lb_ref[...] = local_bias_rows(ln_ref, wbb_ref[...]).reshape(4, HELD, LANES)
    copies_b = push(me, 2, send_sem, recv_sem, lambda peer: lb_ref, rb_ref.at[:, mine, :])
    rb_ref[:, mine, :] = lb_ref[...]
    finish_all(moved)
    zt_ref[...] = zr_ref[...].astype(F32).reshape(CELLS, LANES)
    for row in range(HELD):
        value = zt_ref[pl.ds(row, RES, stride=HELD), :]
        zf_ref[pl.ds(RES * row, RES), :] = value
        ln_ref[pl.ds(RES * row, RES), :] = layer_norm(value)

    def keys_ready():
        finish_all(copies_b)
        bias_ref[...] = rb_ref[...].astype(F32) * LOG2E

    triangle(zf_ref, ln_ref, wb_ref, wob_ref, keep, bias_ref, pt_refs, gt_refs, others, keys_ready)
    out_ref[...] = zf_ref[...].astype(BF16).reshape(HELD, RES, LANES)
    if has_next:
        norm_all(zf_ref, ln_ref)
        nl_ref[...] = local_bias_rows(ln_ref, wn_ref[...]).reshape(HELD, HELD, LANES)
        copies = push(me, 3, send_sem, recv_sem, lambda peer: nl_ref, next_ref.at[:, mine, :])
        next_ref[:, mine, :] = nl_ref[...]
        finish_all(copies)


def norm_all(zf_ref, ln_ref):
    for block in range(8):
        rows = pl.ds(LANES * block, LANES)
        ln_ref[rows, :] = layer_norm(zf_ref[rows, :])


def pair_block(ident, layer, own, full, z, mask, res_mask, weights, w_next):
    has_next = w_next is not None
    out_shape = [jax.ShapeDtypeStruct(z.shape, BF16)]
    picks = [of_layer(w, layer) for w in weights]
    if has_next:
        weights = weights + (w_next,)
        picks.append(of_layer(w_next, layer + 1))
        out_shape.append(jax.ShapeDtypeStruct((HELD, RES, LANES), BF16))
    args = (own, full, z, mask, res_mask)
    return pl.pallas_call(
        functools.partial(pair_kernel, has_next),
        grid=(1,),
        out_shape=out_shape,
        in_specs=[whole(a) for a in args] + picks,
        out_specs=[VMEM] * len(out_shape),
        scratch_shapes=[
            pltpu.VMEM((2048, LANES), F32),
            pltpu.VMEM((8, CELLS, LANES), BF16),
            pltpu.VMEM((CELLS, LANES), BF16),
            pltpu.VMEM((CELLS, LANES), F32),
            pltpu.VMEM((CELLS, LANES), F32),
            pltpu.VMEM((CELLS, LANES), BF16),
            pltpu.VMEM((4, RES, LANES), F32),
            pltpu.VMEM((4, HELD, LANES), BF16),
            pltpu.VMEM((4, RES, LANES), BF16),
            pltpu.VMEM((4, HELD, LANES), BF16),
            pltpu.VMEM((4, RES, LANES), BF16),
            pltpu.VMEM((HELD, RES, LANES), BF16),
            pltpu.VMEM((RES, HELD, LANES), BF16),
            pltpu.VMEM((HELD, HELD, LANES), BF16),
            pltpu.SemaphoreType.DMA((12,)),
            pltpu.SemaphoreType.DMA((12,)),
        ] + attend_scratch(4, 32, RES, LANES)[1:],
        compiler_params=pltpu.CompilerParams(collective_id=ident, has_side_effects=True),
        cost_estimate=pl.CostEstimate(flops=10 ** 10, bytes_accessed=2 ** 22, transcendentals=0),
        name="pair_block",
    )(*args, *weights)


def solution(mesh):
    def local_step(m, z, mask, res_mask, w_row_bias, w_row_in, w_row_out, w_col_in, w_col_out, w_opm_in, w_opm_out, w_ts_bias, w_ts_in, w_ts_out, w_te_bias, w_te_in, w_te_out):
        flat_in = lambda w: jnp.transpose(w, (0, 2, 3, 4, 1)).reshape(2, -1, w.shape[1])
        flat_out = lambda w: w.reshape(2, -1, w.shape[-1])
        flat_bias = lambda w: jnp.transpose(w, (0, 2, 1))
        w_row_in, w_col_in, w_ts_in, w_te_in = map(flat_in, (w_row_in, w_col_in, w_ts_in, w_te_in))
        w_row_out, w_col_out, w_ts_out, w_te_out = map(flat_out, (w_row_out, w_col_out, w_ts_out, w_te_out))
        w_row_bias, w_ts_bias, w_te_bias = map(flat_bias, (w_row_bias, w_ts_bias, w_te_bias))
        w_opm_in = jnp.transpose(w_opm_in, (0, 2, 3, 1)).reshape(2, RES, WIDE)
        w_opm_out = w_opm_out.reshape(2, CELLS, LANES)
        mask = mask.T
        res_mask = res_mask.reshape(1, RES)

        m = row_first(m, z, mask, w_row_bias, w_row_in, w_row_out)
        m, own1, own2, full1, full2 = column_pair(m, mask, w_col_in, w_col_out, w_opm_in)
        z, row_bias = pair_block(
            2, 0, own1, full1, z, mask, res_mask,
            (w_opm_out, w_ts_bias, w_ts_in, w_ts_out, w_te_bias, w_te_in, w_te_out), w_row_bias)
        z, = pair_block(
            3, 1, own2, full2, z, mask, res_mask,
            (w_opm_out, w_te_bias, w_te_in, w_te_out, w_ts_bias, w_ts_in, w_ts_out), None)
        m = row_last(m, row_bias, mask, w_row_in, w_row_out)
        return m, z

    in_specs = (P(('data', 'dap')), P(('data', 'dap')), P('data'), P('data')) + (P(),) * 13
    out_specs = (P(('data', 'dap')), P(('data', 'dap')))
    return jax.shard_map(local_step, mesh=mesh, in_specs=in_specs, out_specs=out_specs, check_vma=False)
```

time: 208 us -> 155 us (0.75)
  local copies, waits for them, and re-layouts: 27 us -> 0.71 us
  waiting for transfers between devices: 11.3 us -> 0 us
  blocking collectives: 7.48 us -> 0 us
  starting transfers between devices: 7.45 us -> 0 us
  Pallas kernels: 146 us -> 153 us
  other arithmetic: 5.23 us -> 0 us
  matrix products: 2.13 us -> 0 us
    all_to_all x2 -> x0, waiting for transfers between devices: 11.3 us -> none  [the longest x1 11.3 us: local_step(): m = lax.all_to_all(m, 'dap', 1, 0, tiled=True)]
    pallas_call x5, Pallas kernels: 146 us -> 153 us  [the longest x1 53 us: column_pair(): pl.pallas_call(col_kernel, in_specs=[VMEM] * 5, out_specs=[VMEM] * 5, out...]
    all_gather x1 -> x0, blocking collectives: 7.48 us -> none  [bias(): return lax.all_gather(part, 'dap', axis=axis, tiled=True)]
    all_to_all x2 -> x0, starting transfers between devices: 7.45 us -> none  [the longest x1 3.74 us: local_step(): m = lax.all_to_all(jnp.transpose(m, (1, 0, 2)), 'dap', 0, 1, tiled=True)]
    slice x7 -> x0, local copies, waits for them, and re-layouts: 5.39 us -> none  [the longest x1 1.7 us: local_step(): w_row_in[1]]
    transpose x4 -> x0, local copies, waits for them, and re-layouts: 4.17 us -> none  [the longest x1 3.47 us: local_step(): m = lax.all_to_all(jnp.transpose(m, (1, 0, 2)), 'dap', 0, 1, tiled=True)]
    reshape x5 -> x0, local copies, waits for them, and re-layouts: 3.93 us -> none  [the longest x2 1.5 us: by_query(): return jnp.repeat(w, RES, axis=1)]
    pallas_call x1 -> x0, local copies, waits for them, and re-layouts: 3.51 us -> none  [row_attention(): pl.pallas_call(functools.partial(row_kernel, heads, dim, per_row, groups...]
  transfers between devices with their start and end apart: 2 -> 0, of which waited for: 1 -> 0; matrix products, arithmetic and copies ran while one was open for 5% -> 0% of each run, Pallas kernels for 36% -> 0%
where the time goes in v5:
time: 155 us
  Pallas kernels  153 us (99%)
    pallas_call x1, Pallas kernels, column_pair(): pl.pallas_call(col_kernel, in_specs=[VMEM] * 5, out_specs=[VMEM] * 5, out...  53 us
    pallas_call x2, Pallas kernels, pair_block(): pl.pallas_call(functools.partial(pair_kernel, has_next), grid=(1,), out_s...  47.7 us
    pallas_call x1, Pallas kernels, row_first(): pl.pallas_call(row_first_kernel, grid=(1,), in_specs=[whole(x), whole(z),...  34 us
    pallas_call x1, Pallas kernels, row_last(): pl.pallas_call(row_last_kernel, grid=(1,), in_specs=[whole(x), whole(rows...  18.8 us

profile of v5, /device:TPU:0, one launch (start us, length us, event | category | flops | bytes accessed | tf_op | source)
XLA Modules:
  0.0 154.8 jit_solution(13252725472638658682)
XLA Ops:
  0.6 34.0 %row_first.1.x_ref = bf16[128,16,384]{2,1,0:T(8,128)(2,1)} custom-call(bf16[32,64,384]{2,1,0:T(8,128)(2,1)} %x_ref.1, bf16[16,64,128]{2,1,0:T(8,128)(2,1)} %z_ref.3, s32[64,128]{1,0:T(8,128)} %bitcast.42, bf16[2,16,128]{2,1,0:T(8,128)(2,1)} %bitcast.47, bf16[2,1536,384]{2,1,0:T(8,128)(2,1)} %bitcast.26, bf16[2,384,384]{2,1,0:T(8,128)(2,1)} %bitcast.29), custom_call_target="tpu_custom_call" | custom-call | flops 10000000000 | bytes 4194304 | tf_op jit(solution)/shard_map/row_first/pallas_call | solution.py:239
  34.6 53.0 %col_pair.1 = (bf16[64,32,384]{2,1,0:T(8,128)(2,1)}, bf16[8,32,256]{2,1,0:T(8,128)(2,1)}, bf16[8,32,256]{2,1,0:T(8,128)(2,1)}, bf16[64,32,128]{2,1,0:T(8,128)(2,1)}, bf16[64,32,128]{2,1,0:T(8,128)(2,1)}) custom-call(bf16[128,16,384]{2,1,0:T(8,128)(2,1)} %row_first.1.x_ref, s32[64,128]{1,0:T(8,128)} %bitcast.43, bf16[2,1536,384]{2,1,0:T(8,128)(2,1)} %bitcast.25, ...), custom_call_target="tpu_custom_call" | custom-call | flops 10000000000 | bytes 4194304 | tf_op jit(solution)/shard_map/col_pair/pallas_call | solution.py:377
  87.6 26.4 %pair_block.2 = (bf16[16,64,128]{2,1,0:T(8,128)(2,1)}, bf16[16,64,128]{2,1,0:T(8,128)(2,1)}) custom-call(bf16[8,32,256]{2,1,0:T(8,128)(2,1)} %get-tuple-element.10.own_ref, bf16[64,32,128]{2,1,0:T(8,128)(2,1)} %get-tuple-element.11.full_ref, bf16[16,64,128]{2,1,0:T(8,128)(2,1)} %z_ref.3, s32[64,128]{1,0:T(8,128)} %bitcast.44, s32[1,64]{1,0:T(1,128)} %bitcast.53, ...), custom_call_target="tpu_custom_call" | custom-call | flops 10000000000 | bytes 4194304 | tf_op jit(solution)/shard_map/pair_block/pallas_call | solution.py:566
  114.0 21.3 %pair_block.3 = bf16[16,64,128]{2,1,0:T(8,128)(2,1)} custom-call(bf16[8,32,256]{2,1,0:T(8,128)(2,1)} %get-tuple-element.13.own_ref, bf16[64,32,128]{2,1,0:T(8,128)(2,1)} %get-tuple-element.14.full_ref, bf16[16,64,128]{2,1,0:T(8,128)(2,1)} %get-tuple-element.15.z_ref, s32[64,128]{1,0:T(8,128)} %bitcast.45, s32[1,64]{1,0:T(1,128)} %bitcast.54, ...), custom_call_target="tpu_custom_call" | custom-call | flops 10000000000 | bytes 4194304 | tf_op jit(solution)/shard_map/pair_block/pallas_call | solution.py:566
  135.3 0.0 copy-start
  135.3 18.8 %row_last.1 = bf16[32,64,384]{2,1,0:T(8,128)(2,1)} custom-call(bf16[64,32,384]{2,1,0:T(8,128)(2,1)} %get-tuple-element.9.x_ref, bf16[16,64,128]{2,1,0:T(8,128)(2,1)} %get-tuple-element.12.rows_ref, s32[64,128]{1,0:T(8,128)} %bitcast.46, bf16[2,1536,384]{2,1,0:T(8,128)(2,1)} %bitcast.27, bf16[2,384,384]{2,1,0:T(8,128)(2,1)} %bitcast.30), custom_call_target="tpu_custom_call" | custom-call | flops 10000000000 | bytes 4194304 | tf_op jit(solution)/shard_map/row_last/pallas_call | solution.py:288
  154.1 0.0 copy-done
  154.1 0.7 copy.20
Async XLA Ops:
  135.3 18.8 %copy-start = (bf16[16,64,128]{2,1,0:T(8,128)(2,1)S(1)}, bf16[16,64,128]{2,1,0:T(8,128)(2,1)}, u32[]{:S(2)}) copy-start(bf16[16,64,128]{2,1,0:T(8,128)(2,1)} %pair_block.3) | copy-start | bytes 786436

commit v6 on v5

--- a/solution.py
+++ b/solution.py
@@ -125,7 +125,7 @@
             i = 2 * turn + 2 - half
             new = jnp.minimum(i, blocks - 1)
             old = jnp.maximum(i - 2, 0)
-            aside(i)
+            aside(i, half)
 
             def norm():
                 ln_ref[...] = layer_norm(read(new))
@@ -175,21 +175,25 @@
         lnz_ref[pl.ds(BLOCK * part, BLOCK), :] = layer_norm(z_ref[pl.ds(4 * part, 4)].reshape(BLOCK, LANES))
     nl_ref[...] = local_bias_rows(lnz_ref, wb_ref[...]).reshape(HELD, HELD, LANES)
     greet(me)
-    copies = push(me, 8, send_sem, recv_sem, lambda peer: nl_ref, rows_ref.at[:, mine, :])
+    copies = group_copies(me, 8, send_sem, recv_sem, lambda peer: nl_ref, rows_ref.at[:, mine, :])
+    start_all(copies)
     rows_ref[:, mine, :] = nl_ref[...]
 
     def ready():
         finish_all(copies)
         bias_by_query(rows_ref, bias_ref)
 
+    def moves(block):
+        return group_copies(
+            me, block, send_sem, recv_sem,
+            lambda peer: mo_ref.at[pl.ds(4 * block, 4), pl.ds(pl.multiple_of(HELD * peer, HELD), HELD), :],
+            out_ref.at[pl.ds(32 * me + 4 * block, 4)])
+
     def emit(block):
-        seqs = pl.ds(4 * block, 4)
-        target = pl.ds(32 * me + 4 * block, 4)
-        push(me, block, send_sem, recv_sem,
-             lambda peer: mo_ref.at[seqs, pl.ds(pl.multiple_of(HELD * peer, HELD), HELD), :], out_ref.at[target])
-        out_ref[target] = mo_ref[seqs, mine, :]
-
-    def aside(i):
+        start_all(moves(block))
+        out_ref[pl.ds(32 * me + 4 * block, 4)] = mo_ref[pl.ds(4 * block, 4), mine, :]
+
+    def aside(i, half):
         @pl.when(i >= 3)
         def _():
             emit(i - 3)
@@ -204,14 +208,7 @@
     emit(7)
 
     def drain(block, carry):
-        seqs = pl.ds(4 * block, 4)
-        for o in range(1, 4):
-            peer = lax.rem(me + o, 4)
-            pltpu.make_async_remote_copy(
-                src_ref=mo_ref.at[seqs, pl.ds(pl.multiple_of(HELD * peer, HELD), HELD), :],
-                dst_ref=out_ref.at[pl.ds(32 * me + 4 * block, 4)], send_sem=send_sem.at[3 * block + o - 1],
-                recv_sem=recv_sem.at[3 * block + o - 1], device_id={'dap': peer},
-                device_id_type=pl.DeviceIdType.MESH).wait()
+        finish_all(moves(block))
         return carry
 
     lax.fori_loop(0, 8, drain, 0)
@@ -257,17 +254,28 @@
     )(x, z, mask, wb, w, wo)
 
 
-def row_last_kernel(x_ref, rows_ref, mask_ref, w_ref, wo_ref, out_ref, wide_ref, m_ref, bias_ref, *scratch):
+def row_last_kernel(x_ref, rows_ref, own_ref, full_ref, z_ref, mask_ref, res_ref, w_ref, wo_ref, wm_ref, wba_ref, wa_ref, woa_ref,
+                    wbb_ref, wb_ref, wob_ref, out_ref, z_out_ref, wide_ref, m_ref, bias_ref, send_sem, recv_sem, *scratch):
     me = lax.axis_index('dap')
+    greet(me)
+    outer, along, across, _ = pair_stages(
+        me, 0, False, own_ref, full_ref, z_ref, mask_ref, res_ref, (wm_ref, wba_ref, wa_ref, woa_ref, wbb_ref, wb_ref, wob_ref),
+        z_out_ref, None, send_sem, recv_sem, scratch[8:])
+    outer()
     turn_tokens(x_ref, wide_ref, m_ref)
     bias_ref[...] = rows_ref[...].astype(F32) * LOG2E
 
     def finish(block, out):
         out_ref[pl.ds(4 * block, 4)] = out.reshape(4, RES, WIDE)
 
-    attend_blocks(8, scratch, lambda at: m_ref[pl.ds(at * 4, 4)].astype(F32).reshape(BLOCK, WIDE),
+    def aside(i, half):
+        if half:
+            pl.when(i == 3)(along)
+            pl.when(i == 5)(across)
+
+    attend_blocks(8, scratch[:8], lambda at: m_ref[pl.ds(at * 4, 4)].astype(F32).reshape(BLOCK, WIDE),
                   lambda at: lambda sl: w_ref[sl, :], lambda at: wo_ref[...],
-                  lambda at: row_keep(mask_ref, 32 * me + 4 * at), bias_ref, finish, lambda: None, lambda i: None)
+                  lambda at: row_keep(mask_ref, 32 * me + 4 * at), bias_ref, finish, lambda: None, aside)
 
 
 def turn_tokens(x_ref, wide_ref, m_ref):
@@ -284,24 +292,28 @@
     lax.fori_loop(0, inner, one, 0, unroll=2)
 
 
-def row_last(x, rows, mask, w, wo):
+def row_last(args, weights):
     return pl.pallas_call(
         row_last_kernel,
         grid=(1,),
-        in_specs=[whole(x), whole(rows), whole(mask)] + [of_layer(a, 1) for a in (w, wo)],
-        out_specs=VMEM,
-        out_shape=jax.ShapeDtypeStruct((32, RES, WIDE), BF16),
+        in_specs=[whole(a) for a in args] + [of_layer(a, 1) for a in weights],
+        out_specs=[VMEM] * 2,
+        out_shape=[jax.ShapeDtypeStruct((32, RES, WIDE), BF16), jax.ShapeDtypeStruct((HELD, RES, LANES), BF16)],
         scratch_shapes=[
             pltpu.VMEM((3, 2048, LANES), F32),
             pltpu.VMEM((32, RES, WIDE), BF16),
             pltpu.VMEM((HELD, RES, LANES), F32),
-        ] + attend_scratch(HELD, 24, RES, WIDE),
+            pltpu.SemaphoreType.DMA((12,)),
+            pltpu.SemaphoreType.DMA((12,)),
+        ] + attend_scratch(HELD, 24, RES, WIDE) + pair_scratch(),
+        compiler_params=pltpu.CompilerParams(collective_id=2, has_side_effects=True),
         cost_estimate=pl.CostEstimate(flops=10 ** 10, bytes_accessed=2 ** 22, transcendentals=0),
         name="row_last",
-    )(x, rows, mask, w, wo)
-
-
-def col_kernel(x_ref, mask_ref, w_ref, wo_ref, wp_ref, out_ref, own1_ref, own2_ref, full1_ref, full2_ref,
+    )(*args, *weights)
+
+
+def col_kernel(x_ref, mask_ref, w_ref, wo_ref, wp_ref, z_ref, res_ref, wm_ref, wba_ref, wa_ref, woa_ref, wbb_ref, wb_ref, wob_ref, wn_ref,
+               out_ref, own2_ref, full2_ref, z_out_ref, next_ref, own1_ref, full1_ref,
                wide_ref, m_ref, part_ref, keys_ref, send_sem, recv_sem, *scratch):
     me = lax.axis_index('dap')
     greet(me)
@@ -325,32 +337,40 @@
             part_ref[block, blk] = jnp.where(layer == 0, parts[1][:, lanes].astype(F32), parts[0][:, lanes].astype(F32)).astype(BF16)
 
     def part_copies(block, full_ref):
-        target = full_ref.at[pl.ds(HELD * me + block % 8 * 2, 2)]
-        return [pltpu.make_async_remote_copy(
-            src_ref=part_ref.at[block], dst_ref=target, send_sem=send_sem.at[3 * block + o - 1],
-            recv_sem=recv_sem.at[3 * block + o - 1], device_id={'dap': lax.rem(me + o, 4)},
-            device_id_type=pl.DeviceIdType.MESH) for o in range(1, 4)]
+        return group_copies(me, block, send_sem, recv_sem, lambda peer: part_ref.at[block],
+                            full_ref.at[pl.ds(HELD * me + block % 8 * 2, 2)])
 
     def seq_copies(pair):
-        target = out_ref.at[pl.ds(HELD * me + 2 * pair, 2)]
-        return [pltpu.make_async_remote_copy(
-            src_ref=m_ref.at[2, pl.ds(2 * pair, 2), pl.ds(pl.multiple_of(32 * lax.rem(me + o, 4), 32), 32), :],
-            dst_ref=target, send_sem=send_sem.at[48 + 3 * pair + o - 1], recv_sem=recv_sem.at[48 + 3 * pair + o - 1],
-            device_id={'dap': lax.rem(me + o, 4)}, device_id_type=pl.DeviceIdType.MESH) for o in range(1, 4)]
+        return group_copies(
+            me, HELD + pair, send_sem, recv_sem,
+            lambda peer: m_ref.at[2, pl.ds(2 * pair, 2), pl.ds(pl.multiple_of(32 * peer, 32), 32), :],
+            out_ref.at[pl.ds(HELD * me + 2 * pair, 2)])
+
+    outer, along, across, close = pair_stages(
+        me, 24, True, own1_ref, full1_ref, z_ref, mask_ref, res_ref, (wm_ref, wba_ref, wa_ref, woa_ref, wbb_ref, wb_ref, wob_ref, wn_ref),
+        z_out_ref, next_ref, send_sem, recv_sem, scratch[8:])
+
+    def open_pairs():
+        drain_parts(0, full1_ref)
+        outer()
+
+    def drain_parts(start, full_ref):
+        def one(pair, carry):
+            finish_all(part_copies(start + pair, full_ref))
+            return carry
+        lax.fori_loop(0, 8, one, 0)
 
     def emit_first(block):
-        for copy in part_copies(block, full1_ref):
-            copy.start()
+        start_all(part_copies(block, full1_ref))
         full1_ref[pl.ds(HELD * me + 2 * block, 2)] = part_ref[block]
 
     def emit_second(block):
         pair = block - 8
-        for copy in part_copies(block, full2_ref) + seq_copies(pair):
-            copy.start()
+        start_all(part_copies(block, full2_ref) + seq_copies(pair))
         full2_ref[pl.ds(HELD * me + 2 * pair, 2)] = part_ref[block]
         out_ref[pl.ds(HELD * me + 2 * pair, 2)] = m_ref[2, pl.ds(2 * pair, 2), pl.ds(pl.multiple_of(32 * me, 32), 32), :]
 
-    def aside(i):
+    def aside(i, half):
         @pl.when(jnp.logical_and(i >= 3, i < 11))
         def _():
             emit_first(i - 3)
@@ -359,44 +379,54 @@
         def _():
             emit_second(i - 3)
 
-    attend_blocks(16, scratch, lambda at: m_ref[at // 8, pl.ds(at % 8 * 2, 2)].astype(F32).reshape(BLOCK, WIDE),
+        if half:
+            pl.when(i == 11)(open_pairs)
+            pl.when(i == 13)(along)
+            pl.when(i == 15)(across)
+
+    attend_blocks(16, scratch[:8], lambda at: m_ref[at // 8, pl.ds(at % 8 * 2, 2)].astype(F32).reshape(BLOCK, WIDE),
                   lambda at: lambda sl: w_ref[at // 8, sl, :], lambda at: wo_ref[at // 8],
                   keep, None, finish, lambda: None, aside)
     emit_second(14)
     emit_second(15)
 
+    close()
+    drain_parts(8, full2_ref)
+
     def drain(pair, carry):
-        for copy in part_copies(pair, full1_ref) + part_copies(pair + 8, full2_ref) + seq_copies(pair):
-            copy.wait()
+        finish_all(seq_copies(pair))
         return carry
 
     lax.fori_loop(0, 8, drain, 0)
 
 
-def column_pair(x, mask, w, wo, wp):
+def column_pair(args, weights, w_next):
     return pl.pallas_call(
         col_kernel,
-        in_specs=[VMEM] * 5,
+        grid=(1,),
+        in_specs=[whole(a) for a in args] + [of_layer(a, 0) for a in weights] + [of_layer(w_next, 1)],
         out_specs=[VMEM] * 5,
         out_shape=[
             jax.ShapeDtypeStruct((RES, 32, WIDE), BF16),
             jax.ShapeDtypeStruct((8, 32, BLOCK), BF16),
-            jax.ShapeDtypeStruct((8, 32, BLOCK), BF16),
             jax.ShapeDtypeStruct((RES, 32, LANES), BF16),
-            jax.ShapeDtypeStruct((RES, 32, LANES), BF16),
+            jax.ShapeDtypeStruct((HELD, RES, LANES), BF16),
+            jax.ShapeDtypeStruct((HELD, RES, LANES), BF16),
         ],
         scratch_shapes=[
+            pltpu.VMEM((8, 32, BLOCK), BF16),
+            pltpu.VMEM((RES, 32, LANES), BF16),
             pltpu.VMEM((3, 2048, LANES), F32),
             pltpu.VMEM((3, HELD, LANES, WIDE), BF16),
             pltpu.VMEM((HELD, 2, 32, LANES), BF16),
             pltpu.VMEM((LANES, HELD), F32),
-            pltpu.SemaphoreType.DMA((72,)),
-            pltpu.SemaphoreType.DMA((72,)),
-        ] + attend_scratch(HELD, 24, LANES, WIDE),
+            pltpu.SemaphoreType.DMA((84,)),
+            pltpu.SemaphoreType.DMA((84,)),
+        ] + attend_scratch(HELD, 24, LANES, WIDE) + pair_scratch(),
         compiler_params=pltpu.CompilerParams(collective_id=1, has_side_effects=True),
         cost_estimate=pl.CostEstimate(flops=10 ** 10, bytes_accessed=2 ** 22, transcendentals=0),
         name="col_pair",
-    )(x, mask, w, wo, wp)
+    )(*args, *weights, w_next)
 
 
 def greet(me):
@@ -406,16 +436,19 @@
     pl.semaphore_wait(barrier, 3)
 
 
-def push(me, kind, send_sem, recv_sem, source, target):
+def group_copies(me, kind, send_sem, recv_sem, source, target):
     copies = []
     for o in range(1, 4):
         peer = lax.rem(me + o, 4)
-        copy = pltpu.make_async_remote_copy(
+        copies.append(pltpu.make_async_remote_copy(
             src_ref=source(peer), dst_ref=target, send_sem=send_sem.at[3 * kind + o - 1],
-            recv_sem=recv_sem.at[3 * kind + o - 1], device_id={'dap': peer}, device_id_type=pl.DeviceIdType.MESH)
+            recv_sem=recv_sem.at[3 * kind + o - 1], device_id={'dap': peer}, device_id_type=pl.DeviceIdType.MESH))
+    return copies
+
+
+def start_all(copies):
+    for copy in copies:
         copy.start()
-        copies.append(copy)
-    return copies
 
 
 def finish_all(copies):
@@ -461,136 +494,126 @@
     leave(3)()
 
 
-def pair_kernel(has_next, own_ref, full_ref, z_ref, mask_ref, res_ref, wm_ref, wba_ref, wa_ref, woa_ref, wbb_ref, wb_ref, wob_ref, *rest):
-    if has_next:
-        wn_ref, out_ref, next_ref = rest[:3]
-        rest = rest[3:]
-    else:
-        out_ref = rest[0]
-        rest = rest[1:]
-    (full32_ref, o_ref, wt_ref, zf_ref, zt_ref, ln_ref, bias_ref, la_ref, ra_ref, lb_ref, rb_ref, zs_ref, zr_ref, nl_ref,
-     send_sem, recv_sem) = rest[:16]
-    att = rest[16:]
+def pair_stages(me, first, swap, own_ref, full_ref, z_ref, mask_ref, res_ref, weights, out_ref, next_ref, send_sem, recv_sem, scratch):
+    wm_ref, wba_ref, wa_ref, woa_ref, wbb_ref, wb_ref, wob_ref = weights[:7]
+    (full32_ref, o_ref, wt_ref, zf_ref, zt_ref, ln_ref, bias_ref, la_ref, ra_ref, lb_ref, rb_ref, zs_ref, zr_ref, nl_ref) = scratch[:14]
+    att = scratch[14:]
     pt_refs, gt_refs, others = att[0:2], att[2:4], att[4:7]
-    me = lax.axis_index('dap')
     mine = pl.ds(pl.multiple_of(HELD * me, HELD), HELD)
-    greet(me)
-    diagonal = lax.broadcasted_iota(jnp.int32, (RES, RES), 0) == lax.broadcasted_iota(jnp.int32, (RES, RES), 1)
-    keys = jnp.sum(jnp.where(diagonal, jnp.broadcast_to(res_ref[...], (RES, RES)), 0).astype(F32), axis=1, keepdims=True)
-    keep = jnp.broadcast_to(keys, (RES, LANES)) > 0.5
-    mask = mask_ref[...].astype(F32).astype(BF16)
-    norm = lax.dot_general(mask, mask_ref[mine, :].astype(F32).astype(BF16), NT, preferred_element_type=F32)
-
-    full32_ref[:CELLS] = wm_ref[...].astype(F32).reshape(CELLS, LANES)
-    if has_next:
-        for q in range(32):
-            wt_ref[pl.ds(32 * q, 32), :] = full32_ref[pl.ds(q, 32, stride=32), :].astype(BF16)
-    else:
-        wt_ref[...] = wm_ref[...].reshape(CELLS, LANES)
-    w_turned = wt_ref[...].T
-    full32_ref[...] = full_ref[...].astype(F32).reshape(2048, LANES)
-    own = own_ref[...].reshape(BLOCK, BLOCK)
-    zeros = jnp.zeros((RES, LANES), BF16)
-
-    def one(q, carry):
-        c_q = full32_ref[pl.ds(q, RES, stride=32), :].astype(BF16)
-        rhs = jnp.concatenate([jnp.concatenate([c_q, zeros], axis=1), jnp.concatenate([zeros, c_q], axis=1)], axis=0)
-        o = lax.dot_general(own, rhs, NT, preferred_element_type=F32).astype(BF16)
+
+    def keep():
+        diagonal = lax.broadcasted_iota(jnp.int32, (RES, RES), 0) == lax.broadcasted_iota(jnp.int32, (RES, RES), 1)
+        keys = jnp.sum(jnp.where(diagonal, jnp.broadcast_to(res_ref[...], (RES, RES)), 0).astype(F32), axis=1, keepdims=True)
+        return jnp.broadcast_to(keys, (RES, LANES)) > 0.5
+
+    def exchange(kind):
+        source, target = (
+            (lambda peer: la_ref, ra_ref.at[:, mine, :]),
+            (lambda peer: zs_ref.at[:, pl.ds(pl.multiple_of(HELD * peer, HELD), HELD), :], zr_ref.at[mine]),
+            (lambda peer: lb_ref, rb_ref.at[:, mine, :]),
+            (lambda peer: nl_ref, None if next_ref is None else next_ref.at[:, mine, :]),
+        )[kind]
+        return group_copies(me, first + kind, send_sem, recv_sem, source, target)
+
+    def outer():
+        mask = mask_ref[...].astype(F32).astype(BF16)
+        norm = lax.dot_general(mask, mask_ref[mine, :].astype(F32).astype(BF16), NT, preferred_element_type=F32)
+        full32_ref[:CELLS] = wm_ref[...].astype(F32).reshape(CELLS, LANES)
+        if swap:
+            for q in range(32):
+                wt_ref[pl.ds(32 * q, 32), :] = full32_ref[pl.ds(q, 32, stride=32), :].astype(BF16)
+        else:
+            wt_ref[...] = wm_ref[...].reshape(CELLS, LANES)
+        w_turned = wt_ref[...].T
+        full32_ref[...] = full_ref[...].astype(F32).reshape(2048, LANES)
+        own = own_ref[...].reshape(BLOCK, BLOCK)
+        zeros = jnp.zeros((RES, LANES), BF16)
+
+        def one(q, carry):
+            c_q = full32_ref[pl.ds(q, RES, stride=32), :].astype(BF16)
+            rhs = jnp.concatenate([jnp.concatenate([c_q, zeros], axis=1), jnp.concatenate([zeros, c_q], axis=1)], axis=0)
+            o = lax.dot_general(own, rhs, NT, preferred_element_type=F32).astype(BF16)
+            for pair in range(8):
+                o_ref[pair, pl.ds(pl.multiple_of(q * 32, 32), 32), :] = o[32 * pair:32 * pair + 32]
+            return carry
+
+        lax.fori_loop(0, 32, one, 0, unroll=4)
         for pair in range(8):
-            o_ref[pair, pl.ds(pl.multiple_of(q * 32, 32), 32), :] = o[32 * pair:32 * pair + 32]
-        return carry
-
-    lax.fori_loop(0, 32, one, 0, unroll=4)
-    for pair in range(8):
-        update = jnp.dot(w_turned, o_ref[pair], preferred_element_type=F32).T
-        z = z_ref[pl.ds(2 * pair, 2)].astype(F32).reshape(LANES, LANES)
-        below = jnp.concatenate([pick_column(norm, 2 * pair), pick_column(norm, 2 * pair + 1)], axis=0)
-        z = (z + update / (1e-3 + below)).astype(BF16).astype(F32)
-        rows = pl.ds(LANES * pair, LANES)
-        zf_ref[rows, :] = z
-        ln_ref[rows, :] = layer_norm(z)
-
-    la_ref[...] = local_bias_rows(ln_ref, wba_ref[...]).reshape(4, HELD, LANES)
-    copies = push(me, 0, send_sem, recv_sem, lambda peer: la_ref, ra_ref.at[:, mine, :])
-    ra_ref[:, mine, :] = la_ref[...]
-
-    def queries_ready():
-        finish_all(copies)
-        bias_by_query(ra_ref, bias_ref)
-
-    triangle(zf_ref, ln_ref, wa_ref, woa_ref, keep, bias_ref, pt_refs, gt_refs, others, queries_ready)
-
-    zs_ref[...] = zf_ref[...].astype(BF16).reshape(HELD, RES, LANES)
-    norm_all(zf_ref, ln_ref)
-    moved = push(me, 1, send_sem, recv_sem, lambda peer: zs_ref.at[:, pl.ds(pl.multiple_of(HELD * peer, HELD), HELD), :], zr_ref.at[mine])
-    zr_ref[mine] = zs_ref[:, mine, :]
-    lb_ref[...] = local_bias_rows(ln_ref, wbb_ref[...]).reshape(4, HELD, LANES)
-    copies_b = push(me, 2, send_sem, recv_sem, lambda peer: lb_ref, rb_ref.at[:, mine, :])
-    rb_ref[:, mine, :] = lb_ref[...]
-    finish_all(moved)
-    zt_ref[...] = zr_ref[...].astype(F32).reshape(CELLS, LANES)
-    for row in range(HELD):
-        value = zt_ref[pl.ds(row, RES, stride=HELD), :]
-        zf_ref[pl.ds(RES * row, RES), :] = value
-        ln_ref[pl.ds(RES * row, RES), :] = layer_norm(value)
-
-    def keys_ready():
-        finish_all(copies_b)
-        bias_ref[...] = rb_ref[...].astype(F32) * LOG2E
-
-    triangle(zf_ref, ln_ref, wb_ref, wob_ref, keep, bias_ref, pt_refs, gt_refs, others, keys_ready)
-    out_ref[...] = zf_ref[...].astype(BF16).reshape(HELD, RES, LANES)
-    if has_next:
+            update = jnp.dot(w_turned, o_ref[pair], preferred_element_type=F32).T
+            z = z_ref[pl.ds(2 * pair, 2)].astype(F32).reshape(LANES, LANES)
+            below = jnp.concatenate([pick_column(norm, 2 * pair), pick_column(norm, 2 * pair + 1)], axis=0)
+            z = (z + update / (1e-3 + below)).astype(BF16).astype(F32)
+            rows = pl.ds(LANES * pair, LANES)
+            zf_ref[rows, :] = z
+            ln_ref[rows, :] = layer_norm(z)
+        la_ref[...] = local_bias_rows(ln_ref, wba_ref[...]).reshape(4, HELD, LANES)
+        start_all(exchange(0))
+        ra_ref[:, mine, :] = la_ref[...]
+
+    def along():
+        def ready():
+            finish_all(exchange(0))
+            bias_by_query(ra_ref, bias_ref)
+
+        triangle(zf_ref, ln_ref, wa_ref, woa_ref, keep(), bias_ref, pt_refs, gt_refs, others, ready)
+        zs_ref[...] = zf_ref[...].astype(BF16).reshape(HELD, RES, LANES)
         norm_all(zf_ref, ln_ref)
-        nl_ref[...] = local_bias_rows(ln_ref, wn_ref[...]).reshape(HELD, HELD, LANES)
-        copies = push(me, 3, send_sem, recv_sem, lambda peer: nl_ref, next_ref.at[:, mine, :])
-        next_ref[:, mine, :] = nl_ref[...]
-        finish_all(copies)
+        start_all(exchange(1))
+        zr_ref[mine] = zs_ref[:, mine, :]
+        lb_ref[...] = local_bias_rows(ln_ref, wbb_ref[...]).reshape(4, HELD, LANES)
+        start_all(exchange(2))
+        rb_ref[:, mine, :] = lb_ref[...]
+
+    def across():
+        finish_all(exchange(1))
+        zt_ref[...] = zr_ref[...].astype(F32).reshape(CELLS, LANES)
+        for row in range(HELD):
+            value = zt_ref[pl.ds(row, RES, stride=HELD), :]
+            zf_ref[pl.ds(RES * row, RES), :] = value
+            ln_ref[pl.ds(RES * row, RES), :] = layer_norm(value)
+
+        def ready():
+            finish_all(exchange(2))
+            bias_ref[...] = rb_ref[...].astype(F32) * LOG2E
+
+        triangle(zf_ref, ln_ref, wb_ref, wob_ref, keep(), bias_ref, pt_refs, gt_refs, others, ready)
+        out_ref[...] = zf_ref[...].astype(BF16).reshape(HELD, RES, LANES)
+        if next_ref is not None:
+            norm_all(zf_ref, ln_ref)
+            nl_ref[...] = local_bias_rows(ln_ref, weights[7][...]).reshape(HELD, HELD, LANES)
+            start_all(exchange(3))
+            next_ref[:, mine, :] = nl_ref[...]
+
+    def close():
+        if next_ref is not None:
+            finish_all(exchange(3))
+
+    return outer, along, across, close
+
+
+def pair_scratch():
+    return [
+        pltpu.VMEM((2048, LANES), F32),
+        pltpu.VMEM((8, CELLS, LANES), BF16),
+        pltpu.VMEM((CELLS, LANES), BF16),
+        pltpu.VMEM((CELLS, LANES), F32),
+        pltpu.VMEM((CELLS, LANES), F32),
+        pltpu.VMEM((CELLS, LANES), BF16),
+        pltpu.VMEM((4, RES, LANES), F32),
+        pltpu.VMEM((4, HELD, LANES), BF16),
+        pltpu.VMEM((4, RES, LANES), BF16),
+        pltpu.VMEM((4, HELD, LANES), BF16),
+        pltpu.VMEM((4, RES, LANES), BF16),
+        pltpu.VMEM((HELD, RES, LANES), BF16),
+        pltpu.VMEM((RES, HELD, LANES), BF16),
+        pltpu.VMEM((HELD, HELD, LANES), BF16),
+    ] + attend_scratch(4, 32, RES, LANES)[1:]
 
 
 def norm_all(zf_ref, ln_ref):
     for block in range(8):
         rows = pl.ds(LANES * block, LANES)
         ln_ref[rows, :] = layer_norm(zf_ref[rows, :])
-
-
-def pair_block(ident, layer, own, full, z, mask, res_mask, weights, w_next):
-    has_next = w_next is not None
-    out_shape = [jax.ShapeDtypeStruct(z.shape, BF16)]
-    picks = [of_layer(w, layer) for w in weights]
-    if has_next:
-        weights = weights + (w_next,)
-        picks.append(of_layer(w_next, layer + 1))
-        out_shape.append(jax.ShapeDtypeStruct((HELD, RES, LANES), BF16))
-    args = (own, full, z, mask, res_mask)
-    return pl.pallas_call(
-        functools.partial(pair_kernel, has_next),
-        grid=(1,),
-        out_shape=out_shape,
-        in_specs=[whole(a) for a in args] + picks,
-        out_specs=[VMEM] * len(out_shape),
-        scratch_shapes=[
-            pltpu.VMEM((2048, LANES), F32),
-            pltpu.VMEM((8, CELLS, LANES), BF16),
-            pltpu.VMEM((CELLS, LANES), BF16),
-            pltpu.VMEM((CELLS, LANES), F32),
-            pltpu.VMEM((CELLS, LANES), F32),
-            pltpu.VMEM((CELLS, LANES), BF16),
-            pltpu.VMEM((4, RES, LANES), F32),
-            pltpu.VMEM((4, HELD, LANES), BF16),
-            pltpu.VMEM((4, RES, LANES), BF16),
-            pltpu.VMEM((4, HELD, LANES), BF16),
-            pltpu.VMEM((4, RES, LANES), BF16),
-            pltpu.VMEM((HELD, RES, LANES), BF16),
-            pltpu.VMEM((RES, HELD, LANES), BF16),
-            pltpu.VMEM((HELD, HELD, LANES), BF16),
-            pltpu.SemaphoreType.DMA((12,)),
-            pltpu.SemaphoreType.DMA((12,)),
-        ] + attend_scratch(4, 32, RES, LANES)[1:],
-        compiler_params=pltpu.CompilerParams(collective_id=ident, has_side_effects=True),
-        cost_estimate=pl.CostEstimate(flops=10 ** 10, bytes_accessed=2 ** 22, transcendentals=0),
-        name="pair_block",
-    )(*args, *weights)
 
 
 def solution(mesh):
@@ -607,14 +630,12 @@
         res_mask = res_mask.reshape(1, RES)
 
         m = row_first(m, z, mask, w_row_bias, w_row_in, w_row_out)
-        m, own1, own2, full1, full2 = column_pair(m, mask, w_col_in, w_col_out, w_opm_in)
-        z, row_bias = pair_block(
-            2, 0, own1, full1, z, mask, res_mask,
+        m, own, full, z, row_bias = column_pair(
+            (m, mask, w_col_in, w_col_out, w_opm_in, z, res_mask),
             (w_opm_out, w_ts_bias, w_ts_in, w_ts_out, w_te_bias, w_te_in, w_te_out), w_row_bias)
-        z, = pair_block(
-            3, 1, own2, full2, z, mask, res_mask,
-            (w_opm_out, w_te_bias, w_te_in, w_te_out, w_ts_bias, w_ts_in, w_ts_out), None)
-        m = row_last(m, row_bias, mask, w_row_in, w_row_out)
+        m, z = row_last(
+            (m, row_bias, own, full, z, mask, res_mask),
+            (w_row_in, w_row_out, w_opm_out, w_te_bias, w_te_in, w_te_out, w_ts_bias, w_ts_in, w_ts_out))
         return m, z
 
     in_specs = (P(('data', 'dap')), P(('data', 'dap')), P('data'), P('data')) + (P(),) * 13

time: 155 us -> 137 us (0.88)
  Pallas kernels: 153 us -> 132 us
  local copies, waits for them, and re-layouts: 0.71 us -> 3.46 us
    pallas_call x4 -> x2, Pallas kernels: 119 us -> 98.4 us  [the longest x1 64.7 us: column_pair(): pl.pallas_call(col_kernel, grid=(1,), in_specs=[whole(a) for a in args] +...]
    unnamed x3 -> x4, local copies, waits for them, and re-layouts: 0.71 us -> 3.46 us
where the time goes in v6:
time: 137 us; the launch traced here: 136 us
  Pallas kernels  132 us (96%)
  local copies, waits for them, and re-layouts  3.46 us (3%)
    pallas_call x1, Pallas kernels, column_pair(): pl.pallas_call(col_kernel, grid=(1,), in_specs=[whole(a) for a in args] +...  64.7 us
    pallas_call x1, Pallas kernels, row_first(): pl.pallas_call(row_first_kernel, grid=(1,), in_specs=[whole(x), whole(z),...  34 us
    pallas_call x1, Pallas kernels, row_last(): pl.pallas_call(row_last_kernel, grid=(1,), in_specs=[whole(a) for a in ar...  33.7 us
    unnamed x4, local copies, waits for them, and re-layouts  3.46 us

profile of v6, /device:TPU:0, one launch (start us, length us, event | category | flops | bytes accessed | tf_op | source)
XLA Modules:
  0.0 136.5 jit_solution(599399477229432398)
XLA Ops:
  0.6 34.0 %row_first.1.x_ref = bf16[128,16,384]{2,1,0:T(8,128)(2,1)} custom-call(bf16[32,64,384]{2,1,0:T(8,128)(2,1)} %x_ref.1, bf16[16,64,128]{2,1,0:T(8,128)(2,1)} %z_ref.3, s32[64,128]{1,0:T(8,128)} %bitcast.42, bf16[2,16,128]{2,1,0:T(8,128)(2,1)} %bitcast.45, bf16[2,1536,384]{2,1,0:T(8,128)(2,1)} %bitcast.26, bf16[2,384,384]{2,1,0:T(8,128)(2,1)} %bitcast.29), custom_call_target="tpu_custom_call" | custom-call | flops 10000000000 | bytes 4194304 | tf_op jit(solution)/shard_map/row_first/pallas_call | solution.py:236
  34.6 64.7 %col_pair.1 = (bf16[64,32,384]{2,1,0:T(8,128)(2,1)}, bf16[8,32,256]{2,1,0:T(8,128)(2,1)}, bf16[64,32,128]{2,1,0:T(8,128)(2,1)}, bf16[16,64,128]{2,1,0:T(8,128)(2,1)}, bf16[16,64,128]{2,1,0:T(8,128)(2,1)}) custom-call(bf16[128,16,384]{2,1,0:T(8,128)(2,1)} %row_first.1.x_ref, s32[64,128]{1,0:T(8,128)} %bitcast.43, bf16[2,1536,384]{2,1,0:T(8,128)(2,1)} %bitcast.25, ...), custom_call_target="tpu_custom_call" | custom-call | flops 10000000000 | bytes 4194304 | tf_op jit(solution)/shard_map/col_pair/pallas_call | solution.py:404
  99.4 33.7 %row_last.1 = (bf16[32,64,384]{2,1,0:T(8,128)(2,1)}, bf16[16,64,128]{2,1,0:T(8,128)(2,1)}) custom-call(bf16[64,32,384]{2,1,0:T(8,128)(2,1)} %get-tuple-element.7.x_ref, bf16[16,64,128]{2,1,0:T(8,128)(2,1)} %get-tuple-element.8.rows_ref, bf16[8,32,256]{2,1,0:T(8,128)(2,1)} %get-tuple-element.9.own_ref, bf16[64,32,128]{2,1,0:T(8,128)(2,1)} %get-tuple-element.10.full_ref, ...), custom_call_target="tpu_custom_call" | custom-call | flops 10000000000 | bytes 4194304 | tf_op jit(solution)/shard_map/row_last/pallas_call | solution.py:296
  133.0 0.0 copy-start
  133.0 2.8 %copy.21 = bf16[32,64,384]{2,1,0:T(8,128)(2,1)} copy(bf16[32,64,384]{2,1,0:T(8,128)(2,1)} %get-tuple-element.14) | data formatting | bytes 3145728
  135.8 0.0 copy-done
  135.8 0.7 copy.22
Async XLA Ops:
  133.0 2.8 %copy-start = (bf16[16,64,128]{2,1,0:T(8,128)(2,1)S(1)}, bf16[16,64,128]{2,1,0:T(8,128)(2,1)}, u32[]{:S(2)}) copy-start(bf16[16,64,128]{2,1,0:T(8,128)(2,1)} %get-tuple-element.15) | copy-start | bytes 786436

commit v7 on v6

--- a/solution.py
+++ b/solution.py
@@ -37,11 +37,13 @@
     return upper, lower
 
 
-def attend_units(pt_ref, gt_ref, kt_ref, lg_ref, pr_ref, heads, dim, keep, bias_ref, work):
+def attend_stream(blocks, others, heads, dim, bias_ref, jobs):
+    kt_ref, lg_ref, pr_ref = others
     width = heads * dim
     rows = 2 * dim
     pairs = heads // 2
-    units = 2 * pairs
+    each = 2 * pairs
+    units = each * len(blocks)
     up, low = half_masks(rows, dim)
     scale = dim ** -0.5 * LOG2E
     if bias_ref is not None:
@@ -50,36 +52,35 @@
         right_b = (1.0 - left.astype(F32)).astype(BF16)
 
     def place(unit):
-        return pl.ds(unit // pairs * LANES, LANES), rows * (unit % pairs)
+        return blocks[unit // each], pl.ds(unit % each // pairs * LANES, LANES), rows * (unit % pairs)
 
     def turn_keys(unit):
-        ln, r = place(unit)
+        (pt_ref, _, _), ln, r = place(unit)
         kt_ref[unit % SLOTS] = pt_ref[pl.ds(width + r, rows), ln].T
 
     def make_logits(unit):
-        ln, r = place(unit)
+        (pt_ref, _, _), ln, r = place(unit)
         q = pt_ref[pl.ds(r, rows), ln]
         rhs = jnp.concatenate([q * up, q * low], axis=1)
         logits2 = jnp.dot(kt_ref[unit % SLOTS], rhs, preferred_element_type=F32)
         for half in range(2):
             lg = logits2[:, LANES * half:LANES * half + LANES]
             if bias_ref is not None:
-                lg = jnp.where(left, lg[0:RES], lg[RES:LANES])
+                lg = jnp.where(left, lg[:RES], lg[RES:])
             lg_ref[unit % SLOTS, half] = lg
 
     def soften(unit):
-        blk, hp = unit // pairs, unit % pairs
+        (_, _, keep), _, _ = place(unit)
         for half in range(2):
             lg = lg_ref[unit % SLOTS, half] * scale
             if bias_ref is not None:
-                lg = lg + bias_ref[2 * hp + half]
-            lg = jnp.where(keep[blk], lg, NEG)
+                lg = lg + bias_ref[2 * (unit % pairs) + half]
+            lg = jnp.where(keep[unit % each // pairs], lg, NEG)
             e = jnp.exp2(lg - jnp.max(lg, axis=0, keepdims=True))
-            p = (e * (1.0 / jnp.sum(e, axis=0, keepdims=True))).astype(BF16)
-            pr_ref[unit % SLOTS, half] = p
+            pr_ref[unit % SLOTS, half] = (e * (1.0 / jnp.sum(e, axis=0, keepdims=True))).astype(BF16)
 
     def mix(unit):
-        ln, r = place(unit)
+        (pt_ref, gt_ref, _), ln, r = place(unit)
         v = pt_ref[pl.ds(2 * width + r, rows), ln]
         g = pt_ref[pl.ds(3 * width + r, rows), ln]
         probs = []
@@ -90,23 +91,24 @@
         gt_ref[pl.ds(r, rows), ln] = (att * jax.nn.sigmoid(g.astype(F32))).astype(BF16)
 
     stages = ((turn_keys, 0), (make_logits, LAG), (soften, 2 * LAG), (mix, 3 * LAG))
-    ticks = units + 3 * LAG
-    for tick in range(ticks):
+    for tick in range(units + 3 * LAG):
         for stage, lag in stages:
             if 0 <= tick - lag < units:
                 stage(tick - lag)
-        for job in work[len(work) * tick // ticks:len(work) * (tick + 1) // ticks]:
-            job()
-
-
-def project(ln_ref, pt_ref, w):
-    rows = pt_ref.shape[0]
-    chunk = BLOCK if rows > CELLS else LANES
+        for start, end, work in jobs:
+            if start <= tick < end:
+                for job in work[len(work) * (tick - start) // (end - start):len(work) * (tick - start + 1) // (end - start)]:
+                    job()
+
+
+def project(ln_ref, pt_ref, w, rows=slice(None)):
+    size = pt_ref.shape[0]
+    chunk = BLOCK if size > CELLS else LANES
 
     def job(part):
         sl = pl.ds(part * chunk, chunk)
-        pt_ref[sl, :] = lax.dot_general(w(sl), ln_ref[...], NT, preferred_element_type=F32).astype(BF16)
-    return [functools.partial(job, part) for part in range(rows // chunk)]
+        pt_ref[sl, :] = lax.dot_general(w(sl), ln_ref[rows, :], NT, preferred_element_type=F32).astype(BF16)
+    return [functools.partial(job, part) for part in range(size // chunk)]
 
 
 def leave(gt_ref, x_old, wo):
@@ -121,11 +123,11 @@
     ready()
 
     def body(turn, carry):
-        for half in (1, 0):
-            i = 2 * turn + 2 - half
-            new = jnp.minimum(i, blocks - 1)
-            old = jnp.maximum(i - 2, 0)
-            aside(i, half)
+        aside(turn)
+
+        def jobs(half):
+            new = jnp.minimum(2 * turn + 2 - half, blocks - 1)
+            old = jnp.maximum(2 * turn - half, 0)
 
             def norm():
                 ln_ref[...] = layer_norm(read(new))
@@ -133,26 +135,28 @@
             def done():
                 finish(old, leave(gt_refs[half], read(old), w_out(old)))
 
-            work = [norm, done] + project(ln_ref, pt_refs[half], w_in(new))
-            attend_units(pt_refs[1 - half], gt_refs[1 - half], *others, 16, 24, keep(i - 1), bias_ref, work)
+            return [norm, done] + project(ln_ref, pt_refs[half], w_in(new))
+
+        both = [(pt_refs[half], gt_refs[half], keep(2 * turn + half)) for half in range(2)]
+        attend_stream(both, others, HELD, 24, bias_ref, [
+            (0, HELD - 2, jobs(1)), (HELD + 3 * LAG, 2 * HELD + 3 * LAG, jobs(0))])
         return carry
 
     lax.fori_loop(0, blocks // 2, body, 0)
     finish(blocks - 1, leave(gt_refs[1], read(blocks - 1), w_out(blocks - 1)))
 
 
-def attend_scratch(heads, dim, keys, channels):
+def attend_scratch(heads, dim, keys, buffers):
     inner = heads * dim
-    return [
-        pltpu.VMEM((BLOCK, channels), BF16),
-        pltpu.VMEM((4 * inner, BLOCK), BF16),
-        pltpu.VMEM((4 * inner, BLOCK), BF16),
-        pltpu.VMEM((inner, BLOCK), BF16),
-        pltpu.VMEM((inner, BLOCK), BF16),
+    return [pltpu.VMEM((4 * inner, BLOCK), BF16)] * buffers + [pltpu.VMEM((inner, BLOCK), BF16)] * buffers + [
         pltpu.VMEM((SLOTS, LANES, 2 * dim), BF16),
         pltpu.VMEM((SLOTS, 2, keys, LANES), F32),
         pltpu.VMEM((SLOTS, 2, keys, LANES), BF16),
     ]
+
+
+def wide_scratch(keys):
+    return [pltpu.VMEM((BLOCK, WIDE), BF16)] + attend_scratch(HELD, 24, keys, 2)
 
 
 def pick_column(table, col):
@@ -167,14 +171,15 @@
     return [jnp.where(left, column[2 * blk], column[2 * blk + 1]) > 0.5 for blk in range(2)]
 
 
-def row_first_kernel(x_ref, z_ref, mask_ref, wb_ref, w_ref, wo_ref, out_ref, mo_ref, lnz_ref, nl_ref, rows_ref, bias_ref,
+def row_first_kernel(x_ref, z_ref, mask_ref, wb_ref, w_ref, wo_ref, out_ref, mo_ref, lnz_ref, nl_ref, rows_ref, bias_ref, spread_ref,
                      send_sem, recv_sem, *scratch):
     me = lax.axis_index('dap')
     mine = pl.ds(pl.multiple_of(HELD * me, HELD), HELD)
+    greet(me)
     for part in range(4):
         lnz_ref[pl.ds(BLOCK * part, BLOCK), :] = layer_norm(z_ref[pl.ds(4 * part, 4)].reshape(BLOCK, LANES))
-    nl_ref[...] = local_bias_rows(lnz_ref, wb_ref[...]).reshape(HELD, HELD, LANES)
-    greet(me)
+    nl_ref[...] = local_bias_rows(lnz_ref, wb_ref, spread_ref)
+    meet()
     copies = group_copies(me, 8, send_sem, recv_sem, lambda peer: nl_ref, rows_ref.at[:, mine, :])
     start_all(copies)
     rows_ref[:, mine, :] = nl_ref[...]
@@ -193,10 +198,14 @@
         start_all(moves(block))
         out_ref[pl.ds(32 * me + 4 * block, 4)] = mo_ref[pl.ds(4 * block, 4), mine, :]
 
-    def aside(i, half):
-        @pl.when(i >= 3)
+    def aside(turn):
+        @pl.when(turn >= 2)
         def _():
-            emit(i - 3)
+            emit(2 * turn - 3)
+
+        @pl.when(turn >= 1)
+        def _():
+            emit(2 * turn - 2)
 
     def finish(block, out):
         mo_ref[pl.ds(4 * block, 4)] = out.reshape(4, RES, WIDE)
@@ -204,6 +213,7 @@
     attend_blocks(8, scratch, lambda at: x_ref[pl.ds(at * 4, 4)].astype(F32).reshape(BLOCK, WIDE),
                   lambda at: lambda sl: w_ref[sl, :], lambda at: wo_ref[...],
                   lambda at: row_keep(mask_ref, 32 * me + 4 * at), bias_ref, finish, ready, aside)
+    emit(5)
     emit(6)
     emit(7)
 
@@ -245,9 +255,10 @@
             pltpu.VMEM((HELD, HELD, LANES), BF16),
             pltpu.VMEM((HELD, RES, LANES), BF16),
             pltpu.VMEM((HELD, RES, LANES), F32),
+            pltpu.VMEM((BLOCK, LANES), F32),
             pltpu.SemaphoreType.DMA((27,)),
             pltpu.SemaphoreType.DMA((27,)),
-        ] + attend_scratch(HELD, 24, RES, WIDE),
+        ] + wide_scratch(RES),
         compiler_params=pltpu.CompilerParams(collective_id=0, has_side_effects=True),
         cost_estimate=pl.CostEstimate(flops=10 ** 10, bytes_accessed=2 ** 22, transcendentals=0),
         name="row_first",
@@ -258,20 +269,20 @@
                     wbb_ref, wb_ref, wob_ref, out_ref, z_out_ref, wide_ref, m_ref, bias_ref, send_sem, recv_sem, *scratch):
     me = lax.axis_index('dap')
     greet(me)
+    meet()
     outer, along, across, _ = pair_stages(
         me, 0, False, own_ref, full_ref, z_ref, mask_ref, res_ref, (wm_ref, wba_ref, wa_ref, woa_ref, wbb_ref, wb_ref, wob_ref),
         z_out_ref, None, send_sem, recv_sem, scratch[8:])
-    outer()
+    outer(lambda: None)
     turn_tokens(x_ref, wide_ref, m_ref)
     bias_ref[...] = rows_ref[...].astype(F32) * LOG2E
 
     def finish(block, out):
         out_ref[pl.ds(4 * block, 4)] = out.reshape(4, RES, WIDE)
 
-    def aside(i, half):
-        if half:
-            pl.when(i == 3)(along)
-            pl.when(i == 5)(across)
+    def aside(turn):
+        pl.when(turn == 1)(along)
+        pl.when(turn == 2)(across)
 
     attend_blocks(8, scratch[:8], lambda at: m_ref[pl.ds(at * 4, 4)].astype(F32).reshape(BLOCK, WIDE),
                   lambda at: lambda sl: w_ref[sl, :], lambda at: wo_ref[...],
@@ -305,7 +316,7 @@
             pltpu.VMEM((HELD, RES, LANES), F32),
             pltpu.SemaphoreType.DMA((12,)),
             pltpu.SemaphoreType.DMA((12,)),
-        ] + attend_scratch(HELD, 24, RES, WIDE) + pair_scratch(),
+        ] + wide_scratch(RES) + pair_scratch(),
         compiler_params=pltpu.CompilerParams(collective_id=2, has_side_effects=True),
         cost_estimate=pl.CostEstimate(flops=10 ** 10, bytes_accessed=2 ** 22, transcendentals=0),
         name="row_last",
@@ -318,6 +329,7 @@
     me = lax.axis_index('dap')
     greet(me)
     turn_tokens(x_ref, wide_ref, m_ref.at[0])
+    meet()
     mine = pl.ds(pl.multiple_of(HELD * me, HELD), HELD)
     keys_ref[...] = mask_ref[mine, :].astype(F32).T
 
@@ -350,10 +362,6 @@
         me, 24, True, own1_ref, full1_ref, z_ref, mask_ref, res_ref, (wm_ref, wba_ref, wa_ref, woa_ref, wbb_ref, wb_ref, wob_ref, wn_ref),
         z_out_ref, next_ref, send_sem, recv_sem, scratch[8:])
 
-    def open_pairs():
-        drain_parts(0, full1_ref)
-        outer()
-
     def drain_parts(start, full_ref):
         def one(pair, carry):
             finish_all(part_copies(start + pair, full_ref))
@@ -370,23 +378,21 @@
         full2_ref[pl.ds(HELD * me + 2 * pair, 2)] = part_ref[block]
         out_ref[pl.ds(HELD * me + 2 * pair, 2)] = m_ref[2, pl.ds(2 * pair, 2), pl.ds(pl.multiple_of(32 * me, 32), 32), :]
 
-    def aside(i, half):
-        @pl.when(jnp.logical_and(i >= 3, i < 11))
-        def _():
-            emit_first(i - 3)
-
-        @pl.when(i >= 11)
-        def _():
-            emit_second(i - 3)
-
-        if half:
-            pl.when(i == 11)(open_pairs)
-            pl.when(i == 13)(along)
-            pl.when(i == 15)(across)
+    def emit_any(block):
+        pl.when(jnp.logical_and(block >= 0, block < 8))(lambda: emit_first(block))
+        pl.when(block >= 8)(lambda: emit_second(block))
+
+    def aside(turn):
+        emit_any(2 * turn - 3)
+        emit_any(2 * turn - 2)
+        pl.when(turn == 5)(lambda: outer(lambda: drain_parts(0, full1_ref)))
+        pl.when(turn == 6)(along)
+        pl.when(turn == 7)(across)
 
     attend_blocks(16, scratch[:8], lambda at: m_ref[at // 8, pl.ds(at % 8 * 2, 2)].astype(F32).reshape(BLOCK, WIDE),
                   lambda at: lambda sl: w_ref[at // 8, sl, :], lambda at: wo_ref[at // 8],
                   keep, None, finish, lambda: None, aside)
+    emit_second(13)
     emit_second(14)
     emit_second(15)
 
@@ -422,7 +428,7 @@
             pltpu.VMEM((LANES, HELD), F32),
             pltpu.SemaphoreType.DMA((84,)),
             pltpu.SemaphoreType.DMA((84,)),
-        ] + attend_scratch(HELD, 24, LANES, WIDE) + pair_scratch(),
+        ] + wide_scratch(LANES) + pair_scratch(),
         compiler_params=pltpu.CompilerParams(collective_id=1, has_side_effects=True),
         cost_estimate=pl.CostEstimate(flops=10 ** 10, bytes_accessed=2 ** 22, transcendentals=0),
         name="col_pair",
@@ -433,7 +439,10 @@
     barrier = pltpu.get_barrier_semaphore()
     for o in range(1, 4):
         pl.semaphore_signal(barrier, inc=1, device_id={'dap': lax.rem(me + o, 4)}, device_id_type=pl.DeviceIdType.MESH)
-    pl.semaphore_wait(barrier, 3)
+
+
+def meet():
+    pl.semaphore_wait(pltpu.get_barrier_semaphore(), 3)
 
 
 def group_copies(me, kind, send_sem, recv_sem, source, target):
@@ -456,49 +465,45 @@
         copy.wait()
 
 
-def local_bias_rows(ln_ref, w):
-    heads = w.shape[0]
-    spread = jnp.concatenate([jnp.broadcast_to(w[head:head + 1], (HELD, LANES)) for head in range(heads)], axis=0)
-    index = lax.broadcasted_iota(jnp.int32, spread.shape, 0) % HELD
-    total = jnp.zeros(spread.shape, F32)
-    for held in range(HELD):
-        chosen = spread * (index == held).astype(F32).astype(BF16)
-        part = ln_ref[pl.ds(RES * held, RES), :]
-        total += lax.dot_general(chosen, jnp.concatenate([part, part], axis=0), NT, preferred_element_type=F32)
-    return total.astype(BF16)
+def local_bias_rows(ln_ref, w_ref, spread_ref):
+    heads = w_ref.shape[0]
+    w = w_ref[...]
+    if heads < 8:
+        w = jnp.concatenate([w, jnp.zeros((8 - heads, LANES), BF16)], axis=0)
+    values = lax.dot_general(w, ln_ref[...], NT, preferred_element_type=F32)
+    left = lax.broadcasted_iota(jnp.int32, (heads, LANES), 1) < RES
+    for two in range(8):
+        value = values[:heads, LANES * two:LANES * two + LANES]
+        turned = pltpu.roll(value, RES, 1)
+        spread_ref[pl.ds(2 * two, heads, stride=HELD), :] = jnp.where(left, value, turned)
+        spread_ref[pl.ds(2 * two + 1, heads, stride=HELD), :] = jnp.where(left, turned, value)
+    return spread_ref[pl.ds(0, HELD * heads), :].astype(BF16).reshape(heads, HELD, LANES)
 
 
 def triangle(zf_ref, ln_ref, w_ref, wo_ref, keep, bias_ref, pt_refs, gt_refs, others, ready):
-    def project(block, part):
+    def fill(block):
+        return project(ln_ref, pt_refs[block], lambda sl: w_ref[sl, :], pl.ds(BLOCK * block, BLOCK))
+
+    def done(block):
         def job():
-            pt_refs[block % 2][pl.ds(LANES * part, LANES), :] = lax.dot_general(
-                w_ref[pl.ds(LANES * part, LANES), :], ln_ref[pl.ds(BLOCK * block, BLOCK), :], NT,
-                preferred_element_type=F32).astype(BF16)
+            rows = pl.ds(BLOCK * block, BLOCK)
+            zf_ref[rows, :] = leave(gt_refs[block], zf_ref[rows, :], wo_ref[...]).astype(F32)
         return job
 
-    def leave(block):
-        def job():
-            update = jnp.dot(gt_refs[block % 2][...].T, wo_ref[...], preferred_element_type=F32)
-            rows = pl.ds(BLOCK * block, BLOCK)
-            zf_ref[rows, :] = (zf_ref[rows, :] + update).astype(BF16).astype(F32)
-        return job
-
-    for part in range(4):
-        project(0, part)()
+    for job in fill(0):
+        job()
     ready()
-    for block in range(4):
-        work = [leave(block - 1)] if block else []
-        if block < 3:
-            work += [project(block + 1, part) for part in range(4)]
-        attend_units(pt_refs[block % 2], gt_refs[block % 2], *others, 4, 32, [keep, keep], bias_ref, work)
-    leave(3)()
+    jobs = [(4 * block - 4, 4 * block - 1, fill(block)) for block in range(1, 4)]
+    jobs += [(4 * block + 4 + 3 * LAG, 4 * block + 5 + 3 * LAG, [done(block)]) for block in range(3)]
+    attend_stream([(pt_refs[block], gt_refs[block], [keep, keep]) for block in range(4)], others, 4, 32, bias_ref, jobs)
+    done(3)()
 
 
 def pair_stages(me, first, swap, own_ref, full_ref, z_ref, mask_ref, res_ref, weights, out_ref, next_ref, send_sem, recv_sem, scratch):
     wm_ref, wba_ref, wa_ref, woa_ref, wbb_ref, wb_ref, wob_ref = weights[:7]
     (full32_ref, o_ref, wt_ref, zf_ref, zt_ref, ln_ref, bias_ref, la_ref, ra_ref, lb_ref, rb_ref, zs_ref, zr_ref, nl_ref) = scratch[:14]
     att = scratch[14:]
-    pt_refs, gt_refs, others = att[0:2], att[2:4], att[4:7]
+    pt_refs, gt_refs, others = att[0:4], att[4:8], att[8:11]
     mine = pl.ds(pl.multiple_of(HELD * me, HELD), HELD)
 
     def keep():
@@ -515,7 +520,7 @@
         )[kind]
         return group_copies(me, first + kind, send_sem, recv_sem, source, target)
 
-    def outer():
+    def outer(arrive):
         mask = mask_ref[...].astype(F32).astype(BF16)
         norm = lax.dot_general(mask, mask_ref[mine, :].astype(F32).astype(BF16), NT, preferred_element_type=F32)
         full32_ref[:CELLS] = wm_ref[...].astype(F32).reshape(CELLS, LANES)
@@ -525,6 +530,7 @@
         else:
             wt_ref[...] = wm_ref[...].reshape(CELLS, LANES)
         w_turned = wt_ref[...].T
+        arrive()
         full32_ref[...] = full_ref[...].astype(F32).reshape(2048, LANES)
         own = own_ref[...].reshape(BLOCK, BLOCK)
         zeros = jnp.zeros((RES, LANES), BF16)
@@ -546,7 +552,7 @@
             rows = pl.ds(LANES * pair, LANES)
             zf_ref[rows, :] = z
             ln_ref[rows, :] = layer_norm(z)
-        la_ref[...] = local_bias_rows(ln_ref, wba_ref[...]).reshape(4, HELD, LANES)
+        la_ref[...] = local_bias_rows(ln_ref, wba_ref, zt_ref)
         start_all(exchange(0))
         ra_ref[:, mine, :] = la_ref[...]
 
@@ -560,7 +566,7 @@
         norm_all(zf_ref, ln_ref)
         start_all(exchange(1))
         zr_ref[mine] = zs_ref[:, mine, :]
-        lb_ref[...] = local_bias_rows(ln_ref, wbb_ref[...]).reshape(4, HELD, LANES)
+        lb_ref[...] = local_bias_rows(ln_ref, wbb_ref, zt_ref)
         start_all(exchange(2))
         rb_ref[:, mine, :] = lb_ref[...]
 
@@ -580,7 +586,7 @@
         out_ref[...] = zf_ref[...].astype(BF16).reshape(HELD, RES, LANES)
         if next_ref is not None:
             norm_all(zf_ref, ln_ref)
-            nl_ref[...] = local_bias_rows(ln_ref, weights[7][...]).reshape(HELD, HELD, LANES)
+            nl_ref[...] = local_bias_rows(ln_ref, weights[7], zt_ref)
             start_all(exchange(3))
             next_ref[:, mine, :] = nl_ref[...]
 
@@ -607,7 +613,7 @@
         pltpu.VMEM((HELD, RES, LANES), BF16),
         pltpu.VMEM((RES, HELD, LANES), BF16),
         pltpu.VMEM((HELD, HELD, LANES), BF16),
-    ] + attend_scratch(4, 32, RES, LANES)[1:]
+    ] + attend_scratch(4, 32, RES, 4)
 
 
 def norm_all(zf_ref, ln_ref):

time: 137 us -> 135 us (0.985)
  Pallas kernels: 132 us -> 130 us
    pallas_call x1, Pallas kernels: 33.7 us -> 31.6 us  [row_last(): pl.pallas_call(row_last_kernel, grid=(1,), in_specs=[whole(a) for a in ar...]
where the time goes in v7:
time: 135 us
  Pallas kernels  130 us (96%)
  local copies, waits for them, and re-layouts  3.46 us (3%)
    pallas_call x1, Pallas kernels, column_pair(): pl.pallas_call(col_kernel, grid=(1,), in_specs=[whole(a) for a in args] +...  65.9 us
    pallas_call x1, Pallas kernels, row_first(): pl.pallas_call(row_first_kernel, grid=(1,), in_specs=[whole(x), whole(z),...  32.9 us
    pallas_call x1, Pallas kernels, row_last(): pl.pallas_call(row_last_kernel, grid=(1,), in_specs=[whole(a) for a in ar...  31.6 us
    unnamed x4, local copies, waits for them, and re-layouts  3.46 us

profile of v7, /device:TPU:0, one launch (start us, length us, event | category | flops | bytes accessed | tf_op | source)
XLA Modules:
  0.0 134.6 jit_solution(3967280687527340923)
XLA Ops:
  0.6 32.9 %row_first.1.x_ref = bf16[128,16,384]{2,1,0:T(8,128)(2,1)} custom-call(bf16[32,64,384]{2,1,0:T(8,128)(2,1)} %x_ref.1, bf16[16,64,128]{2,1,0:T(8,128)(2,1)} %z_ref.3, s32[64,128]{1,0:T(8,128)} %bitcast.42, bf16[2,16,128]{2,1,0:T(8,128)(2,1)} %bitcast.45, bf16[2,1536,384]{2,1,0:T(8,128)(2,1)} %bitcast.26, bf16[2,384,384]{2,1,0:T(8,128)(2,1)} %bitcast.29), custom_call_target="tpu_custom_call" | custom-call | flops 10000000000 | bytes 4194304 | tf_op jit(solution)/shard_map/row_first/pallas_call | solution.py:246
  33.5 65.9 %col_pair.1 = (bf16[64,32,384]{2,1,0:T(8,128)(2,1)}, bf16[8,32,256]{2,1,0:T(8,128)(2,1)}, bf16[64,32,128]{2,1,0:T(8,128)(2,1)}, bf16[16,64,128]{2,1,0:T(8,128)(2,1)}, bf16[16,64,128]{2,1,0:T(8,128)(2,1)}) custom-call(bf16[128,16,384]{2,1,0:T(8,128)(2,1)} %row_first.1.x_ref, s32[64,128]{1,0:T(8,128)} %bitcast.43, bf16[2,1536,384]{2,1,0:T(8,128)(2,1)} %bitcast.25, ...), custom_call_target="tpu_custom_call" | custom-call | flops 10000000000 | bytes 4194304 | tf_op jit(solution)/shard_map/col_pair/pallas_call | solution.py:410
  99.5 31.6 %row_last.1 = (bf16[32,64,384]{2,1,0:T(8,128)(2,1)}, bf16[16,64,128]{2,1,0:T(8,128)(2,1)}) custom-call(bf16[64,32,384]{2,1,0:T(8,128)(2,1)} %get-tuple-element.7.x_ref, bf16[16,64,128]{2,1,0:T(8,128)(2,1)} %get-tuple-element.8.rows_ref, bf16[8,32,256]{2,1,0:T(8,128)(2,1)} %get-tuple-element.9.own_ref, bf16[64,32,128]{2,1,0:T(8,128)(2,1)} %get-tuple-element.10.full_ref, ...), custom_call_target="tpu_custom_call" | custom-call | flops 10000000000 | bytes 4194304 | tf_op jit(solution)/shard_map/row_last/pallas_call | solution.py:307
  131.1 0.0 copy-start
  131.1 2.8 %copy.21 = bf16[32,64,384]{2,1,0:T(8,128)(2,1)} copy(bf16[32,64,384]{2,1,0:T(8,128)(2,1)} %get-tuple-element.14) | data formatting | bytes 3145728
  133.9 0.0 copy-done
  133.9 0.7 copy.22
Async XLA Ops:
  131.1 2.8 %copy-start = (bf16[16,64,128]{2,1,0:T(8,128)(2,1)S(1)}, bf16[16,64,128]{2,1,0:T(8,128)(2,1)}, u32[]{:S(2)}) copy-start(bf16[16,64,128]{2,1,0:T(8,128)(2,1)} %get-tuple-element.15) | copy-start | bytes 786436

commit v8 on v7

--- a/solution.py
+++ b/solution.py
@@ -43,6 +43,7 @@
     rows = 2 * dim
     pairs = heads // 2
     each = 2 * pairs
+    keys = pl.ds(0, LANES if bias_ref is None else RES)
     units = each * len(blocks)
     up, low = half_masks(rows, dim)
     scale = dim ** -0.5 * LOG2E
@@ -67,17 +68,17 @@
             lg = logits2[:, LANES * half:LANES * half + LANES]
             if bias_ref is not None:
                 lg = jnp.where(left, lg[:RES], lg[RES:])
-            lg_ref[unit % SLOTS, half] = lg
+            lg_ref[unit % SLOTS, half, pl.ds(0, lg.shape[0])] = lg
 
     def soften(unit):
         (_, _, keep), _, _ = place(unit)
         for half in range(2):
-            lg = lg_ref[unit % SLOTS, half] * scale
+            lg = lg_ref[unit % SLOTS, half, keys] * scale
             if bias_ref is not None:
                 lg = lg + bias_ref[2 * (unit % pairs) + half]
             lg = jnp.where(keep[unit % each // pairs], lg, NEG)
             e = jnp.exp2(lg - jnp.max(lg, axis=0, keepdims=True))
-            pr_ref[unit % SLOTS, half] = (e * (1.0 / jnp.sum(e, axis=0, keepdims=True))).astype(BF16)
+            pr_ref[unit % SLOTS, half, keys] = (e * (1.0 / jnp.sum(e, axis=0, keepdims=True))).astype(BF16)
 
     def mix(unit):
         (pt_ref, gt_ref, _), ln, r = place(unit)
@@ -85,7 +86,7 @@
         g = pt_ref[pl.ds(3 * width + r, rows), ln]
         probs = []
         for half in range(2):
-            p = pr_ref[unit % SLOTS, half]
+            p = pr_ref[unit % SLOTS, half, keys]
             probs += [p] if bias_ref is None else [p * left_b, p * right_b]
         att = jnp.dot(jnp.concatenate([v * up, v * low], axis=1), jnp.concatenate(probs, axis=0), preferred_element_type=F32)
         gt_ref[pl.ds(r, rows), ln] = (att * jax.nn.sigmoid(g.astype(F32))).astype(BF16)
@@ -171,59 +172,6 @@
     return [jnp.where(left, column[2 * blk], column[2 * blk + 1]) > 0.5 for blk in range(2)]
 
 
-def row_first_kernel(x_ref, z_ref, mask_ref, wb_ref, w_ref, wo_ref, out_ref, mo_ref, lnz_ref, nl_ref, rows_ref, bias_ref, spread_ref,
-                     send_sem, recv_sem, *scratch):
-    me = lax.axis_index('dap')
-    mine = pl.ds(pl.multiple_of(HELD * me, HELD), HELD)
-    greet(me)
-    for part in range(4):
-        lnz_ref[pl.ds(BLOCK * part, BLOCK), :] = layer_norm(z_ref[pl.ds(4 * part, 4)].reshape(BLOCK, LANES))
-    nl_ref[...] = local_bias_rows(lnz_ref, wb_ref, spread_ref)
-    meet()
-    copies = group_copies(me, 8, send_sem, recv_sem, lambda peer: nl_ref, rows_ref.at[:, mine, :])
-    start_all(copies)
-    rows_ref[:, mine, :] = nl_ref[...]
-
-    def ready():
-        finish_all(copies)
-        bias_by_query(rows_ref, bias_ref)
-
-    def moves(block):
-        return group_copies(
-            me, block, send_sem, recv_sem,
-            lambda peer: mo_ref.at[pl.ds(4 * block, 4), pl.ds(pl.multiple_of(HELD * peer, HELD), HELD), :],
-            out_ref.at[pl.ds(32 * me + 4 * block, 4)])
-
-    def emit(block):
-        start_all(moves(block))
-        out_ref[pl.ds(32 * me + 4 * block, 4)] = mo_ref[pl.ds(4 * block, 4), mine, :]
-
-    def aside(turn):
-        @pl.when(turn >= 2)
-        def _():
-            emit(2 * turn - 3)
-
-        @pl.when(turn >= 1)
-        def _():
-            emit(2 * turn - 2)
-
-    def finish(block, out):
-        mo_ref[pl.ds(4 * block, 4)] = out.reshape(4, RES, WIDE)
-
-    attend_blocks(8, scratch, lambda at: x_ref[pl.ds(at * 4, 4)].astype(F32).reshape(BLOCK, WIDE),
-                  lambda at: lambda sl: w_ref[sl, :], lambda at: wo_ref[...],
-                  lambda at: row_keep(mask_ref, 32 * me + 4 * at), bias_ref, finish, ready, aside)
-    emit(5)
-    emit(6)
-    emit(7)
-
-    def drain(block, carry):
-        finish_all(moves(block))
-        return carry
-
-    lax.fori_loop(0, 8, drain, 0)
-
-
 def bias_by_query(rows_ref, bias_ref):
     for head in range(rows_ref.shape[0]):
         turned = (rows_ref[head].astype(F32) * LOG2E).T[:RES]
@@ -242,197 +190,234 @@
     return pl.BlockSpec(array.shape, lambda i: (0,) * array.ndim)
 
 
-def row_first(x, z, mask, wb, w, wo):
-    return pl.pallas_call(
-        row_first_kernel,
-        grid=(1,),
-        in_specs=[whole(x), whole(z), whole(mask)] + [of_layer(a, 0) for a in (wb, w, wo)],
-        out_specs=VMEM,
-        out_shape=jax.ShapeDtypeStruct((LANES, HELD, WIDE), BF16),
-        scratch_shapes=[
-            pltpu.VMEM((32, RES, WIDE), BF16),
-            pltpu.VMEM((CELLS, LANES), BF16),
-            pltpu.VMEM((HELD, HELD, LANES), BF16),
-            pltpu.VMEM((HELD, RES, LANES), BF16),
-            pltpu.VMEM((HELD, RES, LANES), F32),
-            pltpu.VMEM((BLOCK, LANES), F32),
-            pltpu.SemaphoreType.DMA((27,)),
-            pltpu.SemaphoreType.DMA((27,)),
-        ] + wide_scratch(RES),
-        compiler_params=pltpu.CompilerParams(collective_id=0, has_side_effects=True),
-        cost_estimate=pl.CostEstimate(flops=10 ** 10, bytes_accessed=2 ** 22, transcendentals=0),
-        name="row_first",
-    )(x, z, mask, wb, w, wo)
-
-
-def row_last_kernel(x_ref, rows_ref, own_ref, full_ref, z_ref, mask_ref, res_ref, w_ref, wo_ref, wm_ref, wba_ref, wa_ref, woa_ref,
-                    wbb_ref, wb_ref, wob_ref, out_ref, z_out_ref, wide_ref, m_ref, bias_ref, send_sem, recv_sem, *scratch):
+def turn_tokens(x_ref, wide_ref, put):
+    outer, inner = x_ref.shape[:2]
+    for part in range(3):
+        wide_ref[part] = x_ref[:, :, pl.ds(LANES * part, LANES)].astype(F32).reshape(outer * inner, LANES)
+
+    def one(row, carry):
+        for part in range(3):
+            put(row, pl.ds(LANES * part, LANES), wide_ref[part, pl.ds(row, outer, stride=inner), :].astype(BF16))
+        return carry
+
+    lax.fori_loop(0, inner, one, 0, unroll=4)
+
+
+def kernel(x_ref, z_ref, mask_ref, res_ref, wrb_ref, wr_ref, wro_ref, wsb_ref, ws_ref, wso_ref, web_ref, we_ref, weo_ref, wnb_ref,
+           wc_hbm, wco_hbm, wp_hbm, wm_hbm, wr_hbm, wro_hbm, out_ref, z_out_ref,
+           wc_ref, wco_ref, wp_ref, wm_ref, wl_ref, wlo_ref, mo_ref, in_ref, wide_ref, m_ref, back_ref, ml_ref,
+           rows_ref, bias_ref, part_ref, keys_ref, own1_ref, own2_ref, full1_ref, full2_ref, zc_ref, next_ref,
+           send_sem, recv_sem, load_sem, *scratch):
     me = lax.axis_index('dap')
     greet(me)
+    loads = [pltpu.make_async_copy(source, target, load_sem.at[n]) for n, (source, target) in enumerate((
+        (wc_hbm, wc_ref), (wco_hbm, wco_ref), (wp_hbm, wp_ref), (wm_hbm, wm_ref), (wr_hbm.at[1], wl_ref), (wro_hbm.at[1], wlo_ref)))]
+    start_all(loads)
+    mine = pl.ds(pl.multiple_of(HELD * me, HELD), HELD)
+    wide, pair = scratch[:8], scratch[8:]
+    zf_ref, zt_ref, ln_ref, nl_ref = pair[3], pair[4], pair[5], pair[13]
+
+    for part in range(4):
+        ln_ref[pl.ds(BLOCK * part, BLOCK), :] = layer_norm(z_ref[pl.ds(4 * part, 4)].reshape(BLOCK, LANES))
+    nl_ref[...] = local_bias_rows(ln_ref, wrb_ref, zt_ref)
     meet()
-    outer, along, across, _ = pair_stages(
-        me, 0, False, own_ref, full_ref, z_ref, mask_ref, res_ref, (wm_ref, wba_ref, wa_ref, woa_ref, wbb_ref, wb_ref, wob_ref),
-        z_out_ref, None, send_sem, recv_sem, scratch[8:])
-    outer(lambda: None)
-    turn_tokens(x_ref, wide_ref, m_ref)
-    bias_ref[...] = rows_ref[...].astype(F32) * LOG2E
-
-    def finish(block, out):
-        out_ref[pl.ds(4 * block, 4)] = out.reshape(4, RES, WIDE)
-
-    def aside(turn):
-        pl.when(turn == 1)(along)
-        pl.when(turn == 2)(across)
-
-    attend_blocks(8, scratch[:8], lambda at: m_ref[pl.ds(at * 4, 4)].astype(F32).reshape(BLOCK, WIDE),
-                  lambda at: lambda sl: w_ref[sl, :], lambda at: wo_ref[...],
-                  lambda at: row_keep(mask_ref, 32 * me + 4 * at), bias_ref, finish, lambda: None, aside)
-
-
-def turn_tokens(x_ref, wide_ref, m_ref):
-    outer, inner = x_ref.shape[:2]
-    for part in range(3):
-        lanes = pl.ds(LANES * part, LANES)
-        wide_ref[part] = x_ref[:, :, lanes].astype(F32).reshape(outer * inner, LANES)
-
-    def one(row, carry):
-        for part in range(3):
-            m_ref[row, :, pl.ds(LANES * part, LANES)] = wide_ref[part, pl.ds(row, outer, stride=inner), :].astype(BF16)
-        return carry
-
-    lax.fori_loop(0, inner, one, 0, unroll=2)
-
-
-def row_last(args, weights):
-    return pl.pallas_call(
-        row_last_kernel,
-        grid=(1,),
-        in_specs=[whole(a) for a in args] + [of_layer(a, 1) for a in weights],
-        out_specs=[VMEM] * 2,
-        out_shape=[jax.ShapeDtypeStruct((32, RES, WIDE), BF16), jax.ShapeDtypeStruct((HELD, RES, LANES), BF16)],
-        scratch_shapes=[
-            pltpu.VMEM((3, 2048, LANES), F32),
-            pltpu.VMEM((32, RES, WIDE), BF16),
-            pltpu.VMEM((HELD, RES, LANES), F32),
-            pltpu.SemaphoreType.DMA((12,)),
-            pltpu.SemaphoreType.DMA((12,)),
-        ] + wide_scratch(RES) + pair_scratch(),
-        compiler_params=pltpu.CompilerParams(collective_id=2, has_side_effects=True),
-        cost_estimate=pl.CostEstimate(flops=10 ** 10, bytes_accessed=2 ** 22, transcendentals=0),
-        name="row_last",
-    )(*args, *weights)
-
-
-def col_kernel(x_ref, mask_ref, w_ref, wo_ref, wp_ref, z_ref, res_ref, wm_ref, wba_ref, wa_ref, woa_ref, wbb_ref, wb_ref, wob_ref, wn_ref,
-               out_ref, own2_ref, full2_ref, z_out_ref, next_ref, own1_ref, full1_ref,
-               wide_ref, m_ref, part_ref, keys_ref, send_sem, recv_sem, *scratch):
-    me = lax.axis_index('dap')
-    greet(me)
-    turn_tokens(x_ref, wide_ref, m_ref.at[0])
-    meet()
-    mine = pl.ds(pl.multiple_of(HELD * me, HELD), HELD)
+    copies = group_copies(me, 9, send_sem, recv_sem, lambda peer: nl_ref, rows_ref.at[:, mine, :])
+    start_all(copies)
+    rows_ref[:, mine, :] = nl_ref[...]
+
+    def row_ready():
+        finish_all(copies)
+        bias_by_query(rows_ref, bias_ref)
+
+    def moves(block):
+        return group_copies(me, block, send_sem, recv_sem, lambda peer: mo_ref.at[2 * peer, pl.ds(4 * block, 4)],
+                            in_ref.at[0, pl.ds(32 * me + 4 * block, 4)])
+
+    def later_moves():
+        return group_copies(me, 8, send_sem, recv_sem, lambda peer: mo_ref.at[2 * peer + 1], in_ref.at[1, pl.ds(32 * me, 32)])
+
+    def row_aside(turn):
+        pl.when(turn >= 2)(lambda: start_all(moves(2 * turn - 3)))
+        pl.when(turn >= 1)(lambda: start_all(moves(2 * turn - 2)))
+
+    def row_finish(block, out):
+        out = out.astype(F32).reshape(4, 8, 8, WIDE)
+        for group in range(8):
+            mo_ref[group, pl.ds(4 * block, 4)] = out[:, group].astype(BF16)
+
+    attend_blocks(8, wide, lambda at: x_ref[pl.ds(at * 4, 4)].astype(F32).reshape(BLOCK, WIDE),
+                  lambda at: lambda sl: wr_ref[sl, :], lambda at: wro_ref[...],
+                  lambda at: row_keep(mask_ref, 32 * me + 4 * at), bias_ref, row_finish, row_ready, row_aside)
+    for block in range(5, 8):
+        start_all(moves(block))
+    start_all(later_moves())
+    for half in range(2):
+        in_ref[half, pl.ds(32 * me, 32)] = mo_ref[2 * me + half]
+
+    finish_all(loads)
     keys_ref[...] = mask_ref[mine, :].astype(F32).T
 
-    def keep(at):
+    def take(half):
+        def put(row, lanes, value):
+            m_ref[0, 8 * half + row, :, lanes] = value
+        turn_tokens(in_ref.at[half], wide_ref, put)
+
+    def drain(count, copies_of):
+        def one(n, carry):
+            finish_all(copies_of(n))
+            return carry
+        lax.fori_loop(0, count, one, 0)
+
+    def col_keep(at):
         return [jnp.broadcast_to(pick_column(keys_ref[...], at % 8 * 2 + blk), (LANES, LANES)) > 0.5 for blk in range(2)]
 
-    def finish(block, out):
-        layer, pair = block // 8, block % 8
-        m_ref[layer + 1, pl.ds(pair * 2, 2)] = out.reshape(2, LANES, WIDE)
+    def col_finish(block, out):
+        layer, two = block // 8, block % 8
+        m_ref[layer + 1, pl.ds(two * 2, 2)] = out.reshape(2, LANES, WIDE)
         ac = lax.dot_general(wp_ref[layer], layer_norm(out), NT, preferred_element_type=F32)
-        ac = (ac * jnp.concatenate([mask_ref[pl.ds(HELD * me + 2 * pair + blk, 1), :] for blk in range(2)], axis=1).astype(F32)).astype(BF16)
+        ac = (ac * jnp.concatenate([mask_ref[pl.ds(HELD * me + 2 * two + blk, 1), :] for blk in range(2)], axis=1).astype(F32)).astype(BF16)
         parts = (ac[:32], ac[32:])
-        own1_ref[pair] = jnp.where(layer == 0, parts[0].astype(F32), own1_ref[pair].astype(F32)).astype(BF16)
-        own2_ref[pair] = parts[1]
+        own1_ref[two] = jnp.where(layer == 0, parts[0].astype(F32), own1_ref[two].astype(F32)).astype(BF16)
+        own2_ref[two] = parts[1]
         for blk in range(2):
             lanes = slice(LANES * blk, LANES * blk + LANES)
             part_ref[block, blk] = jnp.where(layer == 0, parts[1][:, lanes].astype(F32), parts[0][:, lanes].astype(F32)).astype(BF16)
 
     def part_copies(block, full_ref):
-        return group_copies(me, block, send_sem, recv_sem, lambda peer: part_ref.at[block],
+        return group_copies(me, 10 + block, send_sem, recv_sem, lambda peer: part_ref.at[block],
                             full_ref.at[pl.ds(HELD * me + block % 8 * 2, 2)])
 
-    def seq_copies(pair):
+    def seq_copies(two):
         return group_copies(
-            me, HELD + pair, send_sem, recv_sem,
-            lambda peer: m_ref.at[2, pl.ds(2 * pair, 2), pl.ds(pl.multiple_of(32 * peer, 32), 32), :],
-            out_ref.at[pl.ds(HELD * me + 2 * pair, 2)])
+            me, 26 + two, send_sem, recv_sem,
+            lambda peer: m_ref.at[2, pl.ds(2 * two, 2), pl.ds(pl.multiple_of(32 * peer, 32), HELD), :],
+            back_ref.at[0, pl.ds(HELD * me + 2 * two, 2)])
+
+    def later_seqs():
+        return group_copies(
+            me, 34, send_sem, recv_sem, lambda peer: m_ref.at[2, :, pl.ds(pl.multiple_of(32 * peer + HELD, HELD), HELD), :],
+            back_ref.at[1, mine])
+
+    def emit(block):
+        def first():
+            start_all(part_copies(block, full1_ref))
+            full1_ref[pl.ds(HELD * me + 2 * block, 2)] = part_ref[block]
+
+        def second():
+            start_all(part_copies(block, full2_ref) + seq_copies(block - 8))
+            full2_ref[pl.ds(HELD * me + 2 * (block - 8), 2)] = part_ref[block]
+
+        if isinstance(block, int):
+            second()
+        else:
+            pl.when(jnp.logical_and(block >= 0, block < 8))(first)
+            pl.when(block >= 8)(second)
 
     outer, along, across, close = pair_stages(
-        me, 24, True, own1_ref, full1_ref, z_ref, mask_ref, res_ref, (wm_ref, wba_ref, wa_ref, woa_ref, wbb_ref, wb_ref, wob_ref, wn_ref),
-        z_out_ref, next_ref, send_sem, recv_sem, scratch[8:])
-
-    def drain_parts(start, full_ref):
-        def one(pair, carry):
-            finish_all(part_copies(start + pair, full_ref))
-            return carry
-        lax.fori_loop(0, 8, one, 0)
-
-    def emit_first(block):
-        start_all(part_copies(block, full1_ref))
-        full1_ref[pl.ds(HELD * me + 2 * block, 2)] = part_ref[block]
-
-    def emit_second(block):
-        pair = block - 8
-        start_all(part_copies(block, full2_ref) + seq_copies(pair))
-        full2_ref[pl.ds(HELD * me + 2 * pair, 2)] = part_ref[block]
-        out_ref[pl.ds(HELD * me + 2 * pair, 2)] = m_ref[2, pl.ds(2 * pair, 2), pl.ds(pl.multiple_of(32 * me, 32), 32), :]
-
-    def emit_any(block):
-        pl.when(jnp.logical_and(block >= 0, block < 8))(lambda: emit_first(block))
-        pl.when(block >= 8)(lambda: emit_second(block))
-
-    def aside(turn):
-        emit_any(2 * turn - 3)
-        emit_any(2 * turn - 2)
-        pl.when(turn == 5)(lambda: outer(lambda: drain_parts(0, full1_ref)))
-        pl.when(turn == 6)(along)
-        pl.when(turn == 7)(across)
-
-    attend_blocks(16, scratch[:8], lambda at: m_ref[at // 8, pl.ds(at % 8 * 2, 2)].astype(F32).reshape(BLOCK, WIDE),
-                  lambda at: lambda sl: w_ref[at // 8, sl, :], lambda at: wo_ref[at // 8],
-                  keep, None, finish, lambda: None, aside)
-    emit_second(13)
-    emit_second(14)
-    emit_second(15)
-
-    close()
-    drain_parts(8, full2_ref)
-
-    def drain(pair, carry):
-        finish_all(seq_copies(pair))
-        return carry
-
-    lax.fori_loop(0, 8, drain, 0)
-
-
-def column_pair(args, weights, w_next):
+        me, 35, True, own1_ref, full1_ref, z_ref, mask_ref, res_ref,
+        (wm_ref.at[0], wsb_ref.at[0], ws_ref.at[0], wso_ref.at[0], web_ref.at[0], we_ref.at[0], weo_ref.at[0], wnb_ref),
+        zc_ref, next_ref, send_sem, recv_sem, pair)
+
+    def second_half():
+        finish_all(later_moves())
+        take(1)
+
+    def col_aside(turn):
+        emit(2 * turn - 3)
+        emit(2 * turn - 2)
+        pl.when(turn == 1)(second_half)
+        pl.when(turn == 6)(lambda: outer(lambda: drain(8, lambda n: part_copies(n, full1_ref))))
+        pl.when(turn == 7)(along)
+
+    drain(8, moves)
+    take(0)
+    attend_blocks(16, wide, lambda at: m_ref[at // 8, pl.ds(at % 8 * 2, 2)].astype(F32).reshape(BLOCK, WIDE),
+                  lambda at: lambda sl: wc_ref[at // 8, sl, :], lambda at: wco_ref[at // 8],
+                  col_keep, None, col_finish, lambda: None, col_aside)
+    for block in range(13, 16):
+        emit(block)
+    start_all(later_seqs())
+    for half in range(2):
+        back_ref[half, mine] = m_ref[2, :, pl.ds(pl.multiple_of(32 * me + HELD * half, HELD), HELD), :]
+    across()
+
+    outer, along_2, across_2, _ = pair_stages(
+        me, 39, False, own2_ref, full2_ref, zc_ref, mask_ref, res_ref,
+        (wm_ref.at[1], web_ref.at[1], we_ref.at[1], weo_ref.at[1], wsb_ref.at[1], ws_ref.at[1], wso_ref.at[1]),
+        z_out_ref, None, send_sem, recv_sem, pair)
+    outer(lambda: drain(8, lambda n: part_copies(n + 8, full2_ref)))
+
+    def take_back(half):
+        def put(row, lanes, value):
+            ml_ref[HELD * half + row, :, lanes] = value
+        turn_tokens(back_ref.at[half], wide_ref, put)
+
+    def last_half():
+        finish_all(later_seqs())
+        take_back(1)
+
+    def last_aside(turn):
+        pl.when(turn == 1)(along_2)
+        pl.when(turn == 1)(last_half)
+        pl.when(turn == 2)(across_2)
+
+    def last_ready():
+        close()
+        bias_ref[...] = next_ref[...].astype(F32) * LOG2E
+
+    def last_finish(block, out):
+        out_ref[pl.ds(4 * block, 4)] = out.reshape(4, RES, WIDE)
+
+    drain(8, seq_copies)
+    take_back(0)
+    attend_blocks(8, wide, lambda at: ml_ref[pl.ds(at * 4, 4)].astype(F32).reshape(BLOCK, WIDE),
+                  lambda at: lambda sl: wl_ref[sl, :], lambda at: wlo_ref[...],
+                  lambda at: row_keep(mask_ref, 32 * me + 4 * at), bias_ref, last_finish, last_ready, last_aside)
+
+
+def run_all(m, z, mask, res_mask, row, tri, streamed):
+    w_row_bias, w_row_in, w_row_out = row
+    args = (m, z, mask, res_mask) + row + tri + (w_row_bias,) + streamed
+    specs = [whole(a) for a in args[:4]] + [of_layer(a, 0) for a in row] + [whole(a) for a in tri] + [of_layer(w_row_bias, 1)]
+    specs += [pl.BlockSpec(memory_space=pl.ANY)] * len(streamed)
+    vmem = lambda *shape: pltpu.VMEM(shape, BF16)
     return pl.pallas_call(
-        col_kernel,
+        kernel,
         grid=(1,),
-        in_specs=[whole(a) for a in args] + [of_layer(a, 0) for a in weights] + [of_layer(w_next, 1)],
-        out_specs=[VMEM] * 5,
-        out_shape=[
-            jax.ShapeDtypeStruct((RES, 32, WIDE), BF16),
-            jax.ShapeDtypeStruct((8, 32, BLOCK), BF16),
-            jax.ShapeDtypeStruct((RES, 32, LANES), BF16),
-            jax.ShapeDtypeStruct((HELD, RES, LANES), BF16),
-            jax.ShapeDtypeStruct((HELD, RES, LANES), BF16),
-        ],
+        in_specs=specs,
+        out_specs=[VMEM] * 2,
+        out_shape=[jax.ShapeDtypeStruct(m.shape, BF16), jax.ShapeDtypeStruct(z.shape, BF16)],
         scratch_shapes=[
-            pltpu.VMEM((8, 32, BLOCK), BF16),
-            pltpu.VMEM((RES, 32, LANES), BF16),
-            pltpu.VMEM((3, 2048, LANES), F32),
-            pltpu.VMEM((3, HELD, LANES, WIDE), BF16),
-            pltpu.VMEM((HELD, 2, 32, LANES), BF16),
+            vmem(2, 4 * WIDE, WIDE),
+            vmem(2, WIDE, WIDE),
+            vmem(2, RES, WIDE),
+            vmem(2, CELLS, LANES),
+            vmem(4 * WIDE, WIDE),
+            vmem(WIDE, WIDE),
+            vmem(8, 32, 8, WIDE),
+            vmem(2, LANES, 8, WIDE),
+            pltpu.VMEM((3, CELLS, LANES), F32),
+            vmem(3, HELD, LANES, WIDE),
+            vmem(2, RES, HELD, WIDE),
+            vmem(32, RES, WIDE),
+            vmem(HELD, RES, LANES),
+            pltpu.VMEM((HELD, RES, LANES), F32),
+            vmem(HELD, 2, 32, LANES),
             pltpu.VMEM((LANES, HELD), F32),
-            pltpu.SemaphoreType.DMA((84,)),
-            pltpu.SemaphoreType.DMA((84,)),
+            vmem(8, 32, BLOCK),
+            vmem(8, 32, BLOCK),
+            vmem(RES, 32, LANES),
+            vmem(RES, 32, LANES),
+            vmem(HELD, RES, LANES),
+            vmem(HELD, RES, LANES),
+            pltpu.SemaphoreType.DMA((126,)),
+            pltpu.SemaphoreType.DMA((126,)),
+            pltpu.SemaphoreType.DMA((6,)),
         ] + wide_scratch(LANES) + pair_scratch(),
-        compiler_params=pltpu.CompilerParams(collective_id=1, has_side_effects=True),
+        compiler_params=pltpu.CompilerParams(collective_id=0, has_side_effects=True),
         cost_estimate=pl.CostEstimate(flops=10 ** 10, bytes_accessed=2 ** 22, transcendentals=0),
-        name="col_pair",
-    )(*args, *weights, w_next)
+        name="evoformer",
+    )(*args)
 
 
 def greet(me):
@@ -635,13 +620,10 @@
         mask = mask.T
         res_mask = res_mask.reshape(1, RES)
 
-        m = row_first(m, z, mask, w_row_bias, w_row_in, w_row_out)
-        m, own, full, z, row_bias = column_pair(
-            (m, mask, w_col_in, w_col_out, w_opm_in, z, res_mask),
-            (w_opm_out, w_ts_bias, w_ts_in, w_ts_out, w_te_bias, w_te_in, w_te_out), w_row_bias)
-        m, z = row_last(
-            (m, row_bias, own, full, z, mask, res_mask),
-            (w_row_in, w_row_out, w_opm_out, w_te_bias, w_te_in, w_te_out, w_ts_bias, w_ts_in, w_ts_out))
+        m, z = run_all(
+            m, z, mask, res_mask, (w_row_bias, w_row_in, w_row_out),
+            (w_ts_bias, w_ts_in, w_ts_out, w_te_bias, w_te_in, w_te_out),
+            (w_col_in, w_col_out, w_opm_in, w_opm_out, w_row_in, w_row_out))
         return m, z
 
     in_specs = (P(('data', 'dap')), P(('data', 'dap')), P('data'), P('data')) + (P(),) * 13

time: 135 us -> 114 us (0.84)
  Pallas kernels: 130 us -> 109 us
    pallas_call x3 -> x1, Pallas kernels: 130 us -> 109 us  [run_all(): pl.pallas_call(kernel, grid=(1,), in_specs=specs, out_specs=[VMEM] * 2, o...]
where the time goes in v8:
time: 114 us; the launch traced here: 113 us
  Pallas kernels  109 us (96%)
  local copies, waits for them, and re-layouts  3.46 us (3%)
    pallas_call x1, Pallas kernels, run_all(): pl.pallas_call(kernel, grid=(1,), in_specs=specs, out_specs=[VMEM] * 2, o...  109 us
    unnamed x4, local copies, waits for them, and re-layouts  3.46 us

profile of v8, /device:TPU:0, one launch (start us, length us, event | category | flops | bytes accessed | tf_op | source)
XLA Modules:
  0.0 113.4 jit_solution(10079270648937145339)
XLA Ops:
  0.6 109.3 %evoformer.1 = (bf16[32,64,384]{2,1,0:T(8,128)(2,1)}, bf16[16,64,128]{2,1,0:T(8,128)(2,1)}) custom-call(bf16[32,64,384]{2,1,0:T(8,128)(2,1)} %x_ref.1, bf16[16,64,128]{2,1,0:T(8,128)(2,1)} %z_ref.1, s32[64,128]{1,0:T(8,128)} %bitcast.37, s32[1,64]{1,0:T(1,128)} %bitcast.42, bf16[2,16,128]{2,1,0:T(8,128)(2,1)} %bitcast.38, bf16[2,1536,384]{2,1,0:T(8,128)(2,1)} %bitcast.25, ...), custom_call_target="tpu_custom_call" | custom-call | flops 10000000000 | bytes 4194304 | tf_op jit(solution)/shard_map/evoformer/pallas_call | solution.py:384
  109.9 0.0 copy-start
  109.9 2.8 %copy.21 = bf16[32,64,384]{2,1,0:T(8,128)(2,1)} copy(bf16[32,64,384]{2,1,0:T(8,128)(2,1)} %get-tuple-element.4) | data formatting | bytes 3145728
  112.7 0.0 copy-done
  112.7 0.7 copy.22
Async XLA Ops:
  109.9 2.8 %copy-start = (bf16[16,64,128]{2,1,0:T(8,128)(2,1)S(1)}, bf16[16,64,128]{2,1,0:T(8,128)(2,1)}, u32[]{:S(2)}) copy-start(bf16[16,64,128]{2,1,0:T(8,128)(2,1)} %get-tuple-element.5) | copy-start | bytes 786436

commit v9 on v8

--- a/solution.py
+++ b/solution.py
@@ -14,6 +14,7 @@
 LAG = 2
 SLOTS = 4
 NT = (((1,), (1,)), ((), ()))
+SEQS = 32
 LANES = 128
 RES = 64
 BLOCK = 256
@@ -172,12 +173,6 @@
     return [jnp.where(left, column[2 * blk], column[2 * blk + 1]) > 0.5 for blk in range(2)]
 
 
-def bias_by_query(rows_ref, bias_ref):
-    for head in range(rows_ref.shape[0]):
-        turned = (rows_ref[head].astype(F32) * LOG2E).T[:RES]
-        bias_ref[head] = jnp.concatenate([turned, turned], axis=1)
-
-
 VMEM = pl.BlockSpec(memory_space=pltpu.VMEM)
 
 
@@ -231,14 +226,18 @@
 
     def moves(block):
         return group_copies(me, block, send_sem, recv_sem, lambda peer: mo_ref.at[2 * peer, pl.ds(4 * block, 4)],
-                            in_ref.at[0, pl.ds(32 * me + 4 * block, 4)])
-
-    def later_moves():
-        return group_copies(me, 8, send_sem, recv_sem, lambda peer: mo_ref.at[2 * peer + 1], in_ref.at[1, pl.ds(32 * me, 32)])
+                            in_ref.at[0, pl.ds(SEQS * me + 4 * block, 4)])
+
+    def later_moves(part):
+        start, count, kind = ((0, 4, 8), (4, 4, 42), (8, 24, 43))[part]
+        return group_copies(me, kind, send_sem, recv_sem, lambda peer: mo_ref.at[2 * peer + 1, pl.ds(start, count)],
+                            in_ref.at[1, pl.ds(SEQS * me + start, count)])
 
     def row_aside(turn):
         pl.when(turn >= 2)(lambda: start_all(moves(2 * turn - 3)))
         pl.when(turn >= 1)(lambda: start_all(moves(2 * turn - 2)))
+        pl.when(turn == 2)(lambda: start_all(later_moves(0)))
+        pl.when(turn == 3)(lambda: start_all(later_moves(1)))
 
     def row_finish(block, out):
         out = out.astype(F32).reshape(4, 8, 8, WIDE)
@@ -247,12 +246,12 @@
 
     attend_blocks(8, wide, lambda at: x_ref[pl.ds(at * 4, 4)].astype(F32).reshape(BLOCK, WIDE),
                   lambda at: lambda sl: wr_ref[sl, :], lambda at: wro_ref[...],
-                  lambda at: row_keep(mask_ref, 32 * me + 4 * at), bias_ref, row_finish, row_ready, row_aside)
+                  lambda at: row_keep(mask_ref, SEQS * me + 4 * at), bias_ref, row_finish, row_ready, row_aside)
     for block in range(5, 8):
         start_all(moves(block))
-    start_all(later_moves())
+    start_all(later_moves(2))
     for half in range(2):
-        in_ref[half, pl.ds(32 * me, 32)] = mo_ref[2 * me + half]
+        in_ref[half, pl.ds(SEQS * me, SEQS)] = mo_ref[2 * me + half]
 
     finish_all(loads)
     keys_ref[...] = mask_ref[mine, :].astype(F32).T
@@ -276,7 +275,7 @@
         m_ref[layer + 1, pl.ds(two * 2, 2)] = out.reshape(2, LANES, WIDE)
         ac = lax.dot_general(wp_ref[layer], layer_norm(out), NT, preferred_element_type=F32)
         ac = (ac * jnp.concatenate([mask_ref[pl.ds(HELD * me + 2 * two + blk, 1), :] for blk in range(2)], axis=1).astype(F32)).astype(BF16)
-        parts = (ac[:32], ac[32:])
+        parts = (ac[:SEQS], ac[SEQS:])
         own1_ref[two] = jnp.where(layer == 0, parts[0].astype(F32), own1_ref[two].astype(F32)).astype(BF16)
         own2_ref[two] = parts[1]
         for blk in range(2):
@@ -290,13 +289,15 @@
     def seq_copies(two):
         return group_copies(
             me, 26 + two, send_sem, recv_sem,
-            lambda peer: m_ref.at[2, pl.ds(2 * two, 2), pl.ds(pl.multiple_of(32 * peer, 32), HELD), :],
+            lambda peer: m_ref.at[2, pl.ds(2 * two, 2), pl.ds(pl.multiple_of(SEQS * peer, SEQS), HELD), :],
             back_ref.at[0, pl.ds(HELD * me + 2 * two, 2)])
 
-    def later_seqs():
+    def later_seqs(two):
+        kind = jnp.where(two == 0, 34, 43 + two)
         return group_copies(
-            me, 34, send_sem, recv_sem, lambda peer: m_ref.at[2, :, pl.ds(pl.multiple_of(32 * peer + HELD, HELD), HELD), :],
-            back_ref.at[1, mine])
+            me, kind, send_sem, recv_sem,
+            lambda peer: m_ref.at[2, pl.ds(2 * two, 2), pl.ds(pl.multiple_of(SEQS * peer + HELD, HELD), HELD), :],
+            back_ref.at[1, pl.ds(HELD * me + 2 * two, 2)])
 
     def emit(block):
         def first():
@@ -304,14 +305,11 @@
             full1_ref[pl.ds(HELD * me + 2 * block, 2)] = part_ref[block]
 
         def second():
-            start_all(part_copies(block, full2_ref) + seq_copies(block - 8))
+            start_all(part_copies(block, full2_ref) + seq_copies(block - 8) + later_seqs(block - 8))
             full2_ref[pl.ds(HELD * me + 2 * (block - 8), 2)] = part_ref[block]
 
-        if isinstance(block, int):
-            second()
-        else:
-            pl.when(jnp.logical_and(block >= 0, block < 8))(first)
-            pl.when(block >= 8)(second)
+        pl.when(jnp.logical_and(block >= 0, block < 8))(first)
+        pl.when(block >= 8)(second)
 
     outer, along, across, close = pair_stages(
         me, 35, True, own1_ref, full1_ref, z_ref, mask_ref, res_ref,
@@ -319,7 +317,8 @@
         zc_ref, next_ref, send_sem, recv_sem, pair)
 
     def second_half():
-        finish_all(later_moves())
+        for part in range(3):
+            finish_all(later_moves(part))
         take(1)
 
     def col_aside(turn):
@@ -334,12 +333,17 @@
     attend_blocks(16, wide, lambda at: m_ref[at // 8, pl.ds(at % 8 * 2, 2)].astype(F32).reshape(BLOCK, WIDE),
                   lambda at: lambda sl: wc_ref[at // 8, sl, :], lambda at: wco_ref[at // 8],
                   col_keep, None, col_finish, lambda: None, col_aside)
-    for block in range(13, 16):
-        emit(block)
-    start_all(later_seqs())
+    last = range(13, 16)
+    for block in last:
+        start_all(part_copies(block, full2_ref))
+        full2_ref[pl.ds(HELD * me + 2 * (block - 8), 2)] = part_ref[block]
+    for block in last:
+        start_all(seq_copies(block - 8))
     for half in range(2):
-        back_ref[half, mine] = m_ref[2, :, pl.ds(pl.multiple_of(32 * me + HELD * half, HELD), HELD), :]
+        back_ref[half, mine] = m_ref[2, :, pl.ds(pl.multiple_of(SEQS * me + HELD * half, HELD), HELD), :]
     across()
+    for block in last:
+        start_all(later_seqs(block - 8))
 
     outer, along_2, across_2, _ = pair_stages(
         me, 39, False, own2_ref, full2_ref, zc_ref, mask_ref, res_ref,
@@ -353,7 +357,7 @@
         turn_tokens(back_ref.at[half], wide_ref, put)
 
     def last_half():
-        finish_all(later_seqs())
+        drain(8, later_seqs)
         take_back(1)
 
     def last_aside(turn):
@@ -363,7 +367,7 @@
 
     def last_ready():
         close()
-        bias_ref[...] = next_ref[...].astype(F32) * LOG2E
+        bias_by_key(next_ref, bias_ref)
 
     def last_finish(block, out):
         out_ref[pl.ds(4 * block, 4)] = out.reshape(4, RES, WIDE)
@@ -372,7 +376,7 @@
     take_back(0)
     attend_blocks(8, wide, lambda at: ml_ref[pl.ds(at * 4, 4)].astype(F32).reshape(BLOCK, WIDE),
                   lambda at: lambda sl: wl_ref[sl, :], lambda at: wlo_ref[...],
-                  lambda at: row_keep(mask_ref, 32 * me + 4 * at), bias_ref, last_finish, last_ready, last_aside)
+                  lambda at: row_keep(mask_ref, SEQS * me + 4 * at), bias_ref, last_finish, last_ready, last_aside)
 
 
 def run_all(m, z, mask, res_mask, row, tri, streamed):
@@ -386,7 +390,7 @@
         grid=(1,),
         in_specs=specs,
         out_specs=[VMEM] * 2,
-        out_shape=[jax.ShapeDtypeStruct(m.shape, BF16), jax.ShapeDtypeStruct(z.shape, BF16)],
+        out_shape=[pltpu.VMEM(m.shape, BF16), pltpu.VMEM(z.shape, BF16)],
         scratch_shapes=[
             vmem(2, 4 * WIDE, WIDE),
             vmem(2, WIDE, WIDE),
@@ -394,24 +398,24 @@
             vmem(2, CELLS, LANES),
             vmem(4 * WIDE, WIDE),
             vmem(WIDE, WIDE),
-            vmem(8, 32, 8, WIDE),
+            vmem(8, SEQS, 8, WIDE),
             vmem(2, LANES, 8, WIDE),
             pltpu.VMEM((3, CELLS, LANES), F32),
             vmem(3, HELD, LANES, WIDE),
             vmem(2, RES, HELD, WIDE),
-            vmem(32, RES, WIDE),
+            vmem(SEQS, RES, WIDE),
+            vmem(8, RES, LANES),
+            pltpu.VMEM((HELD, RES, LANES), F32),
+            vmem(HELD, 2, SEQS, LANES),
+            pltpu.VMEM((LANES, HELD), F32),
+            vmem(8, SEQS, BLOCK),
+            vmem(8, SEQS, BLOCK),
+            vmem(RES, SEQS, LANES),
+            vmem(RES, SEQS, LANES),
             vmem(HELD, RES, LANES),
-            pltpu.VMEM((HELD, RES, LANES), F32),
-            vmem(HELD, 2, 32, LANES),
-            pltpu.VMEM((LANES, HELD), F32),
-            vmem(8, 32, BLOCK),
-            vmem(8, 32, BLOCK),
-            vmem(RES, 32, LANES),
-            vmem(RES, 32, LANES),
-            vmem(HELD, RES, LANES),
-            vmem(HELD, RES, LANES),
-            pltpu.SemaphoreType.DMA((126,)),
-            pltpu.SemaphoreType.DMA((126,)),
+            vmem(8, RES, LANES),
+            pltpu.SemaphoreType.DMA((LANES + 25,)),
+            pltpu.SemaphoreType.DMA((LANES + 25,)),
             pltpu.SemaphoreType.DMA((6,)),
         ] + wide_scratch(LANES) + pair_scratch(),
         compiler_params=pltpu.CompilerParams(collective_id=0, has_side_effects=True),
@@ -456,13 +460,33 @@
     if heads < 8:
         w = jnp.concatenate([w, jnp.zeros((8 - heads, LANES), BF16)], axis=0)
     values = lax.dot_general(w, ln_ref[...], NT, preferred_element_type=F32)
-    left = lax.broadcasted_iota(jnp.int32, (heads, LANES), 1) < RES
+    left = lax.broadcasted_iota(jnp.int32, (HELD, LANES), 1) < RES
     for two in range(8):
         value = values[:heads, LANES * two:LANES * two + LANES]
         turned = pltpu.roll(value, RES, 1)
-        spread_ref[pl.ds(2 * two, heads, stride=HELD), :] = jnp.where(left, value, turned)
-        spread_ref[pl.ds(2 * two + 1, heads, stride=HELD), :] = jnp.where(left, turned, value)
-    return spread_ref[pl.ds(0, HELD * heads), :].astype(BF16).reshape(heads, HELD, LANES)
+        low = left[:heads]
+        spread_ref[pl.ds(2 * two, heads, stride=HELD), :] = jnp.where(low, value, turned)
+        spread_ref[pl.ds(2 * two + 1, heads, stride=HELD), :] = jnp.where(low, turned, value)
+    both = [jnp.where(left, spread_ref[pl.ds(2 * HELD * n, HELD), :], spread_ref[pl.ds(2 * HELD * n + HELD, HELD), :])
+            for n in range(heads // 2)]
+    return jnp.concatenate(both, axis=0).astype(BF16).reshape(heads // 2, HELD, LANES)
+
+
+def bias_by_query(rows_ref, bias_ref):
+    for n in range(rows_ref.shape[0]):
+        turned = (rows_ref[n].astype(F32) * LOG2E).T
+        for half in range(2):
+            one = turned[RES * half:RES * half + RES]
+            bias_ref[2 * n + half] = jnp.concatenate([one, one], axis=1)
+
+
+def bias_by_key(rows_ref, bias_ref):
+    left = lax.broadcasted_iota(jnp.int32, (RES, LANES), 1) < RES
+    for n in range(rows_ref.shape[0]):
+        value = rows_ref[n].astype(F32) * LOG2E
+        turned = pltpu.roll(value, RES, 1)
+        bias_ref[2 * n] = jnp.where(left, value, turned)
+        bias_ref[2 * n + 1] = jnp.where(left, turned, value)
 
 
 def triangle(zf_ref, ln_ref, w_ref, wo_ref, keep, bias_ref, pt_refs, gt_refs, others, ready):
@@ -480,7 +504,7 @@
     ready()
     jobs = [(4 * block - 4, 4 * block - 1, fill(block)) for block in range(1, 4)]
     jobs += [(4 * block + 4 + 3 * LAG, 4 * block + 5 + 3 * LAG, [done(block)]) for block in range(3)]
-    attend_stream([(pt_refs[block], gt_refs[block], [keep, keep]) for block in range(4)], others, 4, 32, bias_ref, jobs)
+    attend_stream([(pt_refs[block], gt_refs[block], [keep, keep]) for block in range(4)], others, 4, SEQS, bias_ref, jobs)
     done(3)()
 
 
@@ -510,8 +534,8 @@
         norm = lax.dot_general(mask, mask_ref[mine, :].astype(F32).astype(BF16), NT, preferred_element_type=F32)
         full32_ref[:CELLS] = wm_ref[...].astype(F32).reshape(CELLS, LANES)
         if swap:
-            for q in range(32):
-                wt_ref[pl.ds(32 * q, 32), :] = full32_ref[pl.ds(q, 32, stride=32), :].astype(BF16)
+            for q in range(SEQS):
+                wt_ref[pl.ds(SEQS * q, SEQS), :] = full32_ref[pl.ds(q, SEQS, stride=SEQS), :].astype(BF16)
         else:
             wt_ref[...] = wm_ref[...].reshape(CELLS, LANES)
         w_turned = wt_ref[...].T
@@ -521,14 +545,14 @@
         zeros = jnp.zeros((RES, LANES), BF16)
 
         def one(q, carry):
-            c_q = full32_ref[pl.ds(q, RES, stride=32), :].astype(BF16)
+            c_q = full32_ref[pl.ds(q, RES, stride=SEQS), :].astype(BF16)
             rhs = jnp.concatenate([jnp.concatenate([c_q, zeros], axis=1), jnp.concatenate([zeros, c_q], axis=1)], axis=0)
             o = lax.dot_general(own, rhs, NT, preferred_element_type=F32).astype(BF16)
             for pair in range(8):
-                o_ref[pair, pl.ds(pl.multiple_of(q * 32, 32), 32), :] = o[32 * pair:32 * pair + 32]
+                o_ref[pair, pl.ds(pl.multiple_of(q * SEQS, SEQS), SEQS), :] = o[SEQS * pair:SEQS * pair + SEQS]
             return carry
 
-        lax.fori_loop(0, 32, one, 0, unroll=4)
+        lax.fori_loop(0, SEQS, one, 0, unroll=4)
         for pair in range(8):
             update = jnp.dot(w_turned, o_ref[pair], preferred_element_type=F32).T
             z = z_ref[pl.ds(2 * pair, 2)].astype(F32).reshape(LANES, LANES)
@@ -565,7 +589,7 @@
 
         def ready():
             finish_all(exchange(2))
-            bias_ref[...] = rb_ref[...].astype(F32) * LOG2E
+            bias_by_key(rb_ref, bias_ref)
 
         triangle(zf_ref, ln_ref, wb_ref, wob_ref, keep(), bias_ref, pt_refs, gt_refs, others, ready)
         out_ref[...] = zf_ref[...].astype(BF16).reshape(HELD, RES, LANES)
@@ -591,14 +615,14 @@
         pltpu.VMEM((CELLS, LANES), F32),
         pltpu.VMEM((CELLS, LANES), BF16),
         pltpu.VMEM((4, RES, LANES), F32),
-        pltpu.VMEM((4, HELD, LANES), BF16),
-        pltpu.VMEM((4, RES, LANES), BF16),
-        pltpu.VMEM((4, HELD, LANES), BF16),
-        pltpu.VMEM((4, RES, LANES), BF16),
+        pltpu.VMEM((2, HELD, LANES), BF16),
+        pltpu.VMEM((2, RES, LANES), BF16),
+        pltpu.VMEM((2, HELD, LANES), BF16),
+        pltpu.VMEM((2, RES, LANES), BF16),
         pltpu.VMEM((HELD, RES, LANES), BF16),
         pltpu.VMEM((RES, HELD, LANES), BF16),
-        pltpu.VMEM((HELD, HELD, LANES), BF16),
-    ] + attend_scratch(4, 32, RES, 4)
+        pltpu.VMEM((8, HELD, LANES), BF16),
+    ] + attend_scratch(4, SEQS, RES, 4)
 
 
 def norm_all(zf_ref, ln_ref):

time: 114 us -> 104 us (0.912)
  Pallas kernels: 109 us -> 101 us
  local copies, waits for them, and re-layouts: 3.46 us -> 1.85 us
    pallas_call x1, Pallas kernels: 109 us -> 101 us  [run_all(): pl.pallas_call(kernel, grid=(1,), in_specs=specs, out_specs=[VMEM] * 2, o...]
    unnamed x4 -> x2, local copies, waits for them, and re-layouts: 3.46 us -> 1.85 us
where the time goes in v9:
time: 104 us; the launch traced here: 103 us
  Pallas kernels  101 us (97%)
  local copies, waits for them, and re-layouts  1.85 us (2%)
    pallas_call x1, Pallas kernels, run_all(): pl.pallas_call(kernel, grid=(1,), in_specs=specs, out_specs=[VMEM] * 2, o...  101 us

profile of v9, /device:TPU:0, one launch (start us, length us, event | category | flops | bytes accessed | tf_op | source)
XLA Modules:
  0.0 103.4 jit_solution(15571409773166422958)
XLA Ops:
  0.6 100.9 %evoformer.1 = (bf16[32,64,384]{2,1,0:T(8,128)(2,1)S(1)}, bf16[16,64,128]{2,1,0:T(8,128)(2,1)S(1)}) custom-call(bf16[32,64,384]{2,1,0:T(8,128)(2,1)} %x_ref.1, bf16[16,64,128]{2,1,0:T(8,128)(2,1)} %z_ref.1, s32[64,128]{1,0:T(8,128)} %bitcast.37, s32[1,64]{1,0:T(1,128)} %bitcast.42, bf16[2,16,128]{2,1,0:T(8,128)(2,1)} %bitcast.38, ...), custom_call_target="tpu_custom_call" | custom-call | flops 10000000000 | bytes 4194304 | tf_op jit(solution)/shard_map/evoformer/pallas_call | solution.py:388
  101.5 1.1 %copy.21 = bf16[32,64,384]{2,1,0:T(8,128)(2,1)} copy(bf16[32,64,384]{2,1,0:T(8,128)(2,1)S(1)} %get-tuple-element.2) | data formatting | bytes 3145728
  102.7 0.7 copy.22
